TPU v7x, 256 devices: a whole 4x4x8 slice. The times are simulated.
256 devices in a mesh: seq: 16 (over z, core), vocab: 16 (over y, x).
Axes of the slice: x: 4, y: 4, z: 8, core: 2. Of those that a mesh axis runs over, the one named last changes fastest.
Arguments:
- probe_states: bfloat16 [3, 16384, 6144], P(None, 'seq', 'vocab'), may hold values from -6 to 6
- final_states: bfloat16 [16384, 6144], P('seq', 'vocab'), may hold values from -6 to 6
- translator: bfloat16 [3, 6144, 6144], P(None, 'vocab', 'seq'), may hold values from -0.078125 to 0.078125
- translator_bias: float32 [3, 6144], P(None, 'seq'), may hold values from -4 to 4
- norm_gain: float32 [6144], P('seq'), may hold values from 0.5 to 1.5
- unembed: bfloat16 [32768, 6144], P('vocab', 'seq'), may hold values from -0.21875 to 0.21875
- answer_rows: int32 [16, 32], P('seq'), may hold values from 0 to 1023, as said below
- answer_count: int32 [16], P('seq'), may hold values from 1 to 32, 256 in all
- targets: int32 [16, 32], P('seq'), may hold values from 0 to 32767
Outputs:
- answer_logprob: float32 [4, 16, 32], P(None, 'seq')
- answer_kl: float32 [3, 16, 32], P(None, 'seq')
Inputs may be any that keep to these rules, and one draw needn't show every extreme that they name: `answer_rows`: each row holds 32 different positions. `answer_count`: the counts sum to 256, and some sequence has 32.
All inputs are finite; a program needn't handle non-finite values. No bound on the sum of `answer_count` on one device may be relied on, other than what follows from the above.
Results may differ from a plain program's by a relative error of at most 0.00099.
Values may be sent and summed in bfloat16 or wider, within the bound.
No kernel may reach another device: no remote copies, remote signals or barrier semaphores. Data moves between devices by JAX's collectives and lax.ppermute only.
A program may use at most 64 MiB of HBM per device.

v0:
```python
import math

import jax
import jax.numpy as jnp
from jax import lax
from jax.sharding import Mesh
from jax.sharding import PartitionSpec as P

D = 6144
LAYERS = 3
FLAG_DEV = 16
CAP = 32
SEQ = ("seq_0", "seq_1")
VOCAB = ("vocab_0", "vocab_1")


def gathered_by_axis(value, axes, dim):
    for axis in reversed(axes):
        value = lax.all_gather(value, axis, axis=dim, tiled=True)
    return value


def sent_together(arrays, axis, dim, along):
    widths = [math.prod(a.shape[along:]) for a in arrays]
    both = jnp.concatenate(
        [a.reshape(*a.shape[:along], w) for a, w in zip(arrays, widths)], axis=along
    )
    out = lax.all_gather(both, axis, axis=dim, tiled=True)
    blocks = jnp.split(out, [sum(widths[:k]) for k in range(1, len(widths))], axis=along)
    return tuple((b.reshape(*out.shape[:along], *a.shape[along:]) for a, b in zip(arrays, blocks)))


def split_up(value, dim, count):
    before, after = (value.shape[:dim], value.shape[dim + 1 :])
    return jnp.moveaxis(value.reshape(*before, count, -1, *after), dim, 0)


def summed_on_arrival(value, axis, dim):
    blocks = split_up(value, dim, lax.axis_size(axis))
    arrived = lax.all_to_all(blocks, axis, split_axis=0, concat_axis=0, tiled=True)
    return arrived.sum(axis=0)


def over_axes(value, axes):
    for axis in axes:
        value = lax.psum(value, axis)
    return value


def body(
    probe_states,
    final_states,
    translator,
    translator_bias,
    norm_gain,
    unembed,
    answer_rows,
    answer_count,
    targets,
):
    seq_count = lax.axis_size(SEQ)
    seq_index = lax.axis_index(SEQ)
    vocab_index = lax.axis_index(VOCAB)
    width_in = probe_states.shape[2]
    width_out = translator.shape[2]
    vocab_part = unembed.shape[0]
    picks = answer_rows[0]
    local = jnp.concatenate(
        [jnp.take(probe_states, picks, axis=1), jnp.take(final_states, picks, axis=0)[None]], axis=0
    )
    gathered = gathered_by_axis(local, SEQ, 1)
    offset = seq_count // 2 * FLAG_DEV
    counts_all, targets_all = sent_together((answer_count, targets), SEQ, 0, 1)
    starts = jnp.cumsum(counts_all) - counts_all
    ends = starts + counts_all
    packed_index = jnp.arange(seq_count * FLAG_DEV, dtype=jnp.int32)
    source = jnp.sum((ends[None, :] <= packed_index[:, None]).astype(jnp.int32), axis=1)
    matches = source[:, None] == jnp.arange(seq_count, dtype=jnp.int32)[None, :]
    slot = packed_index - jnp.sum(jnp.where(matches, starts[None, :], 0), axis=1)
    flat = jnp.roll(source * CAP + slot, offset)
    rows = jnp.take(gathered, flat, axis=1)
    own_rows = FLAG_DEV
    flat_targets = jnp.take(targets_all.reshape(-1), flat)
    row_targets = lax.dynamic_slice_in_dim(flat_targets, seq_index * own_rows, own_rows)
    total_rows = rows.shape[1]
    in_pos = vocab_index * width_in + jnp.arange(width_in, dtype=jnp.int32)
    out_pos = seq_index * width_out + jnp.arange(width_out, dtype=jnp.int32)
    identity = (in_pos[:, None] == out_pos[None, :]).astype(jnp.bfloat16)
    carried = jnp.einsum("lrd,de->rle", rows, identity, preferred_element_type=jnp.float32)
    mapped = jnp.einsum(
        "lrd,lde->rle", rows[:LAYERS], translator, preferred_element_type=jnp.float32
    )
    partial_value = carried + jnp.concatenate([mapped, jnp.zeros_like(carried[:, :1])], axis=1)
    summed = lax.psum(partial_value, VOCAB)
    bias_rows = jnp.concatenate([translator_bias, jnp.zeros((1, width_out), jnp.float32)], axis=0)
    lensed = summed + bias_rows[None, :, :]
    squares = jnp.sum(lensed * lensed, axis=2)
    own_square = summed_on_arrival(squares, SEQ, 0)
    scaled = (lensed * norm_gain[None, None, :]).astype(jnp.bfloat16)
    product = jnp.einsum("rld,vd->rlv", scaled, unembed, preferred_element_type=jnp.float32)
    term = lax.psum_scatter(
        product.reshape(own_rows * lax.axis_size(SEQ), (LAYERS + 1) * vocab_part),
        SEQ,
        scatter_dimension=0,
        tiled=True,
    )
    factor = lax.rsqrt(own_square / D + 1e-05)
    logits = term.reshape(own_rows, LAYERS + 1, vocab_part) * factor[:, :, None]
    expz = jnp.exp(logits)
    total_exp = jnp.sum(expz, axis=2)
    final_logits = logits[:, LAYERS:]
    cross = jnp.sum(expz[:, LAYERS:] * (final_logits - logits[:, :LAYERS]), axis=2)
    local_ids = row_targets - vocab_index * vocab_part
    target_hit = jnp.arange(vocab_part, dtype=jnp.int32)[None, :] == local_ids[:, None]
    picked = jnp.sum(jnp.where(target_hit[:, None, :], logits, 0.0), axis=2)
    total_exp, cross, picked = (
        over_axes(total_exp, VOCAB),
        over_axes(cross, VOCAB),
        over_axes(picked, VOCAB),
    )
    log_total = jnp.log(total_exp)
    logprob = picked - log_total
    divergence = cross / total_exp[:, LAYERS:] - log_total[:, LAYERS:] + log_total[:, :LAYERS]
    slots = jnp.arange(CAP, dtype=jnp.int32)
    live = slots < answer_count[0]
    results = jnp.concatenate([logprob, divergence], axis=1)
    every_result = lax.all_gather(results, SEQ, axis=0, tiled=True)
    my_start = jnp.sum(jnp.where(jnp.arange(seq_count, dtype=jnp.int32) == seq_index, starts, 0))
    wanted = (jnp.minimum(my_start + slots, total_rows - 1) + offset) % total_rows
    mine = jnp.take(every_result, wanted, axis=0)
    logprob = mine[:, : LAYERS + 1]
    divergence = mine[:, LAYERS + 1 :]
    out_logprob = jnp.where(live[:, None], logprob, 0.0).T[:, None, :]
    out_divergence = jnp.where(live[:, None], divergence, 0.0).T[:, None, :]
    return (out_logprob, out_divergence)


def solution(mesh):
    split = Mesh(mesh.devices.reshape(8, 2, 4, 4), ("seq_0", "seq_1", "vocab_0", "vocab_1"))
    return jax.shard_map(
        body,
        mesh=split,
        in_specs=(
            P(None, SEQ, VOCAB),
            P(SEQ, VOCAB),
            P(None, VOCAB, SEQ),
            P(None, SEQ),
            P(SEQ),
            P(VOCAB, SEQ),
            P(SEQ, None),
            P(SEQ),
            P(SEQ, None),
        ),
        out_specs=(P(None, SEQ, None), P(None, SEQ, None)),
        check_vma=False,
    )
```

profile of v0, /device:TPU:1, one launch (start us, length us, event | category | flops | bytes accessed | tf_op | source)
XLA Modules:
  0.0 305.5 jit_solution(11106795249357113970)
XLA Ops:
  7.2 0.8 compare_and_fusion
  8.7 1.9 gather_fusion.2
  10.6 0.8 gather_fusion.1
  11.6 4.9 %all_gather.13 = bf16[4,64,384]{2,1,0:T(8,128)(2,1)} all-gather(bf16[4,32,384]{2,1,0:T(8,128)(2,1)S(1)} %pad_maximum_fusion), channel_id=1, replica_groups=mesh['seq_0'=8,'seq_1'=2,'vocab_0'=4,'vocab_1'=4] {'seq_1'}, dimensions={1}, use_global_device_ids=true | all-gather | bytes 294912 | tf_op jit(solution)/shard_map/all_gather | solution.py:19
  17.3 18.5 %all-gather = s32[16,1,33]{2,1,0:T(1,128)S(1)} all-gather(s32[1,1,33]{2,1,0:T(1,128)S(1)} %add_bitcast_fusion), channel_id=1, replica_groups=mesh['seq_0'=8,'seq_1'=2,'vocab_0'=4,'vocab_1'=4] {'seq_0','seq_1'}, dimensions={0}, use_global_device_ids=true | all-gather | bytes 2244 | tf_op jit(solution)/shard_map/all_gather | solution.py:28
  37.1 1.9 gather_fusion
  39.1 13.6 %all-gather.4.cloned.1.call-done = bf16[4,512,384]{2,1,0:T(8,128)(2,1)} async-done(((bf16[4,64,384]{2,1,0:T(8,128)(2,1)}), bf16[4,512,384]{2,1,0:T(8,128)(2,1)}) %all-gather.4.cloned.1.call-update) | async-done | bytes 1572880 | tf_op jit(solution)/shard_map/all_gather | solution.py:19
  52.7 3.8 %copy.39 = bf16[4,512,384]{2,0,1:T(4,128)(2,1)} copy(bf16[4,512,384]{2,1,0:T(8,128)(2,1)} %all-gather.4.cloned.1.call-done) | data formatting | bytes 3145728 | tf_op jit(solution)/shard_map/all_gather | solution.py:19
  56.5 2.9 gather_fusion.3
  59.4 1.9 convolution_bitcast_fusion
  61.2 1.8 bitcast_add_fusion
  63.8 100.1 %all-reduce.6.cloned.1.call-done = f32[256,4,384]{0,2,1:T(8,128)} async-done(((f32[256,4,384]{0,2,1:T(8,128)}), f32[256,4,384]{0,2,1:T(8,128)}) %all-reduce.6.cloned.1.call-update) | async-done | bytes 1572880 | tf_op jit(solution)/shard_map/psum | solution.py:94
  163.9 7.6 %fusion.2 = f32[256,4,2048]{0,2,1:T(8,128)} fusion(bf16[2048,384]{1,0:T(8,128)(2,1)} %param.14, f32[256,4,384]{0,2,1:T(8,128)} %all-reduce.6.cloned.1.call-done, f32[384]{0:T(512)S(1)} %copy-done.1, f32[4,384]{1,0:T(4,128)S(1)} %concatenate.53), kind=kOutput, calls=%fused_computation.10 | convolution fusion | flops 1611792384 | bytes 11542016 | tf_op jit(solution)/shard_map/rld,vd->rlv/dot_general | solution.py:100
  171.5 8.9 %copy.57 = f32[256,8192]{1,0:T(8,128)} copy(f32[256,8192]{0,1:T(8,128)} %bitcast.64) | data formatting | bytes 16777216
  182.0 1.7 multiply_reduce_fusion
  184.4 9.2 %all-to-all-start = ((f32[16,16,4]{1,2,0:T(4,128)}), f32[16,16,4]{1,2,0:T(4,128)S(1)}, u32[]{:S(2)}, u32[]{:S(2)}) async-start(f32[16,16,4]{1,2,0:T(4,128)} %copy.44), calls=%async_computation | async-start | bytes 65536 | tf_op jit(solution)/shard_map/all_to_all | solution.py:40
  193.7 7.6 %all-to-all-done = f32[16,16,4]{1,2,0:T(4,128)S(1)} async-done(((f32[16,16,4]{1,2,0:T(4,128)}), f32[16,16,4]{1,2,0:T(4,128)S(1)}, u32[]{:S(2)}, u32[]{:S(2)}) %all-to-all-start) | async-done | bytes 4128 | tf_op jit(solution)/shard_map/all_to_all | solution.py:40
  201.3 49.0 %reduce-scatter.4.cloned.1.call-done = f32[16,8192]{1,0:T(8,128)} async-done(((f32[256,8192]{1,0:T(8,128)}), f32[16,8192]{1,0:T(8,128)}) %reduce-scatter.4.cloned.1.call-update) | async-done | bytes 524304
  250.2 3.5 %copy.58 = f32[16,8192]{0,1:T(8,128)} copy(f32[16,8192]{1,0:T(8,128)} %reduce-scatter.4.cloned.1.call-done) | data formatting | bytes 1048576
  253.7 2.8 fusion.21
  256.6 1.0 select_reduce_fusion
  258.2 8.5 %all-reduce.3 = (f32[16,4]{0,1:T(4,128)S(1)}, f32[16,3]{0,1:T(4,128)S(1)}, f32[16,4]{0,1:T(4,128)S(1)}) all-reduce(f32[16,4]{0,1:T(4,128)S(1)} %get-tuple-element.11, f32[16,3]{0,1:T(4,128)S(1)} %fusion.1, f32[16,4]{0,1:T(4,128)S(1)} %get-tuple-element.10), channel_id=1, replica_groups=mesh['seq_0'=8,'seq_1'=2,'vocab_0'=4,'vocab_1'=4] {'vocab_0'}, use_global_device_ids=true, to_apply=%region_12.13 | all-reduce | flops 176 | bytes 1408 | tf_op jit(solution)/shard_map/psum | solution.py:46
  266.8 8.3 %all-reduce.2 = (f32[16,4]{0,1:T(4,128)S(1)}, f32[16,3]{0,1:T(4,128)S(1)}, f32[16,4]{0,1:T(4,128)S(1)}) all-reduce(f32[16,4]{0,1:T(4,128)S(1)} %get-tuple-element.15, f32[16,3]{0,1:T(4,128)S(1)} %get-tuple-element.16, f32[16,4]{0,1:T(4,128)S(1)} %get-tuple-element.17), channel_id=1, replica_groups=mesh['seq_0'=8,'seq_1'=2,'vocab_0'=4,'vocab_1'=4] {'vocab_1'}, use_global_device_ids=true, to_apply=%region_13.14 | all-reduce | flops 176 | bytes 1408 | tf_op jit(solution)/shard_map/psum | solution.py:46
  275.1 21.6 %all-gather.1 = f32[16,16,7]{1,2,0:T(8,128)S(1)} all-gather(f32[1,16,7]{1,2,0:T(8,128)S(1)} %maximum_bitcast_fusion), channel_id=1, replica_groups=mesh['seq_0'=8,'seq_1'=2,'vocab_0'=4,'vocab_1'=4] {'seq_0','seq_1'}, dimensions={0}, use_global_device_ids=true | all-gather | bytes 7616 | tf_op jit(solution)/shard_map/all_gather | solution.py:127
  (60 shorter events, 8.3 us)
Async XLA Ops:
  7.2 3.4 %copy-start = (bf16[3,1024,384]{2,1,0:T(8,128)(2,1)S(1)}, bf16[3,1024,384]{2,1,0:T(8,128)(2,1)}, u32[]{:S(2)}) copy-start(bf16[3,1024,384]{2,1,0:T(8,128)(2,1)} %param.9) | copy-start | bytes 7077892
  7.2 10.1 %copy-start.3 = (s32[1,32]{1,0:T(1,128)S(1)}, s32[1,32]{1,0:T(1,128)}, u32[]{:S(2)}) copy-start(s32[1,32]{1,0:T(1,128)} %param.17) | copy-start | bytes 388
  7.2 45.5 %all-gather.4.cloned.1.call-start = ((), (), s32[]{:S(2)}) async-start(), calls=%async_computation.2 | async-start | bytes 1769472 | tf_op jit(solution)/shard_map/all_gather | solution.py:19
  16.5 147.3 %all-reduce.6.cloned.1.call-start = ((), (), s32[]{:S(2)}) async-start(), calls=%async_computation.3 | async-start | bytes 3145728 | tf_op jit(solution)/shard_map/psum | solution.py:94
  63.1 0.7 copy-start.2
  63.1 100.8 %copy-start.1 = (f32[384]{0:T(512)S(1)}, f32[384]{0:T(512)}, u32[]{:S(2)}) copy-start(f32[384]{0:T(512)} %param.13) | copy-start | bytes 4612
  63.1 187.1 %reduce-scatter.4.cloned.1.call-start = ((), (), s32[]{:S(2)}) async-start(), calls=%async_computation.4 | async-start | bytes 8912896
  184.4 16.8 %all-to-all-start = ((f32[16,16,4]{1,2,0:T(4,128)}), f32[16,16,4]{1,2,0:T(4,128)S(1)}, u32[]{:S(2)}, u32[]{:S(2)}) async-start(f32[16,16,4]{1,2,0:T(4,128)} %copy.44), calls=%async_computation | async-start | bytes 65536 | tf_op jit(solution)/shard_map/all_to_all | solution.py:40
Sparse Core Ops, SparseCore 0:
  16.7 36.0 all-gather.3
  63.2 100.6 all-reduce.5
  180.5 69.6 reduce-scatter.3
where the time goes:
time: 306 us
  waiting for transfers between devices  170 us (56%)
  blocking collectives  61.9 us (20%)
  local copies, waits for them, and re-layouts  27.5 us (9%)
  between operations  14.6 us (5%)
  matrix products  11.3 us (4%)
  other arithmetic  10.7 us (3%)
  starting transfers between devices  9.37 us (3%)
    psum x1, waiting for transfers between devices, body(): summed = lax.psum(partial_value, VOCAB)  100 us
    unnamed x4, waiting for transfers between devices  49 us
    all_gather x1, blocking collectives, body(): every_result = lax.all_gather(results, SEQ, axis=0, tiled=True)  21.6 us
    all_gather x1, blocking collectives, sent_together(): out = lax.all_gather(both, axis, axis=dim, tiled=True)  18.5 us
    psum x2, blocking collectives, over_axes(): value = lax.psum(value, axis)  16.8 us
    unnamed x12, local copies, waits for them, and re-layouts  14.3 us
    all_gather x1, waiting for transfers between devices, gathered_by_axis(): value = lax.all_gather(value, axis, axis=dim, tiled=True)  13.6 us
    all_to_all x1, starting transfers between devices, summed_on_arrival(): lax.all_to_all(blocks, axis, split_axis=0, concat_axis=0, tiled=True)  9.25 us
  transfers between devices with their start and end apart: 4, of which 4 were waited for; matrix products, arithmetic and copies ran while one was open for 2% of the time, Pallas kernels for 0%

commit v1 on v0

v1 whole, which is shorter than its diff:
```python
import jax
import jax.numpy as jnp
from jax import lax
from jax.experimental import pallas as pl
from jax.experimental.pallas import tpu as pltpu
from jax.sharding import Mesh
from jax.sharding import PartitionSpec as P

D = 6144
LAYERS = 3
CAP = 32
ROWS = 256
SEQ = ("z", "c")
VOCAB = ("y", "x")
F32 = jnp.float32
BF16 = jnp.bfloat16
NT = (((1,), (1,)), ((), ()))
TN = (((0,), (0,)), ((), ()))
INFO = 128
SHIFT = 16.0


def dot(a, b):
    return jnp.dot(a, b, preferred_element_type=F32)


def exchange(value, axes):
    return lax.all_to_all(value, axes, split_axis=0, concat_axis=0, tiled=True)


def swap_cores(value):
    return lax.ppermute(value, "c", [(0, 1), (1, 0)])


def whole(shape, dtype):
    return jax.ShapeDtypeStruct(shape, dtype)


def translate_kernel(flags, own, other, translator, out):
    low_core = flags[0] == 0
    keep = flags[1].astype(F32)
    lane = lax.broadcasted_iota(jnp.int32, (CAP, ROWS), 1).astype(F32)
    slot = lax.broadcasted_iota(jnp.int32, (CAP, ROWS), 0).astype(F32)
    base = jnp.zeros((1, 1), F32)
    pick_own, pick_other = [], []
    for k in range(8):
        count_own = own[k, INFO + 2 : INFO + 3, 0:1].astype(F32)
        count_other = other[k, INFO + 2 : INFO + 3, 0:1].astype(F32)
        start_own = base + jnp.where(low_core, 0.0, count_other)
        start_other = base + jnp.where(low_core, count_own, 0.0)
        hit_own = (lane == start_own + slot) & (slot < count_own)
        hit_other = (lane == start_other + slot) & (slot < count_other)
        pick_own.append(jnp.where(hit_own, 1.0, 0.0).astype(BF16))
        pick_other.append(jnp.where(hit_other, 1.0, 0.0).astype(BF16))
        base = base + count_own + count_other
    pick_own = jnp.concatenate(pick_own, axis=0)
    pick_other = jnp.concatenate(pick_other, axis=0)
    for layer in range(LAYERS + 1):
        low = layer * CAP
        a = own[:, low : low + CAP, :].reshape(ROWS, -1)
        b = other[:, low : low + CAP, :].reshape(ROWS, -1)
        rows = lax.dot_general(pick_own, a, TN, preferred_element_type=F32)
        rows = rows + lax.dot_general(pick_other, b, TN, preferred_element_type=F32)
        part = rows * keep
        if layer < LAYERS:
            part = part + dot(rows.astype(BF16), translator[layer])
        out[:, layer] = part.astype(BF16).reshape(16, 16, -1)


def high_low(value):
    high = value.astype(BF16).astype(F32)
    row = lax.broadcasted_iota(jnp.int32, value.shape, 0)
    return jnp.where(row == 0, high, jnp.where(row == 1, value - high, 0.0))


def scale_kernel(parts, bias, gain, y_out):
    x = parts[0].astype(F32)
    for k in range(1, 16):
        x = x + parts[k].astype(F32)
    x = x + bias[...]
    y = (x * gain[...]).astype(BF16)
    square = x * x
    square = jnp.concatenate([square, square], axis=0)
    ones = jnp.ones((8, x.shape[1]), F32)
    squares = lax.dot_general(ones, square, NT, precision=lax.Precision.HIGHEST, preferred_element_type=F32)
    squares = high_low(squares)
    for k in range(16):
        y_out[k, 0:64] = y
        y_out[k, 64:72] = jnp.zeros((8, x.shape[1]), BF16)
        y_out[k, 64:72, 0:128] = squares.astype(BF16)


def logits_kernel(y_own, y_other, u_own, u_other, out):
    a = y_own[:, 0:64, :].reshape(1024, -1)
    b = y_other[:, 0:64, :].reshape(1024, -1)
    part = lax.dot_general(a, u_own[...], NT, preferred_element_type=F32)
    part = part + lax.dot_general(b, u_other[...], NT, preferred_element_type=F32)
    out[:, 0:128, :] = (part * (1.0 / SHIFT)).reshape(8, 128, -1)
    out[:, 128:136, :] = jnp.zeros((8, 8, out.shape[2]), F32)

    @pl.when(pl.program_id(0) == 0)
    def _():
        lane = lax.broadcasted_iota(jnp.int32, (8, 128), 1)
        sums = []
        for k in range(16):
            four = y_own[k, 64:72, 0:128].astype(F32) + y_other[k, 64:72, 0:128].astype(F32)
            sums.append(jnp.broadcast_to(four[0:1] + four[1:2], (8, 128)))
        for k in range(8):
            norm = jnp.sqrt(jnp.where(lane < 64, sums[2 * k], sums[2 * k + 1]))
            out[k, 128:136, 0:128] = high_low(norm * (1.0 / SHIFT))


def stats_kernel(summed, norms, target, out):
    square = jnp.zeros((1, 128), F32)
    for k in range(8):
        norm = norms[k, 0:1] + norms[k, 1:2]
        square = square + norm * norm
    factor = SHIFT * lax.rsqrt(square * (SHIFT * SHIFT / D) + 1e-05)
    factor = jnp.broadcast_to(factor, (128, 128)).T[:, 0:1]
    logits = summed[...] * factor
    width = logits.shape[1]
    expz = jnp.exp(logits)
    total = jnp.sum(expz, axis=1, keepdims=True)
    ids = lax.broadcasted_iota(jnp.int32, logits.shape, 1)
    picked = jnp.sum(jnp.where(ids == target[...], logits, 0.0), axis=1, keepdims=True)
    four = logits.reshape(2, 4, 16, width)
    last = expz.reshape(2, 4, 16, width)[:, 3:]
    cross = jnp.sum(last * (four[:, 3:] - four), axis=3, keepdims=True).reshape(128, 1)
    lane = lax.broadcasted_iota(jnp.int32, (128, 128), 1)
    table = jnp.where(lane == 0, total, jnp.where(lane == 1, cross, jnp.where(lane == 2, picked, 0.0)))
    rows = table.T[:8]
    for k in range(32):
        out[k] = rows


def body(
    probe_states,
    final_states,
    translator,
    translator_bias,
    norm_gain,
    unembed,
    answer_rows,
    answer_count,
    targets,
):
    z = lax.axis_index("z")
    c = lax.axis_index("c")
    v = lax.axis_index(VOCAB)
    seq = 2 * z + c
    width = probe_states.shape[2]
    half = unembed.shape[0] // 2
    picks = answer_rows[0]

    u_own = lax.dynamic_slice_in_dim(unembed, c * half, half, 0)
    u_other = swap_cores(lax.dynamic_slice_in_dim(unembed, (1 - c) * half, half, 0))

    info = jnp.concatenate(
        [targets // 256, targets % 256, jnp.broadcast_to(answer_count[:, None], (1, CAP)), jnp.zeros((5, CAP), jnp.int32)]
    )
    info = jnp.pad(info, ((0, 0), (0, width - CAP))).astype(BF16)
    local = jnp.concatenate(
        [
            jnp.take(probe_states, picks, axis=1, mode="clip").reshape(LAYERS * CAP, width),
            jnp.take(final_states, picks, axis=0, mode="clip"),
            info,
        ],
        axis=0,
    )
    own = exchange(jnp.broadcast_to(local[None], (8, *local.shape)), "z")
    other = swap_cores(own)

    flags = jnp.stack([c, (seq == v).astype(jnp.int32)])
    parts = pl.pallas_call(
        translate_kernel,
        out_shape=whole((16, 4, 16, width), BF16),
        in_specs=[pl.BlockSpec(memory_space=pltpu.SMEM)] + [pl.BlockSpec(memory_space=pltpu.VMEM)] * 3,
        name="translate",
    )(flags, own, other, translator)
    arrived = exchange(parts.reshape(16, 64, width), VOCAB)

    bias = jnp.concatenate([translator_bias, jnp.zeros((1, width), F32)], axis=0)
    bias = jnp.repeat(bias, 16, axis=0)
    y_copies = pl.pallas_call(scale_kernel, out_shape=whole((16, 72, width), BF16), name="scale")(
        arrived, bias, norm_gain[None, :]
    )
    y_own = exchange(y_copies, VOCAB)
    y_other = swap_cores(y_own)

    block = 256
    product = pl.pallas_call(
        logits_kernel,
        grid=(half // block,),
        in_specs=[
            pl.BlockSpec((16, 72, width), lambda i: (0, 0, 0)),
            pl.BlockSpec((16, 72, width), lambda i: (0, 0, 0)),
            pl.BlockSpec((block, width), lambda i: (i, 0)),
            pl.BlockSpec((block, width), lambda i: (i, 0)),
        ],
        out_specs=pl.BlockSpec((8, 136, block), lambda i: (0, 0, i)),
        out_shape=whole((8, 136, half), F32),
        name="logits",
    )(y_own, y_other, u_own, u_other)
    info_own, info_other, product = lax.optimization_barrier(
        (own[:, INFO : INFO + 8, :CAP], other[:, INFO : INFO + 8, :CAP], product)
    )
    logit_parts = exchange(product.astype(jnp.float16), "z")
    norms = logit_parts[:, 128:136, :128].astype(F32)
    summed = jnp.sum(logit_parts[:, :128].astype(F32), axis=0)

    info_own = info_own.astype(jnp.int32)
    info_other = info_other.astype(jnp.int32)
    every_info = jnp.stack(
        [jnp.where(c == 0, info_own, info_other), jnp.where(c == 0, info_other, info_own)], axis=1
    ).reshape(16, 8, CAP)
    counts = every_info[:, 2, 0]
    all_targets = every_info[:, 0] * 256 + every_info[:, 1]
    order = jnp.arange(16, dtype=jnp.int32)
    starts = jnp.sum(jnp.where(order[None, :] < order[:, None], counts[None, :], 0), axis=1)
    slots = jnp.arange(CAP, dtype=jnp.int32)
    place = jnp.where(slots[None, :] < counts[:, None], starts[:, None] + slots[None, :], -1)
    row_ids = z * 32 + jnp.arange(32, dtype=jnp.int32)
    hit = place[None] == row_ids[:, None, None]
    row_targets = jnp.sum(jnp.where(hit, all_targets[None], 0), axis=(1, 2))
    local_targets = row_targets - (v * 2 + c) * half
    item_targets = jnp.broadcast_to(local_targets.reshape(2, 1, 16), (2, 4, 16)).reshape(128, 1)
    stats = pl.pallas_call(stats_kernel, out_shape=whole((32, 8, 128), F32), name="stats")(
        summed, norms, item_targets
    )
    sums = jnp.sum(exchange(stats, ("c", "y", "x")), axis=0)
    every = exchange(jnp.broadcast_to(sums[None], (8, 8, 128)), "z")

    table = every[:, :3].reshape(8, 3, 2, 4, 16).transpose(1, 3, 0, 2, 4).reshape(3, 4, 1, ROWS)
    my_start = jnp.sum(jnp.where(order == seq, starts, 0))
    live = slots < answer_count[0]
    wanted = my_start + slots
    mine = wanted[:, None] == jnp.arange(ROWS, dtype=jnp.int32)[None, :]
    mine = jnp.sum(jnp.where(mine[None, None], table, 0.0), axis=3)
    log_total = jnp.log(mine[0])
    logprob = mine[2] - log_total
    divergence = mine[1, :LAYERS] / mine[0, LAYERS:] - log_total[LAYERS:] + log_total[:LAYERS]
    logprob = jnp.where(live[None], logprob, 0.0)[:, None, :]
    divergence = jnp.where(live[None], divergence, 0.0)[:, None, :]
    return (logprob, divergence)


def solution(mesh):
    split = Mesh(mesh.devices.reshape(8, 2, 4, 4), ("z", "c", "y", "x"))
    return jax.shard_map(
        body,
        mesh=split,
        in_specs=(
            P(None, SEQ, VOCAB),
            P(SEQ, VOCAB),
            P(None, VOCAB, SEQ),
            P(None, SEQ),
            P(SEQ),
            P(VOCAB, SEQ),
            P(SEQ, None),
            P(SEQ),
            P(SEQ, None),
        ),
        out_specs=(P(None, SEQ, None), P(None, SEQ, None)),
        check_vma=False,
    )
```

time: 306 us -> 197 us (0.64)
  waiting for transfers between devices: 170 us -> 90.5 us
  blocking collectives: 61.9 us -> 31.5 us
  starting transfers between devices: 9.37 us -> 31 us
  Pallas kernels: 0 us -> 15.1 us
  local copies, waits for them, and re-layouts: 27.5 us -> 12.9 us
  between operations: 14.6 us -> 1.66 us
  matrix products: 11.3 us -> 0 us
    psum x1 -> x0, waiting for transfers between devices: 100 us -> none  [body(): summed = lax.psum(partial_value, VOCAB)]
    all_to_all x1 -> x5, waiting for transfers between devices: 7.58 us -> 88.5 us  [exchange(): return lax.all_to_all(value, axes, split_axis=0, concat_axis=0, tiled=True)]
    unnamed x4 -> x0, waiting for transfers between devices: 49 us -> none
    all_gather x3 -> x0, blocking collectives: 45.1 us -> none  [the longest x1 21.6 us: body(): every_result = lax.all_gather(results, SEQ, axis=0, tiled=True)]
    all_to_all x0 -> x1, blocking collectives: none -> 31.5 us  [exchange(): return lax.all_to_all(value, axes, split_axis=0, concat_axis=0, tiled=True)]
    psum x2 -> x0, blocking collectives: 16.8 us -> none  [over_axes(): value = lax.psum(value, axis)]
    all_to_all x1 -> x5, starting transfers between devices: 9.25 us -> 25.6 us  [exchange(): return lax.all_to_all(value, axes, split_axis=0, concat_axis=0, tiled=True)]
    pallas_call x0 -> x4, Pallas kernels: none -> 15.1 us  [the longest x1 6.4 us: body(): pl.pallas_call(logits_kernel, grid=(half // block,), in_specs=[pl.BlockSp...]
  transfers between devices with their start and end apart: 4 -> 8, of which waited for: 4 -> 7; matrix products, arithmetic and copies ran while one was open for 2% -> 4% of each run, Pallas kernels for 0% -> 0%
where the time goes in v1:
time: 197 us; the launch traced here: 196 us
  waiting for transfers between devices  90.5 us (46%)
  blocking collectives  31.5 us (16%)
  starting transfers between devices  31 us (16%)
  Pallas kernels  15.1 us (8%)
  other arithmetic  13.5 us (7%)
  local copies, waits for them, and re-layouts  12.9 us (7%)
    all_to_all x5, waiting for transfers between devices, exchange(): return lax.all_to_all(value, axes, split_axis=0, concat_axis=0, tiled=True)  88.5 us
    all_to_all x1, blocking collectives, exchange(): return lax.all_to_all(value, axes, split_axis=0, concat_axis=0, tiled=True)  31.5 us
    all_to_all x5, starting transfers between devices, exchange(): return lax.all_to_all(value, axes, split_axis=0, concat_axis=0, tiled=True)  25.6 us
    pallas_call x1, Pallas kernels, body(): pl.pallas_call(logits_kernel, grid=(half // block,), in_specs=[pl.BlockSp...  6.4 us
    ppermute x3, starting transfers between devices, swap_cores(): return lax.ppermute(value, 'c', [(0, 1), (1, 0)])  5.45 us
    convert_element_type x1, other arithmetic, body(): logit_parts = exchange(product.astype(jnp.float16), 'z')  4.1 us
    pallas_call x1, Pallas kernels, body(): pl.pallas_call(translate_kernel, out_shape=whole((16, 4, 16, width), BF16...  3.96 us
  transfers between devices with their start and end apart: 8, of which 7 were waited for; matrix products, arithmetic and copies ran while one was open for 4% of the time, Pallas kernels for 0%

profile of v1, /device:TPU:1, one launch (start us, length us, event | category | flops | bytes accessed | tf_op | source)
XLA Modules:
  0.0 196.1 jit_solution(17458399098357157878)
XLA Ops:
  2.9 1.9 gather_fusion.1
  5.8 31.5 %all_to_all.30.own = bf16[8,136,384]{2,1,0:T(8,128)(2,1)S(1)} all-to-all(bf16[8,136,384]{2,1,0:T(8,128)(2,1)S(1)} %broadcast_in_dim.137), channel_id=1, replica_groups=mesh['z'=8,'c'=2,'y'=4,'x'=4] {'z'}, dimensions={0} | all-to-all | bytes 1671168 | tf_op jit(solution)/shard_map/all_to_all | solution.py:28
  37.3 2.4 %collective-permute-start = (bf16[8,136,384]{2,1,0:T(8,128)(2,1)S(1)}, bf16[8,136,384]{2,1,0:T(8,128)(2,1)}, u32[]{:S(2)}, u32[]{:S(2)}) collective-permute-start(bf16[8,136,384]{2,1,0:T(8,128)(2,1)S(1)} %all_to_all.30.own), channel_id=1, source_target_pairs={{0,16},{16,0},{1,17},{17,1},{2,18},{18,2},{3,19},{19,3},{4,20},{20... | collective-permute-start | bytes 2506760 | tf_op jit(solution)/shard_map/ppermute | solution.py:32
  40.4 1.5 collective-permute-done.other
  41.8 4.0 %translate.1 = bf16[16,4,16,384]{3,2,1,0:T(8,128)(2,1)} custom-call(s32[2]{0:T(128)} %pad_add_fusion.1.flags, bf16[8,136,384]{2,1,0:T(8,128)(2,1)} %copy-done.2, bf16[8,136,384]{2,1,0:T(8,128)(2,1)} %collective-permute-done.other, bf16[3,384,384]{2,1,0:T(8,128)(2,1)} %translator.1), custom_call_target="tpu_custom_call" | custom-call | tf_op jit(solution)/shard_map/translate/pallas_call | solution.py:174
  45.8 6.8 %all-to-all-start.1 = ((bf16[16,64,384]{2,1,0:T(8,128)(2,1)}), bf16[16,64,384]{2,1,0:T(8,128)(2,1)S(1)}, u32[]{:S(2)}, u32[]{:S(2)}) async-start(bf16[16,64,384]{2,1,0:T(8,128)(2,1)} %bitcast.46), calls=%async_computation.1 | async-start | bytes 1572864 | tf_op jit(solution)/shard_map/all_to_all | solution.py:28
  53.1 13.0 %all-to-all-done.1.parts = bf16[16,64,384]{2,1,0:T(8,128)(2,1)S(1)} async-done(((bf16[16,64,384]{2,1,0:T(8,128)(2,1)}), bf16[16,64,384]{2,1,0:T(8,128)(2,1)S(1)}, u32[]{:S(2)}, u32[]{:S(2)}) %all-to-all-start.1) | async-done | bytes 786464 | tf_op jit(solution)/shard_map/all_to_all | solution.py:28
  67.0 2.6 %scale.1 = bf16[16,72,384]{2,1,0:T(8,128)(2,1)} custom-call(bf16[16,64,384]{2,1,0:T(8,128)(2,1)} %copy-done.3, f32[64,384]{1,0:T(8,128)} %bitcast.47, f32[1,384]{1,0:T(1,128)} %broadcast_in_dim.139.gain), custom_call_target="tpu_custom_call" | custom-call | tf_op jit(solution)/shard_map/scale/pallas_call | solution.py:184
  69.6 3.6 %all-to-all-start.2 = ((bf16[16,72,384]{2,1,0:T(8,128)(2,1)}), bf16[16,72,384]{2,1,0:T(8,128)(2,1)S(1)}, u32[]{:S(2)}, u32[]{:S(2)}) async-start(bf16[16,72,384]{2,1,0:T(8,128)(2,1)} %scale.1), calls=%async_computation.2 | async-start | bytes 1769472 | tf_op jit(solution)/shard_map/all_to_all | solution.py:28
  73.3 13.7 %all-to-all-done.2.y_own = bf16[16,72,384]{2,1,0:T(8,128)(2,1)S(1)} async-done(((bf16[16,72,384]{2,1,0:T(8,128)(2,1)}), bf16[16,72,384]{2,1,0:T(8,128)(2,1)S(1)}, u32[]{:S(2)}, u32[]{:S(2)}) %all-to-all-start.2) | async-done | bytes 884768 | tf_op jit(solution)/shard_map/all_to_all | solution.py:28
  86.9 2.7 %collective-permute-start.1 = (bf16[16,72,384]{2,1,0:T(8,128)(2,1)S(1)}, bf16[16,72,384]{2,1,0:T(8,128)(2,1)S(1)}, u32[]{:S(2)}, u32[]{:S(2)}) collective-permute-start(bf16[16,72,384]{2,1,0:T(8,128)(2,1)S(1)} %all-to-all-done.2.y_own), channel_id=1, source_target_pairs={{0,16},{16,0},{1,17},{17,1},{2,18},{18,2},{3,19},{19,3},{4,20},{20... | collective-permute-start | bytes 2654216 | tf_op jit(solution)/shard_map/ppermute | solution.py:32
  89.7 2.4 %constant_dynamic-slice_fusion = (bf16[1024,384]{1,0:T(8,128)(2,1)S(1)}, bf16[1024,384]{1,0:T(8,128)(2,1)}) fusion(bf16[2048,384]{1,0:T(8,128)(2,1)} %param.14, s32[]{:T(128)S(6)} %select_n.73, s32[]{:T(128)S(6)} %select_n.72), kind=kLoop, calls=%fused_computation.46 | loop fusion | bytes 3145736 | tf_op jit(solution)/shard_map/dynamic_slice | solution.py:156
  95.2 1.0 copy-done.4
  96.2 6.4 %logits.1 = f32[8,136,1024]{2,1,0:T(8,128)} custom-call(bf16[16,72,384]{2,1,0:T(8,128)(2,1)} %copy-done.1, bf16[16,72,384]{2,1,0:T(8,128)(2,1)} %copy-done.4, bf16[1024,384]{1,0:T(8,128)(2,1)} %get-tuple-element.19.u_own, bf16[1024,384]{1,0:T(8,128)(2,1)} %copy-done.5), custom_call_target="tpu_custom_call" | custom-call | tf_op jit(solution)/shard_map/logits/pallas_call | solution.py:191
  102.6 4.1 %convert_element_type.19 = f16[8,136,1024]{2,1,0:T(8,128)(2,1)} convert(f32[8,136,1024]{2,1,0:T(8,128)} %logits.1) | non-fusion elementwise | flops 1114112 | bytes 6684672 | tf_op jit(solution)/shard_map/convert_element_type | solution.py:207
  106.7 4.4 %all-to-all-start.3 = ((f16[8,136,1024]{2,1,0:T(8,128)(2,1)}), f16[8,136,1024]{2,1,0:T(8,128)(2,1)}, u32[]{:S(2)}, u32[]{:S(2)}) async-start(f16[8,136,1024]{2,1,0:T(8,128)(2,1)} %convert_element_type.19), calls=%async_computation.3 | async-start | bytes 4456448 | tf_op jit(solution)/shard_map/all_to_all | solution.py:28
  113.3 48.9 %all-to-all-done.3 = f16[8,136,1024]{2,1,0:T(8,128)(2,1)} async-done(((f16[8,136,1024]{2,1,0:T(8,128)(2,1)}), f16[8,136,1024]{2,1,0:T(8,128)(2,1)}, u32[]{:S(2)}, u32[]{:S(2)}) %all-to-all-start.3) | async-done | bytes 2228256 | tf_op jit(solution)/shard_map/all_to_all | solution.py:28
  162.2 1.3 slice_convert_fusion.norms
  163.5 2.9 %convert_reduce_fusion.summed = f32[128,1024]{1,0:T(8,128)} fusion(f16[8,136,1024]{2,1,0:T(8,128)(2,1)} %all-to-all-done.3), kind=kLoop, calls=%fused_computation.2 | loop fusion | flops 1966080 | bytes 2621440 | tf_op jit(solution)/shard_map/reduce_sum | solution.py:209
  166.5 2.2 %stats.1 = f32[32,8,128]{2,1,0:T(8,128)} custom-call(f32[128,1024]{1,0:T(8,128)} %convert_reduce_fusion.summed, f32[8,8,128]{2,1,0:T(8,128)} %slice_convert_fusion.norms, s32[128,1]{1,0:T(8,128)} %reshape.196.target), custom_call_target="tpu_custom_call" | custom-call | tf_op jit(solution)/shard_map/stats/pallas_call | solution.py:227
  168.7 7.5 %all-to-all-start.4 = ((f32[32,8,128]{2,1,0:T(8,128)}), f32[32,8,128]{2,1,0:T(8,128)S(1)}, u32[]{:S(2)}, u32[]{:S(2)}) async-start(f32[32,8,128]{2,1,0:T(8,128)} %stats.1), calls=%async_computation.4 | async-start | bytes 262144 | tf_op jit(solution)/shard_map/all_to_all | solution.py:28
  177.4 6.3 %all-to-all-done.4 = f32[32,8,128]{2,1,0:T(8,128)S(1)} async-done(((f32[32,8,128]{2,1,0:T(8,128)}), f32[32,8,128]{2,1,0:T(8,128)S(1)}, u32[]{:S(2)}, u32[]{:S(2)}) %all-to-all-start.4) | async-done | bytes 131104 | tf_op jit(solution)/shard_map/all_to_all | solution.py:28
  184.3 3.3 %all-to-all-start.5 = ((f32[8,8,128]{2,1,0:T(8,128)}), f32[8,8,128]{2,1,0:T(8,128)S(1)}, u32[]{:S(2)}, u32[]{:S(2)}) async-start(f32[8,8,128]{2,1,0:T(8,128)} %broadcast_in_dim.149), calls=%async_computation.5 | async-start | bytes 65536 | tf_op jit(solution)/shard_map/all_to_all | solution.py:28
  187.7 6.7 %all-to-all-done.5 = f32[8,8,128]{2,1,0:T(8,128)S(1)} async-done(((f32[8,8,128]{2,1,0:T(8,128)}), f32[8,8,128]{2,1,0:T(8,128)S(1)}, u32[]{:S(2)}, u32[]{:S(2)}) %all-to-all-start.5) | async-done | bytes 32800 | tf_op jit(solution)/shard_map/all_to_all | solution.py:28
  (63 shorter events, 13.6 us)
Async XLA Ops:
  0.6 4.2 %copy-start = (bf16[3,1024,384]{2,1,0:T(8,128)(2,1)S(1)}, bf16[3,1024,384]{2,1,0:T(8,128)(2,1)}, u32[]{:S(2)}) copy-start(bf16[3,1024,384]{2,1,0:T(8,128)(2,1)} %param.9) | copy-start | bytes 7077892
  37.3 4.5 %copy-start.2 = (bf16[8,136,384]{2,1,0:T(8,128)(2,1)}, bf16[8,136,384]{2,1,0:T(8,128)(2,1)S(1)}, u32[]{:S(2)}) copy-start(bf16[8,136,384]{2,1,0:T(8,128)(2,1)S(1)} %all_to_all.30.own) | copy-start | bytes 2506756
  37.3 4.5 %collective-permute-start = (bf16[8,136,384]{2,1,0:T(8,128)(2,1)S(1)}, bf16[8,136,384]{2,1,0:T(8,128)(2,1)}, u32[]{:S(2)}, u32[]{:S(2)}) collective-permute-start(bf16[8,136,384]{2,1,0:T(8,128)(2,1)S(1)} %all_to_all.30.own), channel_id=1, source_target_pairs={{0,16},{16,0},{1,17},{17,1},{2,18},{18,2},{3,19},{19,3},{4,20},{20... | collective-permute-start | bytes 2506760 | tf_op jit(solution)/shard_map/ppermute | solution.py:32
  40.4 12.2 %copy-start.7 = (f32[384]{0:T(512)S(1)}, f32[384]{0:T(512)}, u32[]{:S(2)}) copy-start(f32[384]{0:T(512)} %param.13) | copy-start | bytes 4612
  40.4 12.8 %copy-start.6 = (f32[3,384]{1,0:T(4,128)S(1)}, f32[3,384]{1,0:T(4,128)}, u32[]{:S(2)}) copy-start(f32[3,384]{1,0:T(4,128)} %param.12) | copy-start | bytes 13828
  45.8 20.3 %all-to-all-start.1 = ((bf16[16,64,384]{2,1,0:T(8,128)(2,1)}), bf16[16,64,384]{2,1,0:T(8,128)(2,1)S(1)}, u32[]{:S(2)}, u32[]{:S(2)}) async-start(bf16[16,64,384]{2,1,0:T(8,128)(2,1)} %bitcast.46), calls=%async_computation.1 | async-start | bytes 1572864 | tf_op jit(solution)/shard_map/all_to_all | solution.py:28
  66.1 0.9 copy-start.3
  69.6 17.3 %all-to-all-start.2 = ((bf16[16,72,384]{2,1,0:T(8,128)(2,1)}), bf16[16,72,384]{2,1,0:T(8,128)(2,1)S(1)}, u32[]{:S(2)}, u32[]{:S(2)}) async-start(bf16[16,72,384]{2,1,0:T(8,128)(2,1)} %scale.1), calls=%async_computation.2 | async-start | bytes 1769472 | tf_op jit(solution)/shard_map/all_to_all | solution.py:28
  86.9 9.3 %copy-start.1 = (bf16[16,72,384]{2,1,0:T(8,128)(2,1)}, bf16[16,72,384]{2,1,0:T(8,128)(2,1)S(1)}, u32[]{:S(2)}) copy-start(bf16[16,72,384]{2,1,0:T(8,128)(2,1)S(1)} %all-to-all-done.2.y_own) | copy-start | bytes 2654212
  86.9 7.4 %collective-permute-start.1 = (bf16[16,72,384]{2,1,0:T(8,128)(2,1)S(1)}, bf16[16,72,384]{2,1,0:T(8,128)(2,1)S(1)}, u32[]{:S(2)}, u32[]{:S(2)}) collective-permute-start(bf16[16,72,384]{2,1,0:T(8,128)(2,1)S(1)} %all-to-all-done.2.y_own), channel_id=1, source_target_pairs={{0,16},{16,0},{1,17},{17,1},{2,18},{18,2},{3,19},{19,3},{4,20},{20... | collective-permute-start | bytes 2654216 | tf_op jit(solution)/shard_map/ppermute | solution.py:32
  92.1 2.3 %collective-permute-start.2 = (bf16[1024,384]{1,0:T(8,128)(2,1)S(1)}, bf16[1024,384]{1,0:T(8,128)(2,1)S(1)}, u32[]{:S(2)}, u32[]{:S(2)}) collective-permute-start(bf16[1024,384]{1,0:T(8,128)(2,1)S(1)} %get-tuple-element.18), channel_id=1, source_target_pairs={{0,16},{16,0},{1,17},{17,1},{2,18},{18,2},{3,19},{19,3},{4,20},{20... | collective-permute-start | bytes 2359304 | tf_op jit(solution)/shard_map/ppermute | solution.py:32
  94.4 0.9 copy-start.5
  95.2 1.0 copy-start.4
  106.7 55.5 %all-to-all-start.3 = ((f16[8,136,1024]{2,1,0:T(8,128)(2,1)}), f16[8,136,1024]{2,1,0:T(8,128)(2,1)}, u32[]{:S(2)}, u32[]{:S(2)}) async-start(f16[8,136,1024]{2,1,0:T(8,128)(2,1)} %convert_element_type.19), calls=%async_computation.3 | async-start | bytes 4456448 | tf_op jit(solution)/shard_map/all_to_all | solution.py:28
  168.7 15.0 %all-to-all-start.4 = ((f32[32,8,128]{2,1,0:T(8,128)}), f32[32,8,128]{2,1,0:T(8,128)S(1)}, u32[]{:S(2)}, u32[]{:S(2)}) async-start(f32[32,8,128]{2,1,0:T(8,128)} %stats.1), calls=%async_computation.4 | async-start | bytes 262144 | tf_op jit(solution)/shard_map/all_to_all | solution.py:28
  184.3 10.1 %all-to-all-start.5 = ((f32[8,8,128]{2,1,0:T(8,128)}), f32[8,8,128]{2,1,0:T(8,128)S(1)}, u32[]{:S(2)}, u32[]{:S(2)}) async-start(f32[8,8,128]{2,1,0:T(8,128)} %broadcast_in_dim.149), calls=%async_computation.5 | async-start | bytes 65536 | tf_op jit(solution)/shard_map/all_to_all | solution.py:28

commit v2 on v1

v2 whole, which is shorter than its diff:
```python
import jax
import jax.numpy as jnp
from jax import lax
from jax.experimental import pallas as pl
from jax.experimental.pallas import tpu as pltpu
from jax.sharding import Mesh
from jax.sharding import PartitionSpec as P


D = 6144
LAYERS = 3
CAP = 32
ROWS = 256
Z = ("zq", "zp")
SEQ = ("zq", "zp", "c")
VOCAB = ("y", "x")
F32 = jnp.float32
BF16 = jnp.bfloat16
NT = (((1,), (1,)), ((), ()))
TN = (((0,), (0,)), ((), ()))
INFO = 128
SHIFT = 16.0


def dot(a, b):
    return jnp.dot(a, b, preferred_element_type=F32)


def exchange(value, axes):
    return lax.all_to_all(value, axes, split_axis=0, concat_axis=0, tiled=True)


def swap_cores(value):
    return lax.ppermute(value, "c", [(0, 1), (1, 0)])


def whole(shape, dtype):
    return jax.ShapeDtypeStruct(shape, dtype)


def translate_kernel(flags, own, other, translator, out, info):
    low_core = flags[0] == 0
    keep = flags[1].astype(F32)
    lane = lax.broadcasted_iota(jnp.int32, (CAP, ROWS), 1).astype(F32)
    slot = lax.broadcasted_iota(jnp.int32, (CAP, ROWS), 0).astype(F32)
    base = jnp.zeros((1, 1), F32)
    pick_own, pick_other = [], []
    for k in range(8):
        count_own = own[k, INFO + 2 : INFO + 3, 0:1].astype(F32)
        count_other = other[k, INFO + 2 : INFO + 3, 0:1].astype(F32)
        start_own = base + jnp.where(low_core, 0.0, count_other)
        start_other = base + jnp.where(low_core, count_own, 0.0)
        hit_own = (lane == start_own + slot) & (slot < count_own)
        hit_other = (lane == start_other + slot) & (slot < count_other)
        pick_own.append(jnp.where(hit_own, 1.0, 0.0).astype(BF16))
        pick_other.append(jnp.where(hit_other, 1.0, 0.0).astype(BF16))
        base = base + count_own + count_other
        a = own[k, INFO : INFO + 8, 0:128].astype(F32)
        b = other[k, INFO : INFO + 8, 0:128].astype(F32)
        info[2 * k] = jnp.where(low_core, a, b)
        info[2 * k + 1] = jnp.where(low_core, b, a)
    pick_own = jnp.concatenate(pick_own, axis=0)
    pick_other = jnp.concatenate(pick_other, axis=0)
    for layer in range(LAYERS + 1):
        low = layer * CAP
        a = own[:, low : low + CAP, :].reshape(ROWS, -1)
        b = other[:, low : low + CAP, :].reshape(ROWS, -1)
        rows = lax.dot_general(pick_own, a, TN, preferred_element_type=F32)
        rows = rows + lax.dot_general(pick_other, b, TN, preferred_element_type=F32)
        part = rows * keep
        if layer < LAYERS:
            part = part + dot(rows.astype(BF16), translator[layer])
        out[:, layer] = part.astype(BF16).reshape(16, 16, -1)


def high_low(value):
    high = value.astype(BF16).astype(F32)
    row = lax.broadcasted_iota(jnp.int32, value.shape, 0)
    return jnp.where(row == 0, high, jnp.where(row == 1, value - high, 0.0))


def scale_kernel(parts, bias, gain, y_out):
    x = parts[0].astype(F32)
    for k in range(1, 16):
        x = x + parts[k].astype(F32)
    x = x + bias[...]
    y = (x * gain[...]).astype(BF16)
    square = x * x
    square = jnp.concatenate([square] * 4, axis=0)
    ones = jnp.ones((8, x.shape[1]), F32)
    squares = lax.dot_general(ones, square, NT, precision=lax.Precision.HIGHEST, preferred_element_type=F32)
    squares = high_low(squares)
    for k in range(32):
        y_out[k, 0:64] = y
        y_out[k, 64:72] = jnp.zeros((8, x.shape[1]), BF16)
        y_out[k, 64:72, 0:256] = squares.astype(BF16)


def logits_kernel(flags, y_own, y_other, u0, u1, u2, u3, out):
    pair = flags[2]
    part = jnp.zeros((1024, u0.shape[0]), F32)
    for k in range(2):
        at = pl.ds(16 * (pair if k == 0 else 1 - pair), 16)
        a = y_own[at, 0:64, :].reshape(1024, -1)
        b = y_other[at, 0:64, :].reshape(1024, -1)
        part = part + lax.dot_general(a, (u0, u2)[k][...], NT, preferred_element_type=F32)
        part = part + lax.dot_general(b, (u1, u3)[k][...], NT, preferred_element_type=F32)
    out[:, 0:256, :] = (part * (1.0 / SHIFT)).reshape(4, 256, -1)
    out[:, 256:264, :] = jnp.zeros((4, 8, out.shape[2]), F32)
    lane = lax.broadcasted_iota(jnp.int32, (8, 256), 1)
    for k in range(4):
        square = jnp.zeros((8, 256), F32)
        for j in range(4):
            total = jnp.zeros((1, 256), F32)
            for half in range(2):
                at = 16 * half + 4 * k + j
                both = y_own[at, 64:72, 0:256].astype(F32) + y_other[at, 64:72, 0:256].astype(F32)
                total = total + both[0:1] + both[1:2]
            square = jnp.where(lane // 64 == j, jnp.broadcast_to(total, (8, 256)), square)
        out[k, 256:264, 0:256] = high_low(jnp.sqrt(square) * (1.0 / SHIFT))


def stats_kernel(summed, norms, target, out):
    square = jnp.zeros((1, 256), F32)
    for k in range(4):
        norm = norms[k, 0:1] + norms[k, 1:2]
        square = square + norm * norm
    factor = SHIFT * lax.rsqrt(square * (SHIFT * SHIFT / D) + 1e-05)
    factor = jnp.broadcast_to(factor, (128, 256)).T[:, 0:1]
    logits = summed[...] * factor
    width = logits.shape[1]
    expz = jnp.exp(logits)
    total = jnp.sum(expz, axis=1, keepdims=True)
    ids = lax.broadcasted_iota(jnp.int32, logits.shape, 1)
    picked = jnp.sum(jnp.where(ids == target[...], logits, 0.0), axis=1, keepdims=True)
    four = logits.reshape(4, 4, 16, width)
    last = expz.reshape(4, 4, 16, width)[:, 3:]
    cross = jnp.sum(last * (four[:, 3:] - four), axis=3, keepdims=True).reshape(256, 1)
    lane = lax.broadcasted_iota(jnp.int32, (256, 128), 1)
    table = jnp.where(lane == 0, total, jnp.where(lane == 1, cross, jnp.where(lane == 2, picked, 0.0)))
    rows = table.T[:8]
    for k in range(64):
        out[k] = rows


def body(
    probe_states,
    final_states,
    translator,
    translator_bias,
    norm_gain,
    unembed,
    answer_rows,
    answer_count,
    targets,
):
    zq = lax.axis_index("zq")
    c = lax.axis_index("c")
    quarter = 2 * lax.axis_index("zp") + c
    v = lax.axis_index(VOCAB)
    seq = 4 * zq + quarter
    width = probe_states.shape[2]
    part = unembed.shape[0] // 4
    picks = answer_rows[0]

    info = jnp.concatenate(
        [targets // 256, targets % 256, jnp.broadcast_to(answer_count[:, None], (1, CAP)), jnp.zeros((5, CAP), jnp.int32)]
    )
    info = jnp.pad(info, ((0, 0), (0, width - CAP))).astype(BF16)
    local = jnp.concatenate(
        [
            jnp.take(probe_states, picks, axis=1, mode="clip").reshape(LAYERS * CAP, width),
            jnp.take(final_states, picks, axis=0, mode="clip"),
            info,
        ],
        axis=0,
    )
    own = exchange(jnp.broadcast_to(local[None], (8, *local.shape)), Z)
    other = swap_cores(own)

    flags = jnp.stack([c, (seq == v).astype(jnp.int32), quarter // 2])
    parts, every_info = pl.pallas_call(
        translate_kernel,
        out_shape=(whole((16, 4, 16, width), BF16), whole((16, 8, 128), F32)),
        in_specs=[pl.BlockSpec(memory_space=pltpu.SMEM)] + [pl.BlockSpec(memory_space=pltpu.VMEM)] * 3,
        name="translate",
    )(flags, own, other, translator)
    arrived = exchange(parts.reshape(16, 64, width), VOCAB)
    fours = unembed.reshape(4, part, width)
    quarters = []
    for k in range(4):
        block = lax.dynamic_index_in_dim(fours, quarter ^ k, 0, keepdims=False)
        if k:
            block = lax.ppermute(block, ("zp", "c"), [(j, j ^ k) for j in range(4)])
        quarters.append(block)

    bias = jnp.concatenate([translator_bias, jnp.zeros((1, width), F32)], axis=0)
    bias = jnp.repeat(bias, 16, axis=0)
    y_copies = pl.pallas_call(scale_kernel, out_shape=whole((32, 72, width), BF16), name="scale")(
        arrived, bias, norm_gain[None, :]
    )
    y_own = exchange(y_copies, ("zp", *VOCAB))
    y_other = swap_cores(y_own)

    product = pl.pallas_call(
        logits_kernel,
        out_shape=whole((4, 264, part), F32),
        in_specs=[pl.BlockSpec(memory_space=pltpu.SMEM)] + [pl.BlockSpec(memory_space=pltpu.VMEM)] * 6,
        name="logits",
    )(flags, y_own, y_other, *quarters)
    every_info, product = lax.optimization_barrier((every_info, product))
    logit_parts = exchange(product.astype(jnp.float16), "zq")
    norms = logit_parts[:, 256:264, :256].astype(F32)
    summed = jnp.sum(logit_parts[:, :256].astype(F32), axis=0)

    every_info = every_info[:, :3, :CAP].astype(jnp.int32)
    counts = every_info[:, 2, 0]
    all_targets = every_info[:, 0] * 256 + every_info[:, 1]
    order = jnp.arange(16, dtype=jnp.int32)
    starts = jnp.sum(jnp.where(order[None, :] < order[:, None], counts[None, :], 0), axis=1)
    slots = jnp.arange(CAP, dtype=jnp.int32)
    place = jnp.where(slots[None, :] < counts[:, None], starts[:, None] + slots[None, :], -1)
    row_ids = zq * 64 + jnp.arange(64, dtype=jnp.int32)
    hit = place[None] == row_ids[:, None, None]
    row_targets = jnp.sum(jnp.where(hit, all_targets[None], 0), axis=(1, 2))
    local_targets = row_targets - (v * 4 + quarter) * part
    item_targets = jnp.broadcast_to(local_targets.reshape(4, 1, 16), (4, 4, 16)).reshape(256, 1)
    stats = pl.pallas_call(stats_kernel, out_shape=whole((64, 8, 256), F32), name="stats")(
        summed, norms, item_targets
    )
    sums = jnp.sum(exchange(stats, ("zp", "c", *VOCAB)), axis=0)
    every = exchange(jnp.broadcast_to(sums[None], (4, 8, 256)), "zq")

    table = every[:, :3].reshape(4, 3, 4, 4, 16).transpose(1, 3, 0, 2, 4).reshape(3, 4, 1, ROWS)
    my_start = jnp.sum(jnp.where(order == seq, starts, 0))
    live = slots < answer_count[0]
    wanted = my_start + slots
    mine = wanted[:, None] == jnp.arange(ROWS, dtype=jnp.int32)[None, :]
    mine = jnp.sum(jnp.where(mine[None, None], table, 0.0), axis=3)
    log_total = jnp.log(mine[0])
    logprob = mine[2] - log_total
    divergence = mine[1, :LAYERS] / mine[0, LAYERS:] - log_total[LAYERS:] + log_total[:LAYERS]
    logprob = jnp.where(live[None], logprob, 0.0)[:, None, :]
    divergence = jnp.where(live[None], divergence, 0.0)[:, None, :]
    return (logprob, divergence)


def solution(mesh):
    split = Mesh(mesh.devices.reshape(4, 2, 2, 4, 4), ("zq", "zp", "c", "y", "x"))
    return jax.shard_map(
        body,
        mesh=split,
        in_specs=(
            P(None, SEQ, VOCAB),
            P(SEQ, VOCAB),
            P(None, VOCAB, SEQ),
            P(None, SEQ),
            P(SEQ),
            P(VOCAB, SEQ),
            P(SEQ, None),
            P(SEQ),
            P(SEQ, None),
        ),
        out_specs=(P(None, SEQ, None), P(None, SEQ, None)),
        check_vma=False,
    )
```

time: 197 us -> 198 us (level)
  blocking collectives: 31.5 us -> 58.7 us
  waiting for transfers between devices: 90.5 us -> 71.9 us
  other arithmetic: 13.5 us -> 9.08 us
  local copies, waits for them, and re-layouts: 12.9 us -> 10.2 us
    all_to_all x5 -> x4, waiting for transfers between devices: 88.5 us -> 53.8 us  [exchange(): return lax.all_to_all(value, axes, split_axis=0, concat_axis=0, tiled=True)]
    all_to_all x1 -> x2, blocking collectives: 31.5 us -> 58.7 us  [exchange(): return lax.all_to_all(value, axes, split_axis=0, concat_axis=0, tiled=True)]
    ppermute x0 -> x3, waiting for transfers between devices: none -> 16.6 us  [body(): block = lax.ppermute(block, ('zp', 'c'), [(j, j ^ k) for j in range(4)])]
    all_to_all x5 -> x4, starting transfers between devices: 25.6 us -> 21.9 us  [exchange(): return lax.all_to_all(value, axes, split_axis=0, concat_axis=0, tiled=True)]
    dynamic_slice x1 -> x0, local copies, waits for them, and re-layouts: 2.41 us -> none  [body(): lax.dynamic_slice_in_dim(unembed, (1 - c) * half, half, 0)]
    squeeze x0 -> x1, local copies, waits for them, and re-layouts: none -> 2.25 us  [body(): block = lax.dynamic_index_in_dim(fours, quarter ^ k, 0, keepdims=False)]
    ppermute x0 -> x3, starting transfers between devices: none -> 2.14 us  [body(): block = lax.ppermute(block, ('zp', 'c'), [(j, j ^ k) for j in range(4)])]
    convert_element_type x2 -> x3, other arithmetic: 5.42 us -> 3.48 us  [the longest x1 2.86 us: body(): logit_parts = exchange(product.astype(jnp.float16), 'zq')]
  transfers between devices with their start and end apart: 8 -> 9, of which waited for: 7 -> 7; matrix products, arithmetic and copies ran while one was open for 4% -> 3% of each run, Pallas kernels for 0% -> 0%
where the time goes in v2:
time: 198 us; the launch traced here: 197 us
  waiting for transfers between devices  71.9 us (36%)
  blocking collectives  58.7 us (30%)
  starting transfers between devices  29.8 us (15%)
  Pallas kernels  15.4 us (8%)
  local copies, waits for them, and re-layouts  10.2 us (5%)
  other arithmetic  9.08 us (5%)
    all_to_all x2, blocking collectives, exchange(): return lax.all_to_all(value, axes, split_axis=0, concat_axis=0, tiled=True)  58.7 us
    all_to_all x4, waiting for transfers between devices, exchange(): return lax.all_to_all(value, axes, split_axis=0, concat_axis=0, tiled=True)  53.8 us
    all_to_all x4, starting transfers between devices, exchange(): return lax.all_to_all(value, axes, split_axis=0, concat_axis=0, tiled=True)  21.9 us
    ppermute x3, waiting for transfers between devices, body(): block = lax.ppermute(block, ('zp', 'c'), [(j, j ^ k) for j in range(4)])  16.6 us
    pallas_call x1, Pallas kernels, body(): pl.pallas_call(logits_kernel, out_shape=whole((4, 264, part), F32), in_sp...  6.14 us
    ppermute x2, starting transfers between devices, swap_cores(): return lax.ppermute(value, 'c', [(0, 1), (1, 0)])  5.77 us
  transfers between devices with their start and end apart: 9, of which 7 were waited for; matrix products, arithmetic and copies ran while one was open for 3% of the time, Pallas kernels for 0%

profile of v2, /device:TPU:1, one launch (start us, length us, event | category | flops | bytes accessed | tf_op | source)
XLA Modules:
  0.0 196.8 jit_solution(6219674764060058079)
XLA Ops:
  2.9 1.9 gather_fusion.1
  5.8 31.5 %all_to_all.30.own = bf16[8,136,384]{2,1,0:T(8,128)(2,1)S(1)} all-to-all(bf16[8,136,384]{2,1,0:T(8,128)(2,1)S(1)} %broadcast_in_dim.137), channel_id=1, replica_groups=mesh['zq'=4,'zp'=2,'c'=2,'y'=4,'x'=4] {'zq','zp'}, dimensions={0} | all-to-all | bytes 1671168 | tf_op jit(solution)/shard_map/all_to_all | solution.py:30
  37.3 2.4 %collective-permute-start = (bf16[8,136,384]{2,1,0:T(8,128)(2,1)S(1)}, bf16[8,136,384]{2,1,0:T(8,128)(2,1)}, u32[]{:S(2)}, u32[]{:S(2)}) collective-permute-start(bf16[8,136,384]{2,1,0:T(8,128)(2,1)S(1)} %all_to_all.30.own), channel_id=1, source_target_pairs={{0,16},{16,0},{1,17},{17,1},{2,18},{18,2},{3,19},{19,3},{4,20},{20... | collective-permute-start | bytes 2506760 | tf_op jit(solution)/shard_map/ppermute | solution.py:34
  40.4 1.5 collective-permute-done.other
  41.8 3.9 %translate.1 = (bf16[16,4,16,384]{3,2,1,0:T(8,128)(2,1)}, f32[16,8,128]{2,1,0:T(8,128)}) custom-call(s32[3]{0:T(128)} %pad_add_fusion.flags, bf16[8,136,384]{2,1,0:T(8,128)(2,1)} %copy-done.1, bf16[8,136,384]{2,1,0:T(8,128)(2,1)} %collective-permute-done.other, bf16[3,384,384]{2,1,0:T(8,128)(2,1)} %translator.1), custom_call_target="tpu_custom_call" | custom-call | tf_op jit(solution)/shard_map/translate/pallas_call | solution.py:182
  45.8 6.8 %all-to-all-start.1 = ((bf16[16,64,384]{2,1,0:T(8,128)(2,1)}), bf16[16,64,384]{2,1,0:T(8,128)(2,1)S(1)}, u32[]{:S(2)}, u32[]{:S(2)}) async-start(bf16[16,64,384]{2,1,0:T(8,128)(2,1)} %bitcast.52), calls=%async_computation.1 | async-start | bytes 1572864 | tf_op jit(solution)/shard_map/all_to_all | solution.py:30
  53.1 12.9 %all-to-all-done.1.parts = bf16[16,64,384]{2,1,0:T(8,128)(2,1)S(1)} async-done(((bf16[16,64,384]{2,1,0:T(8,128)(2,1)}), bf16[16,64,384]{2,1,0:T(8,128)(2,1)S(1)}, u32[]{:S(2)}, u32[]{:S(2)}) %all-to-all-start.1) | async-done | bytes 786464 | tf_op jit(solution)/shard_map/all_to_all | solution.py:30
  67.0 3.0 %scale.1 = bf16[32,72,384]{2,1,0:T(8,128)(2,1)} custom-call(bf16[16,64,384]{2,1,0:T(8,128)(2,1)} %copy-done.2, f32[64,384]{1,0:T(8,128)} %bitcast.53, f32[1,384]{1,0:T(1,128)} %broadcast_in_dim.139.gain), custom_call_target="tpu_custom_call" | custom-call | tf_op jit(solution)/shard_map/scale/pallas_call | solution.py:199
  70.0 27.2 %all_to_all.31.y_own = bf16[32,72,384]{2,1,0:T(8,128)(2,1)} all-to-all(bf16[32,72,384]{2,1,0:T(8,128)(2,1)} %scale.1), channel_id=1, replica_groups=mesh['zq'=4,'zp'=2,'c'=2,'y'=4,'x'=4] {'zp','y','x'}, dimensions={0} | all-to-all | bytes 3538944 | tf_op jit(solution)/shard_map/all_to_all | solution.py:30
  97.1 3.4 %collective-permute-start.1 = (bf16[32,72,384]{2,1,0:T(8,128)(2,1)}, bf16[32,72,384]{2,1,0:T(8,128)(2,1)}, u32[]{:S(2)}, u32[]{:S(2)}) collective-permute-start(bf16[32,72,384]{2,1,0:T(8,128)(2,1)} %all_to_all.31.y_own), channel_id=1, source_target_pairs={{0,16},{16,0},{1,17},{17,1},{2,18},{18,2},{3,19},{19,3},{4,20},{20... | collective-permute-start | bytes 5308424 | tf_op jit(solution)/shard_map/ppermute | solution.py:34
  100.5 2.3 %dynamic-slice_bitcast_fusion = (bf16[512,384]{1,0:T(8,128)(2,1)S(1)}, bf16[512,384]{1,0:T(8,128)(2,1)S(1)}, bf16[512,384]{1,0:T(8,128)(2,1)S(1)}, bf16[512,384]{1,0:T(8,128)(2,1)}) fusion(bf16[4,512,384]{2,1,0:T(8,128)(2,1)} %bitcast.51, s32[]{:T(128)S(6)} %select_n.74, s32[]{:T(128)S(6)} %select_n.73, s32[]{:T(128)S(6)} %select_n.72, s32[]{:T(128)S(6)} %select_n.71), kind=kLoop, calls=%fused_computation.4 | loop fusion | bytes 3145744 | tf_op jit(solution)/shard_map/jit(dynamic_index_in_dim)/squeeze | solution.py:192
  103.2 1.0 collective-permute-start.3
  104.9 9.3 %collective-permute-done.4.u3 = bf16[512,384]{1,0:T(8,128)(2,1)S(1)} collective-permute-done((bf16[512,384]{1,0:T(8,128)(2,1)S(1)}, bf16[512,384]{1,0:T(8,128)(2,1)S(1)}, u32[]{:S(2)}, u32[]{:S(2)}) %collective-permute-start.4) | collective-permute-done | bytes 393248 | tf_op jit(solution)/shard_map/ppermute | solution.py:194
  114.2 7.3 %collective-permute-done.3.u2 = bf16[512,384]{1,0:T(8,128)(2,1)S(1)} collective-permute-done((bf16[512,384]{1,0:T(8,128)(2,1)S(1)}, bf16[512,384]{1,0:T(8,128)(2,1)S(1)}, u32[]{:S(2)}, u32[]{:S(2)}) %collective-permute-start.3) | collective-permute-done | bytes 393248 | tf_op jit(solution)/shard_map/ppermute | solution.py:194
  122.4 6.1 %logits.1 = f32[4,264,512]{2,1,0:T(8,128)} custom-call(s32[3]{0:T(128)} %pad_add_fusion.flags, bf16[32,72,384]{2,1,0:T(8,128)(2,1)} %all_to_all.31.y_own, bf16[32,72,384]{2,1,0:T(8,128)(2,1)} %collective-permute-done.1.y_other, bf16[512,384]{1,0:T(8,128)(2,1)} %get-tuple-element.23.u0, bf16[512,384]{1,0:T(8,128)(2,1)} %copy-done.5, ...), custom_call_target="tpu_custom_call" | custom-call | tf_op jit(solution)/shard_map/logits/pallas_call | solution.py:205
  128.6 2.9 %convert_element_type.15 = f16[4,264,512]{2,1,0:T(8,128)(2,1)} convert(f32[4,264,512]{2,1,0:T(8,128)} %logits.1) | non-fusion elementwise | flops 540672 | bytes 3244032 | tf_op jit(solution)/shard_map/convert_element_type | solution.py:212
  131.4 3.6 %all-to-all-start.3 = ((f16[4,264,512]{2,1,0:T(8,128)(2,1)}), f16[4,264,512]{2,1,0:T(8,128)(2,1)S(1)}, u32[]{:S(2)}, u32[]{:S(2)}) async-start(f16[4,264,512]{2,1,0:T(8,128)(2,1)} %convert_element_type.15), calls=%async_computation.3 | async-start | bytes 2162688 | tf_op jit(solution)/shard_map/all_to_all | solution.py:30
  136.8 24.0 %all-to-all-done.3 = f16[4,264,512]{2,1,0:T(8,128)(2,1)S(1)} async-done(((f16[4,264,512]{2,1,0:T(8,128)(2,1)}), f16[4,264,512]{2,1,0:T(8,128)(2,1)S(1)}, u32[]{:S(2)}, u32[]{:S(2)}) %all-to-all-start.3) | async-done | bytes 1081376 | tf_op jit(solution)/shard_map/all_to_all | solution.py:30
  161.4 0.9 convert_reduce_fusion.summed
  162.4 2.3 %stats.1 = f32[64,8,256]{2,1,0:T(8,128)} custom-call(f32[256,512]{1,0:T(8,128)} %convert_reduce_fusion.summed, f32[4,8,256]{2,1,0:T(8,128)} %slice_convert_fusion.1.norms, s32[256,1]{1,0:T(8,128)} %reshape.196.target), custom_call_target="tpu_custom_call" | custom-call | tf_op jit(solution)/shard_map/stats/pallas_call | solution.py:228
  164.7 8.2 %all-to-all-start.4 = ((f32[64,8,256]{2,1,0:T(8,128)}), f32[64,8,256]{2,1,0:T(8,128)S(1)}, u32[]{:S(2)}, u32[]{:S(2)}) async-start(f32[64,8,256]{2,1,0:T(8,128)} %stats.1), calls=%async_computation.4 | async-start | bytes 1048576 | tf_op jit(solution)/shard_map/all_to_all | solution.py:30
  174.2 10.2 %all-to-all-done.4 = f32[64,8,256]{2,1,0:T(8,128)S(1)} async-done(((f32[64,8,256]{2,1,0:T(8,128)}), f32[64,8,256]{2,1,0:T(8,128)S(1)}, u32[]{:S(2)}, u32[]{:S(2)}) %all-to-all-start.4) | async-done | bytes 524320 | tf_op jit(solution)/shard_map/all_to_all | solution.py:30
  185.1 3.3 %all-to-all-start.5 = ((f32[4,8,256]{2,1,0:T(8,128)}), f32[4,8,256]{2,1,0:T(8,128)S(1)}, u32[]{:S(2)}, u32[]{:S(2)}) async-start(f32[4,8,256]{2,1,0:T(8,128)} %broadcast_in_dim.149), calls=%async_computation.5 | async-start | bytes 65536 | tf_op jit(solution)/shard_map/all_to_all | solution.py:30
  188.4 6.7 %all-to-all-done.5 = f32[4,8,256]{2,1,0:T(8,128)S(1)} async-done(((f32[4,8,256]{2,1,0:T(8,128)}), f32[4,8,256]{2,1,0:T(8,128)S(1)}, u32[]{:S(2)}, u32[]{:S(2)}) %all-to-all-start.5) | async-done | bytes 32800 | tf_op jit(solution)/shard_map/all_to_all | solution.py:30
  (64 shorter events, 12.6 us)
Async XLA Ops:
  0.6 4.2 %copy-start = (bf16[3,1024,384]{2,1,0:T(8,128)(2,1)S(1)}, bf16[3,1024,384]{2,1,0:T(8,128)(2,1)}, u32[]{:S(2)}) copy-start(bf16[3,1024,384]{2,1,0:T(8,128)(2,1)} %param.9) | copy-start | bytes 7077892
  37.3 4.5 %copy-start.1 = (bf16[8,136,384]{2,1,0:T(8,128)(2,1)}, bf16[8,136,384]{2,1,0:T(8,128)(2,1)S(1)}, u32[]{:S(2)}) copy-start(bf16[8,136,384]{2,1,0:T(8,128)(2,1)S(1)} %all_to_all.30.own) | copy-start | bytes 2506756
  37.3 4.5 %collective-permute-start = (bf16[8,136,384]{2,1,0:T(8,128)(2,1)S(1)}, bf16[8,136,384]{2,1,0:T(8,128)(2,1)}, u32[]{:S(2)}, u32[]{:S(2)}) collective-permute-start(bf16[8,136,384]{2,1,0:T(8,128)(2,1)S(1)} %all_to_all.30.own), channel_id=1, source_target_pairs={{0,16},{16,0},{1,17},{17,1},{2,18},{18,2},{3,19},{19,3},{4,20},{20... | collective-permute-start | bytes 2506760 | tf_op jit(solution)/shard_map/ppermute | solution.py:34
  40.4 12.2 %copy-start.8 = (f32[384]{0:T(512)S(1)}, f32[384]{0:T(512)}, u32[]{:S(2)}) copy-start(f32[384]{0:T(512)} %param.13) | copy-start | bytes 4612
  40.4 12.8 %copy-start.7 = (f32[3,384]{1,0:T(4,128)S(1)}, f32[3,384]{1,0:T(4,128)}, u32[]{:S(2)}) copy-start(f32[3,384]{1,0:T(4,128)} %param.12) | copy-start | bytes 13828
  45.8 20.3 %all-to-all-start.1 = ((bf16[16,64,384]{2,1,0:T(8,128)(2,1)}), bf16[16,64,384]{2,1,0:T(8,128)(2,1)S(1)}, u32[]{:S(2)}, u32[]{:S(2)}) async-start(bf16[16,64,384]{2,1,0:T(8,128)(2,1)} %bitcast.52), calls=%async_computation.1 | async-start | bytes 1572864 | tf_op jit(solution)/shard_map/all_to_all | solution.py:30
  66.1 0.9 copy-start.2
  97.1 24.4 %collective-permute-start.1 = (bf16[32,72,384]{2,1,0:T(8,128)(2,1)}, bf16[32,72,384]{2,1,0:T(8,128)(2,1)}, u32[]{:S(2)}, u32[]{:S(2)}) collective-permute-start(bf16[32,72,384]{2,1,0:T(8,128)(2,1)} %all_to_all.31.y_own), channel_id=1, source_target_pairs={{0,16},{16,0},{1,17},{17,1},{2,18},{18,2},{3,19},{19,3},{4,20},{20... | collective-permute-start | bytes 5308424 | tf_op jit(solution)/shard_map/ppermute | solution.py:34
  102.8 11.4 %collective-permute-start.4 = (bf16[512,384]{1,0:T(8,128)(2,1)S(1)}, bf16[512,384]{1,0:T(8,128)(2,1)S(1)}, u32[]{:S(2)}, u32[]{:S(2)}) collective-permute-start(bf16[512,384]{1,0:T(8,128)(2,1)S(1)} %get-tuple-element.20), channel_id=1, source_target_pairs={{0,48},{16,32},{32,16},{48,0},{1,49},{17,33},{33,17},{49,1},{2,50}... | collective-permute-start | bytes 1179656 | tf_op jit(solution)/shard_map/ppermute | solution.py:194
  103.2 18.4 %collective-permute-start.3 = (bf16[512,384]{1,0:T(8,128)(2,1)S(1)}, bf16[512,384]{1,0:T(8,128)(2,1)S(1)}, u32[]{:S(2)}, u32[]{:S(2)}) collective-permute-start(bf16[512,384]{1,0:T(8,128)(2,1)S(1)} %get-tuple-element.21), channel_id=1, source_target_pairs={{0,32},{16,48},{32,0},{48,16},{1,33},{17,49},{33,1},{49,17},{2,34}... | collective-permute-start | bytes 1179656 | tf_op jit(solution)/shard_map/ppermute | solution.py:194
  104.1 17.4 %collective-permute-start.2 = (bf16[512,384]{1,0:T(8,128)(2,1)S(1)}, bf16[512,384]{1,0:T(8,128)(2,1)S(1)}, u32[]{:S(2)}, u32[]{:S(2)}) collective-permute-start(bf16[512,384]{1,0:T(8,128)(2,1)S(1)} %get-tuple-element.22), channel_id=1, source_target_pairs={{0,16},{16,0},{32,48},{48,32},{1,17},{17,1},{33,49},{49,33},{2,18}... | collective-permute-start | bytes 1179656 | tf_op jit(solution)/shard_map/ppermute | solution.py:194
  114.2 7.4 %copy-start.3 = (bf16[512,384]{1,0:T(8,128)(2,1)}, bf16[512,384]{1,0:T(8,128)(2,1)S(1)}, u32[]{:S(2)}) copy-start(bf16[512,384]{1,0:T(8,128)(2,1)S(1)} %collective-permute-done.4.u3) | copy-start | bytes 1179652
  121.5 0.8 copy-start.4
  121.5 0.9 copy-start.5
  131.4 3.7 %copy-start.6 = (f32[16,8,128]{2,1,0:T(8,128)S(1)}, f32[16,8,128]{2,1,0:T(8,128)}, u32[]{:S(2)}) copy-start(f32[16,8,128]{2,1,0:T(8,128)} %get-tuple-element.8) | copy-start | bytes 196612
  131.4 29.4 %all-to-all-start.3 = ((f16[4,264,512]{2,1,0:T(8,128)(2,1)}), f16[4,264,512]{2,1,0:T(8,128)(2,1)S(1)}, u32[]{:S(2)}, u32[]{:S(2)}) async-start(f16[4,264,512]{2,1,0:T(8,128)(2,1)} %convert_element_type.15), calls=%async_computation.3 | async-start | bytes 2162688 | tf_op jit(solution)/shard_map/all_to_all | solution.py:30
  164.7 19.7 %all-to-all-start.4 = ((f32[64,8,256]{2,1,0:T(8,128)}), f32[64,8,256]{2,1,0:T(8,128)S(1)}, u32[]{:S(2)}, u32[]{:S(2)}) async-start(f32[64,8,256]{2,1,0:T(8,128)} %stats.1), calls=%async_computation.4 | async-start | bytes 1048576 | tf_op jit(solution)/shard_map/all_to_all | solution.py:30
  185.1 10.0 %all-to-all-start.5 = ((f32[4,8,256]{2,1,0:T(8,128)}), f32[4,8,256]{2,1,0:T(8,128)S(1)}, u32[]{:S(2)}, u32[]{:S(2)}) async-start(f32[4,8,256]{2,1,0:T(8,128)} %broadcast_in_dim.149), calls=%async_computation.5 | async-start | bytes 65536 | tf_op jit(solution)/shard_map/all_to_all | solution.py:30

commit v3 on v2

--- a/solution.py
+++ b/solution.py
@@ -35,7 +35,20 @@
 
 
 def whole(shape, dtype):
+    return pltpu.VMEM(shape, dtype)
+
+
+def far(shape, dtype):
     return jax.ShapeDtypeStruct(shape, dtype)
+
+
+def near(value):
+    return pltpu.with_memory_space_constraint(value, pltpu.VMEM)
+
+
+SCALARS = pl.BlockSpec(memory_space=pltpu.SMEM)
+VECTORS = pl.BlockSpec(memory_space=pltpu.VMEM)
+LIMIT = pltpu.CompilerParams(vmem_limit_bytes=24 * 1024 * 1024)
 
 
 def translate_kernel(flags, own, other, translator, out, info):
@@ -136,8 +149,11 @@
     four = logits.reshape(4, 4, 16, width)
     last = expz.reshape(4, 4, 16, width)[:, 3:]
     cross = jnp.sum(last * (four[:, 3:] - four), axis=3, keepdims=True).reshape(256, 1)
-    lane = lax.broadcasted_iota(jnp.int32, (256, 128), 1)
-    table = jnp.where(lane == 0, total, jnp.where(lane == 1, cross, jnp.where(lane == 2, picked, 0.0)))
+    lane = lax.broadcasted_iota(jnp.int32, (128, 128), 1)
+    table = jnp.zeros((128, 128), F32)
+    for h in range(2):
+        for k, value in enumerate((total, cross, picked)):
+            table = jnp.where(lane == 3 * h + k, value[128 * h : 128 * h + 128], table)
     rows = table.T[:8]
     for k in range(64):
         out[k] = rows
@@ -181,10 +197,12 @@
     flags = jnp.stack([c, (seq == v).astype(jnp.int32), quarter // 2])
     parts, every_info = pl.pallas_call(
         translate_kernel,
-        out_shape=(whole((16, 4, 16, width), BF16), whole((16, 8, 128), F32)),
-        in_specs=[pl.BlockSpec(memory_space=pltpu.SMEM)] + [pl.BlockSpec(memory_space=pltpu.VMEM)] * 3,
+        out_shape=(far((16, 4, 16, width), BF16), far((16, 8, 128), F32)),
+        in_specs=[SCALARS] + [VECTORS] * 3,
+        out_specs=(VECTORS, VECTORS),
+        compiler_params=LIMIT,
         name="translate",
-    )(flags, own, other, translator)
+    )(flags, near(own), near(other), translator)
     arrived = exchange(parts.reshape(16, 64, width), VOCAB)
     fours = unembed.reshape(4, part, width)
     quarters = []
@@ -196,18 +214,25 @@
 
     bias = jnp.concatenate([translator_bias, jnp.zeros((1, width), F32)], axis=0)
     bias = jnp.repeat(bias, 16, axis=0)
-    y_copies = pl.pallas_call(scale_kernel, out_shape=whole((32, 72, width), BF16), name="scale")(
-        arrived, bias, norm_gain[None, :]
-    )
+    y_copies = pl.pallas_call(
+        scale_kernel,
+        out_shape=whole((32, 72, width), BF16),
+        in_specs=[VECTORS] * 3,
+        out_specs=VECTORS,
+        compiler_params=LIMIT,
+        name="scale",
+    )(near(arrived), bias, norm_gain[None, :])
     y_own = exchange(y_copies, ("zp", *VOCAB))
     y_other = swap_cores(y_own)
 
     product = pl.pallas_call(
         logits_kernel,
         out_shape=whole((4, 264, part), F32),
-        in_specs=[pl.BlockSpec(memory_space=pltpu.SMEM)] + [pl.BlockSpec(memory_space=pltpu.VMEM)] * 6,
+        in_specs=[SCALARS] + [VECTORS] * 6,
+        out_specs=VECTORS,
+        compiler_params=LIMIT,
         name="logits",
-    )(flags, y_own, y_other, *quarters)
+    )(flags, near(y_own), near(y_other), *[near(block) for block in quarters])
     every_info, product = lax.optimization_barrier((every_info, product))
     logit_parts = exchange(product.astype(jnp.float16), "zq")
     norms = logit_parts[:, 256:264, :256].astype(F32)
@@ -225,17 +250,27 @@
     row_targets = jnp.sum(jnp.where(hit, all_targets[None], 0), axis=(1, 2))
     local_targets = row_targets - (v * 4 + quarter) * part
     item_targets = jnp.broadcast_to(local_targets.reshape(4, 1, 16), (4, 4, 16)).reshape(256, 1)
-    stats = pl.pallas_call(stats_kernel, out_shape=whole((64, 8, 256), F32), name="stats")(
-        summed, norms, item_targets
-    )
+    stats = pl.pallas_call(
+        stats_kernel,
+        out_shape=far((64, 8, 128), F32),
+        in_specs=[VECTORS] * 3,
+        out_specs=VECTORS,
+        compiler_params=LIMIT,
+        name="stats",
+    )(near(summed), near(norms), item_targets)
     sums = jnp.sum(exchange(stats, ("zp", "c", *VOCAB)), axis=0)
-    every = exchange(jnp.broadcast_to(sums[None], (4, 8, 256)), "zq")
-
-    table = every[:, :3].reshape(4, 3, 4, 4, 16).transpose(1, 3, 0, 2, 4).reshape(3, 4, 1, ROWS)
+    every = [sums]
+    for k in (1, 2, 3):
+        every.append(lax.ppermute(sums, "zq", [(j, (j + k) % 4) for j in range(4)]))
+    every = jnp.stack(every)
+
+    table = every[:, :6].reshape(4, 2, 3, 2, 4, 16).transpose(2, 4, 0, 1, 3, 5).reshape(3, 4, 1, ROWS)
+    chunk = (zq - jnp.arange(4, dtype=jnp.int32)) % 4
+    held = (chunk[:, None] * 64 + jnp.arange(64, dtype=jnp.int32)[None, :]).reshape(1, ROWS)
     my_start = jnp.sum(jnp.where(order == seq, starts, 0))
     live = slots < answer_count[0]
     wanted = my_start + slots
-    mine = wanted[:, None] == jnp.arange(ROWS, dtype=jnp.int32)[None, :]
+    mine = wanted[:, None] == held
     mine = jnp.sum(jnp.where(mine[None, None], table, 0.0), axis=3)
     log_total = jnp.log(mine[0])
     logprob = mine[2] - log_total

time: 198 us -> 186 us (0.939)
  Pallas kernels: 15.4 us -> 8.66 us
  local copies, waits for them, and re-layouts: 10.2 us -> 8.07 us
    all_to_all x4 -> x3, waiting for transfers between devices: 53.8 us -> 47 us  [exchange(): return lax.all_to_all(value, axes, split_axis=0, concat_axis=0, tiled=True)]
    pallas_call x3, Pallas kernels: 9.29 us -> 4.3 us  [the longest x1 2.57 us: body(): pl.pallas_call(translate_kernel, out_shape=(far((16, 4, 16, width), BF16)...]
    ppermute x0 -> x3, waiting for transfers between devices: none -> 4.48 us  [body(): every.append(lax.ppermute(sums, 'zq', [(j, (j + k) % 4) for j in range(4)]))]
    ppermute x0 -> x3, starting transfers between devices: none -> 4.42 us  [body(): every.append(lax.ppermute(sums, 'zq', [(j, (j + k) % 4) for j in range(4)]))]
    all_to_all x4 -> x3, starting transfers between devices: 21.9 us -> 18.1 us  [exchange(): return lax.all_to_all(value, axes, split_axis=0, concat_axis=0, tiled=True)]
  transfers between devices with their start and end apart: 9 -> 11, of which waited for: 7 -> 9; matrix products, arithmetic and copies ran while one was open for 3% -> 2% of each run, Pallas kernels for 0% -> 0%
where the time goes in v3:
time: 186 us; the launch traced here: 185 us
  waiting for transfers between devices  70.8 us (38%)
  blocking collectives  57.8 us (31%)
  starting transfers between devices  30.5 us (16%)
  Pallas kernels  8.66 us (5%)
  local copies, waits for them, and re-layouts  8.07 us (4%)
  other arithmetic  7.81 us (4%)
    all_to_all x2, blocking collectives, exchange(): return lax.all_to_all(value, axes, split_axis=0, concat_axis=0, tiled=True)  57.8 us
    all_to_all x3, waiting for transfers between devices, exchange(): return lax.all_to_all(value, axes, split_axis=0, concat_axis=0, tiled=True)  47 us
    all_to_all x3, starting transfers between devices, exchange(): return lax.all_to_all(value, axes, split_axis=0, concat_axis=0, tiled=True)  18.1 us
    ppermute x3, waiting for transfers between devices, body(): block = lax.ppermute(block, ('zp', 'c'), [(j, j ^ k) for j in range(4)])  17.2 us
    ppermute x2, starting transfers between devices, swap_cores(): return lax.ppermute(value, 'c', [(0, 1), (1, 0)])  5.82 us
    ppermute x3, waiting for transfers between devices, body(): every.append(lax.ppermute(sums, 'zq', [(j, (j + k) % 4) for j in range(4)]))  4.48 us
    ppermute x3, starting transfers between devices, body(): every.append(lax.ppermute(sums, 'zq', [(j, (j + k) % 4) for j in range(4)]))  4.42 us
    pallas_call x1, Pallas kernels, body(): pl.pallas_call(logits_kernel, out_shape=whole((4, 264, part), F32), in_sp...  4.37 us
  transfers between devices with their start and end apart: 11, of which 9 were waited for; matrix products, arithmetic and copies ran while one was open for 2% of the time, Pallas kernels for 0%

profile of v3, /device:TPU:1, one launch (start us, length us, event | category | flops | bytes accessed | tf_op | source)
XLA Modules:
  0.0 185.2 jit_solution(17946385371734197630)
XLA Ops:
  2.9 1.9 %gather_fusion.1 = bf16[32,384]{1,0:T(8,128)(2,1)S(1)} fusion(bf16[1024,384]{1,0:T(8,128)(2,1)} %param.10, s32[1024]{0:T(1024)S(1)} %pad_clamp_fusion), kind=kCustom, calls=%fused_computation.1 | custom fusion | bytes 49280 | tf_op jit(solution)/shard_map/jit(_take)/gather | solution.py:189
  5.8 31.5 %all_to_all.25.own = bf16[8,136,384]{2,1,0:T(8,128)(2,1)S(1)} all-to-all(bf16[8,136,384]{2,1,0:T(8,128)(2,1)S(1)} %broadcast_in_dim.132), channel_id=1, replica_groups=mesh['zq'=4,'zp'=2,'c'=2,'y'=4,'x'=4] {'zq','zp'}, dimensions={0} | all-to-all | bytes 1671168 | tf_op jit(solution)/shard_map/all_to_all | solution.py:30
  37.3 2.4 %collective-permute-start = (bf16[8,136,384]{2,1,0:T(8,128)(2,1)S(1)}, bf16[8,136,384]{2,1,0:T(8,128)(2,1)}, u32[]{:S(2)}, u32[]{:S(2)}) collective-permute-start(bf16[8,136,384]{2,1,0:T(8,128)(2,1)S(1)} %all_to_all.25.own), channel_id=1, source_target_pairs={{0,16},{16,0},{1,17},{17,1},{2,18},{18,2},{3,19},{19,3},{4,20},{20... | collective-permute-start | bytes 2506760 | tf_op jit(solution)/shard_map/ppermute | solution.py:34
  39.8 2.0 %collective-permute-done.other = bf16[8,136,384]{2,1,0:T(8,128)(2,1)} collective-permute-done((bf16[8,136,384]{2,1,0:T(8,128)(2,1)S(1)}, bf16[8,136,384]{2,1,0:T(8,128)(2,1)}, u32[]{:S(2)}, u32[]{:S(2)}) %collective-permute-start) | collective-permute-done | bytes 835616 | tf_op jit(solution)/shard_map/ppermute | solution.py:34
  41.8 1.2 copy-done.1
  43.0 2.6 %translate.1 = (bf16[16,4,16,384]{3,2,1,0:T(8,128)(2,1)S(1)}, f32[16,8,128]{2,1,0:T(8,128)S(1)}) custom-call(s32[3]{0:T(128)S(1)} %pad_add_fusion.flags, bf16[8,136,384]{2,1,0:T(8,128)(2,1)S(1)} %all_to_all.25.own, bf16[8,136,384]{2,1,0:T(8,128)(2,1)} %collective-permute-done.other, bf16[3,384,384]{2,1,0:T(8,128)(2,1)S(1)} %copy-done.1), custom_call_target="tpu_custom_call" | custom-call | tf_op jit(solution)/shard_map/translate/pallas_call | solution.py:198
  46.5 6.8 %all-to-all-start.1 = ((bf16[16,64,384]{2,1,0:T(8,128)(2,1)}), bf16[16,64,384]{2,1,0:T(8,128)(2,1)S(1)}, u32[]{:S(2)}, u32[]{:S(2)}) async-start(bf16[16,64,384]{2,1,0:T(8,128)(2,1)} %bitcast.61), calls=%async_computation.1 | async-start | bytes 1572864 | tf_op jit(solution)/shard_map/all_to_all | solution.py:30
  53.3 13.5 %all-to-all-done.1.parts = bf16[16,64,384]{2,1,0:T(8,128)(2,1)S(1)} async-done(((bf16[16,64,384]{2,1,0:T(8,128)(2,1)}), bf16[16,64,384]{2,1,0:T(8,128)(2,1)S(1)}, u32[]{:S(2)}, u32[]{:S(2)}) %all-to-all-start.1) | async-done | bytes 786464 | tf_op jit(solution)/shard_map/all_to_all | solution.py:30
  67.4 26.3 %all_to_all.26.y_own = bf16[32,72,384]{2,1,0:T(8,128)(2,1)} all-to-all(bf16[32,72,384]{2,1,0:T(8,128)(2,1)S(1)} %scale.1), channel_id=1, replica_groups=mesh['zq'=4,'zp'=2,'c'=2,'y'=4,'x'=4] {'zp','y','x'}, dimensions={0} | all-to-all | bytes 3538944 | tf_op jit(solution)/shard_map/all_to_all | solution.py:30
  93.7 3.4 %collective-permute-start.1 = (bf16[32,72,384]{2,1,0:T(8,128)(2,1)}, bf16[32,72,384]{2,1,0:T(8,128)(2,1)}, u32[]{:S(2)}, u32[]{:S(2)}) collective-permute-start(bf16[32,72,384]{2,1,0:T(8,128)(2,1)} %all_to_all.26.y_own), channel_id=1, source_target_pairs={{0,16},{16,0},{1,17},{17,1},{2,18},{18,2},{3,19},{19,3},{4,20},{20... | collective-permute-start | bytes 5308424 | tf_op jit(solution)/shard_map/ppermute | solution.py:34
  97.1 1.5 dynamic-slice_bitcast_fusion
  99.2 1.6 collective-permute-start.4
  101.2 7.9 %collective-permute-done.3.u2 = bf16[512,384]{1,0:T(8,128)(2,1)S(1)} collective-permute-done((bf16[512,384]{1,0:T(8,128)(2,1)S(1)}, bf16[512,384]{1,0:T(8,128)(2,1)S(1)}, u32[]{:S(2)}, u32[]{:S(2)}) %collective-permute-start.3) | collective-permute-done | bytes 393248 | tf_op jit(solution)/shard_map/ppermute | solution.py:212
  109.0 9.0 %collective-permute-done.4.u3 = bf16[512,384]{1,0:T(8,128)(2,1)S(1)} collective-permute-done((bf16[512,384]{1,0:T(8,128)(2,1)S(1)}, bf16[512,384]{1,0:T(8,128)(2,1)S(1)}, u32[]{:S(2)}, u32[]{:S(2)}) %collective-permute-start.4) | collective-permute-done | bytes 393248 | tf_op jit(solution)/shard_map/ppermute | solution.py:212
  118.0 4.4 %logits.1 = f32[4,264,512]{2,1,0:T(8,128)S(1)} custom-call(s32[3]{0:T(128)S(1)} %pad_add_fusion.flags, bf16[32,72,384]{2,1,0:T(8,128)(2,1)} %all_to_all.26.y_own, bf16[32,72,384]{2,1,0:T(8,128)(2,1)} %collective-permute-done.1.y_other, bf16[512,384]{1,0:T(8,128)(2,1)S(1)} %get-tuple-element.21.u0, bf16[512,384]{1,0:T(8,128)(2,1)S(1)} %collective-permute-done.2.u1, ...), custom_call_target="tpu_custom_call" | custom-call | tf_op jit(solution)/shard_map/logits/pallas_call | solution.py:228
  122.4 1.3 convert_element_type.15
  123.7 4.2 %all-to-all-start.3 = ((f16[4,264,512]{2,1,0:T(8,128)(2,1)}), f16[4,264,512]{2,1,0:T(8,128)(2,1)}, u32[]{:S(2)}, u32[]{:S(2)}) async-start(f16[4,264,512]{2,1,0:T(8,128)(2,1)} %convert_element_type.15), calls=%async_computation.3 | async-start | bytes 2162688 | tf_op jit(solution)/shard_map/all_to_all | solution.py:30
  129.0 25.7 %all-to-all-done.3 = f16[4,264,512]{2,1,0:T(8,128)(2,1)} async-done(((f16[4,264,512]{2,1,0:T(8,128)(2,1)}), f16[4,264,512]{2,1,0:T(8,128)(2,1)}, u32[]{:S(2)}, u32[]{:S(2)}) %all-to-all-start.3) | async-done | bytes 1081376 | tf_op jit(solution)/shard_map/all_to_all | solution.py:30
  154.8 1.4 convert_reduce_fusion.summed
  158.1 7.1 %all-to-all-start.4 = ((f32[64,8,128]{2,1,0:T(8,128)}), f32[64,8,128]{2,1,0:T(8,128)S(1)}, u32[]{:S(2)}, u32[]{:S(2)}) async-start(f32[64,8,128]{2,1,0:T(8,128)} %stats.1), calls=%async_computation.4 | async-start | bytes 524288 | tf_op jit(solution)/shard_map/all_to_all | solution.py:30
  166.6 7.8 %all-to-all-done.4 = f32[64,8,128]{2,1,0:T(8,128)S(1)} async-done(((f32[64,8,128]{2,1,0:T(8,128)}), f32[64,8,128]{2,1,0:T(8,128)S(1)}, u32[]{:S(2)}, u32[]{:S(2)}) %all-to-all-start.4) | async-done | bytes 262176 | tf_op jit(solution)/shard_map/all_to_all | solution.py:30
  174.9 4.0 %collective-permute-start.6 = (f32[8,128]{1,0:T(8,128)S(1)}, f32[8,128]{1,0:T(8,128)S(1)}, u32[]{:S(2)}, u32[]{:S(2)}) collective-permute-start(f32[8,128]{1,0:T(8,128)S(1)} %reduce_sum.58), channel_id=1, source_target_pairs={{0,128},{64,192},{128,0},{192,64},{1,129},{65,193},{129,1},{193,65... | collective-permute-start | bytes 12296 | tf_op jit(solution)/shard_map/ppermute | solution.py:264
  179.0 2.3 %collective-permute-done.6 = f32[8,128]{1,0:T(8,128)S(1)} collective-permute-done((f32[8,128]{1,0:T(8,128)S(1)}, f32[8,128]{1,0:T(8,128)S(1)}, u32[]{:S(2)}, u32[]{:S(2)}) %collective-permute-start.6) | collective-permute-done | bytes 4128 | tf_op jit(solution)/shard_map/ppermute | solution.py:264
  181.3 2.2 %collective-permute-done.5 = f32[8,128]{1,0:T(8,128)S(1)} collective-permute-done((f32[8,128]{1,0:T(8,128)S(1)}, f32[8,128]{1,0:T(8,128)S(1)}, u32[]{:S(2)}, u32[]{:S(2)}) %collective-permute-start.5) | collective-permute-done | bytes 4128 | tf_op jit(solution)/shard_map/ppermute | solution.py:264
  (61 shorter events, 11.8 us)
Async XLA Ops:
  0.6 4.2 %copy-start = (bf16[3,1024,384]{2,1,0:T(8,128)(2,1)S(1)}, bf16[3,1024,384]{2,1,0:T(8,128)(2,1)}, u32[]{:S(2)}) copy-start(bf16[3,1024,384]{2,1,0:T(8,128)(2,1)} %param.9) | copy-start | bytes 7077892
  37.3 4.5 %collective-permute-start = (bf16[8,136,384]{2,1,0:T(8,128)(2,1)S(1)}, bf16[8,136,384]{2,1,0:T(8,128)(2,1)}, u32[]{:S(2)}, u32[]{:S(2)}) collective-permute-start(bf16[8,136,384]{2,1,0:T(8,128)(2,1)S(1)} %all_to_all.25.own), channel_id=1, source_target_pairs={{0,16},{16,0},{1,17},{17,1},{2,18},{18,2},{3,19},{19,3},{4,20},{20... | collective-permute-start | bytes 2506760 | tf_op jit(solution)/shard_map/ppermute | solution.py:34
  41.8 1.2 copy-start.1
  43.0 10.2 %copy-start.4 = (f32[384]{0:T(512)S(1)}, f32[384]{0:T(512)}, u32[]{:S(2)}) copy-start(f32[384]{0:T(512)} %param.13) | copy-start | bytes 4612
  43.0 10.3 %copy-start.3 = (f32[3,384]{1,0:T(4,128)S(1)}, f32[3,384]{1,0:T(4,128)}, u32[]{:S(2)}) copy-start(f32[3,384]{1,0:T(4,128)} %param.12) | copy-start | bytes 13828
  45.6 0.9 copy-start.2
  46.5 20.3 %all-to-all-start.1 = ((bf16[16,64,384]{2,1,0:T(8,128)(2,1)}), bf16[16,64,384]{2,1,0:T(8,128)(2,1)S(1)}, u32[]{:S(2)}, u32[]{:S(2)}) async-start(bf16[16,64,384]{2,1,0:T(8,128)(2,1)} %bitcast.61), calls=%async_computation.1 | async-start | bytes 1572864 | tf_op jit(solution)/shard_map/all_to_all | solution.py:30
  93.7 24.4 %collective-permute-start.1 = (bf16[32,72,384]{2,1,0:T(8,128)(2,1)}, bf16[32,72,384]{2,1,0:T(8,128)(2,1)}, u32[]{:S(2)}, u32[]{:S(2)}) collective-permute-start(bf16[32,72,384]{2,1,0:T(8,128)(2,1)} %all_to_all.26.y_own), channel_id=1, source_target_pairs={{0,16},{16,0},{1,17},{17,1},{2,18},{18,2},{3,19},{19,3},{4,20},{20... | collective-permute-start | bytes 5308424 | tf_op jit(solution)/shard_map/ppermute | solution.py:34
  98.6 2.6 %collective-permute-start.2 = (bf16[512,384]{1,0:T(8,128)(2,1)S(1)}, bf16[512,384]{1,0:T(8,128)(2,1)S(1)}, u32[]{:S(2)}, u32[]{:S(2)}) collective-permute-start(bf16[512,384]{1,0:T(8,128)(2,1)S(1)} %get-tuple-element.20), channel_id=1, source_target_pairs={{0,16},{16,0},{32,48},{48,32},{1,17},{17,1},{33,49},{49,33},{2,18}... | collective-permute-start | bytes 1179656 | tf_op jit(solution)/shard_map/ppermute | solution.py:212
  98.7 10.4 %collective-permute-start.3 = (bf16[512,384]{1,0:T(8,128)(2,1)S(1)}, bf16[512,384]{1,0:T(8,128)(2,1)S(1)}, u32[]{:S(2)}, u32[]{:S(2)}) collective-permute-start(bf16[512,384]{1,0:T(8,128)(2,1)S(1)} %get-tuple-element.19), channel_id=1, source_target_pairs={{0,32},{16,48},{32,0},{48,16},{1,33},{17,49},{33,1},{49,17},{2,34}... | collective-permute-start | bytes 1179656 | tf_op jit(solution)/shard_map/ppermute | solution.py:212
  99.2 18.8 %collective-permute-start.4 = (bf16[512,384]{1,0:T(8,128)(2,1)S(1)}, bf16[512,384]{1,0:T(8,128)(2,1)S(1)}, u32[]{:S(2)}, u32[]{:S(2)}) collective-permute-start(bf16[512,384]{1,0:T(8,128)(2,1)S(1)} %get-tuple-element.18), channel_id=1, source_target_pairs={{0,48},{16,32},{32,16},{48,0},{1,49},{17,33},{33,17},{49,1},{2,50}... | collective-permute-start | bytes 1179656 | tf_op jit(solution)/shard_map/ppermute | solution.py:212
  123.7 31.1 %all-to-all-start.3 = ((f16[4,264,512]{2,1,0:T(8,128)(2,1)}), f16[4,264,512]{2,1,0:T(8,128)(2,1)}, u32[]{:S(2)}, u32[]{:S(2)}) async-start(f16[4,264,512]{2,1,0:T(8,128)(2,1)} %convert_element_type.15), calls=%async_computation.3 | async-start | bytes 2162688 | tf_op jit(solution)/shard_map/all_to_all | solution.py:30
  158.1 16.3 %all-to-all-start.4 = ((f32[64,8,128]{2,1,0:T(8,128)}), f32[64,8,128]{2,1,0:T(8,128)S(1)}, u32[]{:S(2)}, u32[]{:S(2)}) async-start(f32[64,8,128]{2,1,0:T(8,128)} %stats.1), calls=%async_computation.4 | async-start | bytes 524288 | tf_op jit(solution)/shard_map/all_to_all | solution.py:30
  174.5 4.5 %collective-permute-start.7 = (f32[8,128]{1,0:T(8,128)S(1)}, f32[8,128]{1,0:T(8,128)S(1)}, u32[]{:S(2)}, u32[]{:S(2)}) collective-permute-start(f32[8,128]{1,0:T(8,128)S(1)} %reduce_sum.58), channel_id=1, source_target_pairs={{0,192},{64,0},{128,64},{192,128},{1,193},{65,1},{129,65},{193,129... | collective-permute-start | bytes 12296 | tf_op jit(solution)/shard_map/ppermute | solution.py:264
  174.9 6.4 %collective-permute-start.6 = (f32[8,128]{1,0:T(8,128)S(1)}, f32[8,128]{1,0:T(8,128)S(1)}, u32[]{:S(2)}, u32[]{:S(2)}) collective-permute-start(f32[8,128]{1,0:T(8,128)S(1)} %reduce_sum.58), channel_id=1, source_target_pairs={{0,128},{64,192},{128,0},{192,64},{1,129},{65,193},{129,1},{193,65... | collective-permute-start | bytes 12296 | tf_op jit(solution)/shard_map/ppermute | solution.py:264
  178.9 4.6 %collective-permute-start.5 = (f32[8,128]{1,0:T(8,128)S(1)}, f32[8,128]{1,0:T(8,128)S(1)}, u32[]{:S(2)}, u32[]{:S(2)}) collective-permute-start(f32[8,128]{1,0:T(8,128)S(1)} %reduce_sum.58), channel_id=1, source_target_pairs={{0,64},{64,128},{128,192},{192,0},{1,65},{65,129},{129,193},{193,1... | collective-permute-start | bytes 12296 | tf_op jit(solution)/shard_map/ppermute | solution.py:264

commit v4 on v3

--- a/solution.py
+++ b/solution.py
@@ -1,3 +1,5 @@
+import functools
+
 import jax
 import jax.numpy as jnp
 from jax import lax
@@ -20,6 +22,8 @@
 TN = (((0,), (0,)), ((), ()))
 INFO = 128
 SHIFT = 16.0
+SCALE = 262144.0
+LARGE = 16.0
 
 
 def dot(a, b):
@@ -39,7 +43,7 @@
 
 
 def far(shape, dtype):
-    return jax.ShapeDtypeStruct(shape, dtype)
+    return pltpu.HBM(shape, dtype)
 
 
 def near(value):
@@ -51,7 +55,9 @@
 LIMIT = pltpu.CompilerParams(vmem_limit_bytes=24 * 1024 * 1024)
 
 
-def translate_kernel(flags, own, other, translator, out, info):
+def translate_kernel(flags, own, other, matrices, out, info, translator, arrived):
+    fetch = pltpu.make_async_copy(matrices, translator, arrived)
+    fetch.start()
     low_core = flags[0] == 0
     keep = flags[1].astype(F32)
     lane = lax.broadcasted_iota(jnp.int32, (CAP, ROWS), 1).astype(F32)
@@ -74,6 +80,7 @@
         info[2 * k + 1] = jnp.where(low_core, b, a)
     pick_own = jnp.concatenate(pick_own, axis=0)
     pick_other = jnp.concatenate(pick_other, axis=0)
+    fetch.wait()
     for layer in range(LAYERS + 1):
         low = layer * CAP
         a = own[:, low : low + CAP, :].reshape(ROWS, -1)
@@ -109,38 +116,53 @@
         y_out[k, 64:72, 0:256] = squares.astype(BF16)
 
 
-def logits_kernel(flags, y_own, y_other, u0, u1, u2, u3, out):
+def squares_of(y, chunk):
+    lane = lax.broadcasted_iota(jnp.int32, (8, 256), 1)
+    square = jnp.zeros((8, 256), F32)
+    for j in range(4):
+        total = jnp.zeros((1, 256), F32)
+        for half in range(2):
+            both = y[16 * half + 4 * chunk + j, 64:72, 0:256].astype(F32)
+            total = total + both[0:1] + both[1:2]
+        square = jnp.where(lane // 64 == j, jnp.broadcast_to(total, (8, 256)), square)
+    return square
+
+
+def own_kernel(flags, y, u_near, u_far, out):
     pair = flags[2]
-    part = jnp.zeros((1024, u0.shape[0]), F32)
-    for k in range(2):
-        at = pl.ds(16 * (pair if k == 0 else 1 - pair), 16)
-        a = y_own[at, 0:64, :].reshape(1024, -1)
-        b = y_other[at, 0:64, :].reshape(1024, -1)
-        part = part + lax.dot_general(a, (u0, u2)[k][...], NT, preferred_element_type=F32)
-        part = part + lax.dot_general(b, (u1, u3)[k][...], NT, preferred_element_type=F32)
-    out[:, 0:256, :] = (part * (1.0 / SHIFT)).reshape(4, 256, -1)
-    out[:, 256:264, :] = jnp.zeros((4, 8, out.shape[2]), F32)
-    lane = lax.broadcasted_iota(jnp.int32, (8, 256), 1)
+    a = y[pl.ds(16 * pair, 16), 0:64, :].reshape(1024, -1)
+    b = y[pl.ds(16 * (1 - pair), 16), 0:64, :].reshape(1024, -1)
+    part = lax.dot_general(a, u_near[...], NT, preferred_element_type=F32)
+    part = part + lax.dot_general(b, u_far[...], NT, preferred_element_type=F32)
+    out[:, 0:256, :] = part.reshape(4, 256, -1)
     for k in range(4):
-        square = jnp.zeros((8, 256), F32)
-        for j in range(4):
-            total = jnp.zeros((1, 256), F32)
-            for half in range(2):
-                at = 16 * half + 4 * k + j
-                both = y_own[at, 64:72, 0:256].astype(F32) + y_other[at, 64:72, 0:256].astype(F32)
-                total = total + both[0:1] + both[1:2]
-            square = jnp.where(lane // 64 == j, jnp.broadcast_to(total, (8, 256)), square)
-        out[k, 256:264, 0:256] = high_low(jnp.sqrt(square) * (1.0 / SHIFT))
-
-
-def stats_kernel(summed, norms, target, out):
-    square = jnp.zeros((1, 256), F32)
-    for k in range(4):
-        norm = norms[k, 0:1] + norms[k, 1:2]
-        square = square + norm * norm
-    factor = SHIFT * lax.rsqrt(square * (SHIFT * SHIFT / D) + 1e-05)
+        out[k, 256:264, 0:256] = squares_of(y, k)
+
+
+def chunk_kernel(step, flags, own_part, y_other, u_near, u_far, out):
+    pair = flags[2]
+    chunk = (flags[3] + step) % 4
+    a = y_other[pl.ds(16 * pair + 4 * chunk, 4), 0:64, :].reshape(256, -1)
+    b = y_other[pl.ds(16 * (1 - pair) + 4 * chunk, 4), 0:64, :].reshape(256, -1)
+    part = lax.dot_general(a, u_near[...], NT, preferred_element_type=F32)
+    part = part + lax.dot_general(b, u_far[...], NT, preferred_element_type=F32)
+    out[0:256, :] = (own_part[chunk, 0:256, :] + part) * (1.0 / SHIFT)
+    out[256:264, :] = jnp.zeros((8, out.shape[1]), F32)
+    square = own_part[chunk, 256:264, 0:256] + squares_of(y_other, chunk)
+    row = lax.broadcasted_iota(jnp.int32, square.shape, 0)
+    large = square >= LARGE
+    value = jnp.where(row < 2, jnp.where(large, square * (1.0 / SCALE), 0.0), jnp.where(large, 0.0, square))
+    high = value.astype(BF16).astype(F32)
+    value = jnp.where(row % 2 == 0, high, value - high)
+    out[256:264, 0:256] = jnp.where(row < 4, value, 0.0)
+
+
+def stats_kernel(summed, target, out):
+    rows = summed[256:264, 0:256]
+    square = (rows[0:1] + rows[1:2]) * SCALE + rows[2:3] + rows[3:4]
+    factor = SHIFT * lax.rsqrt(square * (1.0 / D) + 1e-05)
     factor = jnp.broadcast_to(factor, (128, 256)).T[:, 0:1]
-    logits = summed[...] * factor
+    logits = summed[0:256] * factor
     width = logits.shape[1]
     expz = jnp.exp(logits)
     total = jnp.sum(expz, axis=1, keepdims=True)
@@ -194,15 +216,16 @@
     own = exchange(jnp.broadcast_to(local[None], (8, *local.shape)), Z)
     other = swap_cores(own)
 
-    flags = jnp.stack([c, (seq == v).astype(jnp.int32), quarter // 2])
+    flags = jnp.stack([c, (seq == v).astype(jnp.int32), quarter // 2, zq])
     parts, every_info = pl.pallas_call(
         translate_kernel,
         out_shape=(far((16, 4, 16, width), BF16), far((16, 8, 128), F32)),
-        in_specs=[SCALARS] + [VECTORS] * 3,
+        in_specs=[SCALARS, VECTORS, VECTORS, pl.BlockSpec(memory_space=pltpu.HBM)],
         out_specs=(VECTORS, VECTORS),
+        scratch_shapes=[pltpu.VMEM(translator.shape, BF16), pltpu.SemaphoreType.DMA(())],
         compiler_params=LIMIT,
         name="translate",
-    )(flags, near(own), near(other), translator)
+    )(flags, near(own), near(other), pltpu.with_memory_space_constraint(translator, pltpu.HBM))
     arrived = exchange(parts.reshape(16, 64, width), VOCAB)
     fours = unembed.reshape(4, part, width)
     quarters = []
@@ -225,18 +248,34 @@
     y_own = exchange(y_copies, ("zp", *VOCAB))
     y_other = swap_cores(y_own)
 
-    product = pl.pallas_call(
-        logits_kernel,
+    quarters = [near(block) for block in quarters]
+    y_own, y_other = near(y_own), near(y_other)
+    own_part = pl.pallas_call(
+        own_kernel,
         out_shape=whole((4, 264, part), F32),
-        in_specs=[SCALARS] + [VECTORS] * 6,
+        in_specs=[SCALARS] + [VECTORS] * 3,
         out_specs=VECTORS,
         compiler_params=LIMIT,
-        name="logits",
-    )(flags, near(y_own), near(y_other), *[near(block) for block in quarters])
-    every_info, product = lax.optimization_barrier((every_info, product))
-    logit_parts = exchange(product.astype(jnp.float16), "zq")
-    norms = logit_parts[:, 256:264, :256].astype(F32)
-    summed = jnp.sum(logit_parts[:, :256].astype(F32), axis=0)
+        name="own_logits",
+    )(flags, y_own, quarters[0], quarters[2])
+    chunks = []
+    for k in (2, 1, 3, 0):
+        chunk = pl.pallas_call(
+            functools.partial(chunk_kernel, k),
+            out_shape=whole((264, part), F32),
+            in_specs=[SCALARS] + [VECTORS] * 4,
+            out_specs=VECTORS,
+            compiler_params=LIMIT,
+        )(flags, near(own_part), y_other, quarters[1], quarters[3])
+        if k:
+            chunk = chunk.astype(jnp.float16)
+            chunk = lax.ppermute(chunk, "zq", [(j, (j + k) % 4) for j in range(4)])
+        else:
+            every_info, chunk = lax.optimization_barrier((every_info, chunk))
+        chunks.append(chunk)
+    summed = chunks[3]
+    for chunk in chunks[:3]:
+        summed = summed + chunk.astype(F32)
 
     every_info = every_info[:, :3, :CAP].astype(jnp.int32)
     counts = every_info[:, 2, 0]
@@ -253,11 +292,11 @@
     stats = pl.pallas_call(
         stats_kernel,
         out_shape=far((64, 8, 128), F32),
-        in_specs=[VECTORS] * 3,
+        in_specs=[VECTORS] * 2,
         out_specs=VECTORS,
         compiler_params=LIMIT,
         name="stats",
-    )(near(summed), near(norms), item_targets)
+    )(near(summed), item_targets)
     sums = jnp.sum(exchange(stats, ("zp", "c", *VOCAB)), axis=0)
     every = [sums]
     for k in (1, 2, 3):

time: 186 us -> 181 us (0.973)
  waiting for transfers between devices: 70.8 us -> 57.3 us
  Pallas kernels: 8.66 us -> 16.9 us
    all_to_all x3 -> x2, waiting for transfers between devices: 47 us -> 21.3 us  [exchange(): return lax.all_to_all(value, axes, split_axis=0, concat_axis=0, tiled=True)]
    ppermute x0 -> x3, waiting for transfers between devices: none -> 17.5 us  [body(): chunk = lax.ppermute(chunk, 'zq', [(j, (j + k) % 4) for j in range(4)])]
    pallas_call x1 -> x5, Pallas kernels: 4.37 us -> 10.6 us  [the longest x4 7.81 us: body(): pl.pallas_call(functools.partial(chunk_kernel, k), out_shape=whole((264,...]
    all_to_all x3 -> x2, starting transfers between devices: 18.1 us -> 12.7 us  [exchange(): return lax.all_to_all(value, axes, split_axis=0, concat_axis=0, tiled=True)]
    ppermute x0 -> x3, starting transfers between devices: none -> 4.83 us  [body(): chunk = lax.ppermute(chunk, 'zq', [(j, (j + k) % 4) for j in range(4)])]
    ppermute x3, waiting for transfers between devices: 4.48 us -> 1.65 us  [body(): every.append(lax.ppermute(sums, 'zq', [(j, (j + k) % 4) for j in range(4)]))]
    ppermute x3, waiting for transfers between devices: 17.2 us -> 14.8 us  [body(): block = lax.ppermute(block, ('zp', 'c'), [(j, j ^ k) for j in range(4)])]
    pallas_call x1, Pallas kernels: 2.57 us -> 4.56 us  [body(): pl.pallas_call(translate_kernel, out_shape=(far((16, 4, 16, width), BF16)...]
  transfers between devices with their start and end apart: 11 -> 13, of which waited for: 9 -> 9; matrix products, arithmetic and copies ran while one was open for 2% -> 3% of each run, Pallas kernels for 0% -> 4%
where the time goes in v4:
time: 181 us; the launch traced here: 179 us
  blocking collectives  57.8 us (32%)
  waiting for transfers between devices  57.3 us (32%)
  starting transfers between devices  31.6 us (17%)
  Pallas kernels  16.9 us (9%)
  local copies, waits for them, and re-layouts  7.75 us (4%)
  other arithmetic  6.4 us (4%)
    all_to_all x2, blocking collectives, exchange(): return lax.all_to_all(value, axes, split_axis=0, concat_axis=0, tiled=True)  57.8 us
    all_to_all x2, waiting for transfers between devices, exchange(): return lax.all_to_all(value, axes, split_axis=0, concat_axis=0, tiled=True)  21.3 us
    ppermute x3, waiting for transfers between devices, body(): chunk = lax.ppermute(chunk, 'zq', [(j, (j + k) % 4) for j in range(4)])  17.5 us
    ppermute x3, waiting for transfers between devices, body(): block = lax.ppermute(block, ('zp', 'c'), [(j, j ^ k) for j in range(4)])  14.8 us
    all_to_all x2, starting transfers between devices, exchange(): return lax.all_to_all(value, axes, split_axis=0, concat_axis=0, tiled=True)  12.7 us
    pallas_call x4, Pallas kernels, body(): pl.pallas_call(functools.partial(chunk_kernel, k), out_shape=whole((264,...  7.81 us
    ppermute x3, starting transfers between devices, body(): every.append(lax.ppermute(sums, 'zq', [(j, (j + k) % 4) for j in range(4)]))  6.34 us
    ppermute x2, starting transfers between devices, swap_cores(): return lax.ppermute(value, 'c', [(0, 1), (1, 0)])  5.82 us
  transfers between devices with their start and end apart: 13, of which 9 were waited for; matrix products, arithmetic and copies ran while one was open for 3% of the time, Pallas kernels for 4%

profile of v4, /device:TPU:1, one launch (start us, length us, event | category | flops | bytes accessed | tf_op | source)
XLA Modules:
  0.0 179.4 jit_solution(17568422936419251438)
XLA Ops:
  5.8 31.5 %all_to_all.20.own = bf16[8,136,384]{2,1,0:T(8,128)(2,1)S(1)} all-to-all(bf16[8,136,384]{2,1,0:T(8,128)(2,1)S(1)} %broadcast_in_dim.132), channel_id=1, replica_groups=mesh['zq'=4,'zp'=2,'c'=2,'y'=4,'x'=4] {'zq','zp'}, dimensions={0} | all-to-all | bytes 1671168 | tf_op jit(solution)/shard_map/all_to_all | solution.py:34
  37.3 2.4 %collective-permute-start = (bf16[8,136,384]{2,1,0:T(8,128)(2,1)S(1)}, bf16[8,136,384]{2,1,0:T(8,128)(2,1)}, u32[]{:S(2)}, u32[]{:S(2)}) collective-permute-start(bf16[8,136,384]{2,1,0:T(8,128)(2,1)S(1)} %all_to_all.20.own), channel_id=1, source_target_pairs={{0,16},{16,0},{1,17},{17,1},{2,18},{18,2},{3,19},{19,3},{4,20},{20... | collective-permute-start | bytes 2506760 | tf_op jit(solution)/shard_map/ppermute | solution.py:38
  39.8 2.0 %collective-permute-done.other = bf16[8,136,384]{2,1,0:T(8,128)(2,1)} collective-permute-done((bf16[8,136,384]{2,1,0:T(8,128)(2,1)S(1)}, bf16[8,136,384]{2,1,0:T(8,128)(2,1)}, u32[]{:S(2)}, u32[]{:S(2)}) %collective-permute-start) | collective-permute-done | bytes 835616 | tf_op jit(solution)/shard_map/ppermute | solution.py:38
  41.8 4.6 %translate.1 = (bf16[16,4,16,384]{3,2,1,0:T(8,128)(2,1)}, f32[16,8,128]{2,1,0:T(8,128)}) custom-call(s32[4]{0:T(128)S(1)} %pad_add_fusion.flags, bf16[8,136,384]{2,1,0:T(8,128)(2,1)S(1)} %all_to_all.20.own, bf16[8,136,384]{2,1,0:T(8,128)(2,1)} %collective-permute-done.other, bf16[3,384,384]{2,1,0:T(8,128)(2,1)} %matrices.1), custom_call_target="tpu_custom_call" | custom-call | tf_op jit(solution)/shard_map/translate/pallas_call | solution.py:220
  46.4 6.8 %all-to-all-start.1 = ((bf16[16,64,384]{2,1,0:T(8,128)(2,1)}), bf16[16,64,384]{2,1,0:T(8,128)(2,1)S(1)}, u32[]{:S(2)}, u32[]{:S(2)}) async-start(bf16[16,64,384]{2,1,0:T(8,128)(2,1)} %bitcast.64), calls=%async_computation.1 | async-start | bytes 1572864 | tf_op jit(solution)/shard_map/all_to_all | solution.py:34
  53.2 13.5 %all-to-all-done.1.parts = bf16[16,64,384]{2,1,0:T(8,128)(2,1)S(1)} async-done(((bf16[16,64,384]{2,1,0:T(8,128)(2,1)}), bf16[16,64,384]{2,1,0:T(8,128)(2,1)S(1)}, u32[]{:S(2)}, u32[]{:S(2)}) %all-to-all-start.1) | async-done | bytes 786464 | tf_op jit(solution)/shard_map/all_to_all | solution.py:34
  67.3 26.3 %all_to_all.21.y = bf16[32,72,384]{2,1,0:T(8,128)(2,1)} all-to-all(bf16[32,72,384]{2,1,0:T(8,128)(2,1)S(1)} %scale.1), channel_id=1, replica_groups=mesh['zq'=4,'zp'=2,'c'=2,'y'=4,'x'=4] {'zp','y','x'}, dimensions={0} | all-to-all | bytes 3538944 | tf_op jit(solution)/shard_map/all_to_all | solution.py:34
  93.6 3.4 %collective-permute-start.2 = (bf16[32,72,384]{2,1,0:T(8,128)(2,1)}, bf16[32,72,384]{2,1,0:T(8,128)(2,1)}, u32[]{:S(2)}, u32[]{:S(2)}) collective-permute-start(bf16[32,72,384]{2,1,0:T(8,128)(2,1)} %all_to_all.21.y), channel_id=1, source_target_pairs={{0,16},{16,0},{1,17},{17,1},{2,18},{18,2},{3,19},{19,3},{4,20},{20... | collective-permute-start | bytes 5308424 | tf_op jit(solution)/shard_map/ppermute | solution.py:38
  97.0 2.4 %dynamic-slice_bitcast_fusion = (bf16[512,384]{1,0:T(8,128)(2,1)}, bf16[512,384]{1,0:T(8,128)(2,1)}, bf16[512,384]{1,0:T(8,128)(2,1)}, bf16[512,384]{1,0:T(8,128)(2,1)S(1)}) fusion(bf16[4,512,384]{2,1,0:T(8,128)(2,1)} %bitcast.63, s32[]{:T(128)S(6)} %select_n.84, s32[]{:T(128)S(6)} %select_n.83, s32[]{:T(128)S(6)} %select_n.82, s32[]{:T(128)S(6)} %select_n.81), kind=kLoop, calls=%fused_computation.4 | loop fusion | bytes 3145744 | tf_op jit(solution)/shard_map/jit(dynamic_index_in_dim)/squeeze | solution.py:233
  101.3 9.1 %collective-permute-done.1.u_far = bf16[512,384]{1,0:T(8,128)(2,1)} collective-permute-done((bf16[512,384]{1,0:T(8,128)(2,1)}, bf16[512,384]{1,0:T(8,128)(2,1)}, u32[]{:S(2)}, u32[]{:S(2)}) %collective-permute-start.1) | collective-permute-done | bytes 393248 | tf_op jit(solution)/shard_map/ppermute | solution.py:235
  110.4 2.8 %own_logits.1.own_part = f32[4,264,512]{2,1,0:T(8,128)S(1)} custom-call(s32[4]{0:T(128)S(1)} %pad_add_fusion.flags, bf16[32,72,384]{2,1,0:T(8,128)(2,1)} %all_to_all.21.y, bf16[512,384]{1,0:T(8,128)(2,1)S(1)} %get-tuple-element.21.u_near, bf16[512,384]{1,0:T(8,128)(2,1)} %collective-permute-done.1.u_far), custom_call_target="tpu_custom_call" | custom-call | tf_op jit(solution)/shard_map/own_logits/pallas_call | solution.py:253
  113.2 5.7 %collective-permute-done.4.u_far = bf16[512,384]{1,0:T(8,128)(2,1)S(1)} collective-permute-done((bf16[512,384]{1,0:T(8,128)(2,1)}, bf16[512,384]{1,0:T(8,128)(2,1)S(1)}, u32[]{:S(2)}, u32[]{:S(2)}) %collective-permute-start.4) | collective-permute-done | bytes 393248 | tf_op jit(solution)/shard_map/ppermute | solution.py:235
  118.9 1.9 %shard_map.104 = f32[264,512]{1,0:T(8,128)S(1)} custom-call(s32[4]{0:T(128)S(1)} %pad_add_fusion.flags, f32[4,264,512]{2,1,0:T(8,128)S(1)} %own_logits.1.own_part, bf16[32,72,384]{2,1,0:T(8,128)(2,1)} %collective-permute-done.2.y_other, bf16[512,384]{1,0:T(8,128)(2,1)S(1)} %collective-permute-done.3.u_near, bf16[512,384]{1,0:T(8,128)(2,1)S(1)} %collective-permute-done.4.u_far), custom_call_target="tpu_custom_call" | custom-call | tf_op jit(solution)/shard_map/pallas_call | solution.py:263
  122.3 2.0 %shard_map.105 = f32[264,512]{1,0:T(8,128)S(1)} custom-call(s32[4]{0:T(128)S(1)} %pad_add_fusion.flags, f32[4,264,512]{2,1,0:T(8,128)S(1)} %own_logits.1.own_part, bf16[32,72,384]{2,1,0:T(8,128)(2,1)} %collective-permute-done.2.y_other, bf16[512,384]{1,0:T(8,128)(2,1)S(1)} %collective-permute-done.3.u_near, bf16[512,384]{1,0:T(8,128)(2,1)S(1)} %collective-permute-done.4.u_far), custom_call_target="tpu_custom_call" | custom-call | tf_op jit(solution)/shard_map/pallas_call | solution.py:263
  125.5 2.0 %shard_map.106 = f32[264,512]{1,0:T(8,128)S(1)} custom-call(s32[4]{0:T(128)S(1)} %pad_add_fusion.flags, f32[4,264,512]{2,1,0:T(8,128)S(1)} %own_logits.1.own_part, bf16[32,72,384]{2,1,0:T(8,128)(2,1)} %collective-permute-done.2.y_other, bf16[512,384]{1,0:T(8,128)(2,1)S(1)} %collective-permute-done.3.u_near, bf16[512,384]{1,0:T(8,128)(2,1)S(1)} %collective-permute-done.4.u_far), custom_call_target="tpu_custom_call" | custom-call | tf_op jit(solution)/shard_map/pallas_call | solution.py:263
  129.9 2.0 %shard_map.107 = f32[264,512]{1,0:T(8,128)S(1)} custom-call(s32[4]{0:T(128)S(1)} %pad_add_fusion.flags, f32[4,264,512]{2,1,0:T(8,128)S(1)} %own_logits.1.own_part, bf16[32,72,384]{2,1,0:T(8,128)(2,1)} %collective-permute-done.2.y_other, bf16[512,384]{1,0:T(8,128)(2,1)S(1)} %collective-permute-done.3.u_near, bf16[512,384]{1,0:T(8,128)(2,1)S(1)} %collective-permute-done.4.u_far), custom_call_target="tpu_custom_call" | custom-call | tf_op jit(solution)/shard_map/pallas_call | solution.py:263
  131.9 2.0 %collective-permute-start.7 = (f16[264,512]{1,0:T(8,128)(2,1)S(1)}, f16[264,512]{1,0:T(8,128)(2,1)S(1)}, u32[]{:S(2)}, u32[]{:S(2)}) collective-permute-start(f16[264,512]{1,0:T(8,128)(2,1)S(1)} %convert_element_type.28), channel_id=1, source_target_pairs={{0,192},{64,0},{128,64},{192,128},{1,193},{65,1},{129,65},{193,129... | collective-permute-start | bytes 811016 | tf_op jit(solution)/shard_map/ppermute | solution.py:272
  134.3 5.0 %collective-permute-done.5 = f16[264,512]{1,0:T(8,128)(2,1)} collective-permute-done((f16[264,512]{1,0:T(8,128)(2,1)S(1)}, f16[264,512]{1,0:T(8,128)(2,1)}, u32[]{:S(2)}, u32[]{:S(2)}) %collective-permute-start.5) | collective-permute-done | bytes 270368 | tf_op jit(solution)/shard_map/ppermute | solution.py:272
  139.2 6.8 %collective-permute-done.6 = f16[264,512]{1,0:T(8,128)(2,1)} collective-permute-done((f16[264,512]{1,0:T(8,128)(2,1)}, f16[264,512]{1,0:T(8,128)(2,1)}, u32[]{:S(2)}, u32[]{:S(2)}) %collective-permute-start.6) | collective-permute-done | bytes 270368 | tf_op jit(solution)/shard_map/ppermute | solution.py:272
  146.0 5.8 %collective-permute-done.7 = f16[264,512]{1,0:T(8,128)(2,1)S(1)} collective-permute-done((f16[264,512]{1,0:T(8,128)(2,1)S(1)}, f16[264,512]{1,0:T(8,128)(2,1)S(1)}, u32[]{:S(2)}, u32[]{:S(2)}) %collective-permute-start.7) | collective-permute-done | bytes 270368 | tf_op jit(solution)/shard_map/ppermute | solution.py:272
  154.4 6.0 %all-to-all-start.3 = ((f32[64,8,128]{2,1,0:T(8,128)}), f32[64,8,128]{2,1,0:T(8,128)S(1)}, u32[]{:S(2)}, u32[]{:S(2)}) async-start(f32[64,8,128]{2,1,0:T(8,128)} %stats.1), calls=%async_computation.3 | async-start | bytes 524288 | tf_op jit(solution)/shard_map/all_to_all | solution.py:34
  161.8 7.8 %all-to-all-done.3 = f32[64,8,128]{2,1,0:T(8,128)S(1)} async-done(((f32[64,8,128]{2,1,0:T(8,128)}), f32[64,8,128]{2,1,0:T(8,128)S(1)}, u32[]{:S(2)}, u32[]{:S(2)}) %all-to-all-start.3) | async-done | bytes 262176 | tf_op jit(solution)/shard_map/all_to_all | solution.py:34
  171.3 2.6 %collective-permute-start.9 = (f32[8,128]{1,0:T(8,128)S(1)}, f32[8,128]{1,0:T(8,128)S(1)}, u32[]{:S(2)}, u32[]{:S(2)}) collective-permute-start(f32[8,128]{1,0:T(8,128)S(1)} %reduce_sum.48), channel_id=1, source_target_pairs={{0,128},{64,192},{128,0},{192,64},{1,129},{65,193},{129,1},{193,65... | collective-permute-start | bytes 12296 | tf_op jit(solution)/shard_map/ppermute | solution.py:303
  173.9 2.1 %collective-permute-start.10 = (f32[8,128]{1,0:T(8,128)S(1)}, f32[8,128]{1,0:T(8,128)S(1)}, u32[]{:S(2)}, u32[]{:S(2)}) collective-permute-start(f32[8,128]{1,0:T(8,128)S(1)} %reduce_sum.48), channel_id=1, source_target_pairs={{0,192},{64,0},{128,64},{192,128},{1,193},{65,1},{129,65},{193,129... | collective-permute-start | bytes 12296 | tf_op jit(solution)/shard_map/ppermute | solution.py:303
  (70 shorter events, 21.6 us)
Async XLA Ops:
  0.6 2.3 %copy-start = (bf16[3,1024,384]{2,1,0:T(8,128)(2,1)S(1)}, bf16[3,1024,384]{2,1,0:T(8,128)(2,1)}, u32[]{:S(2)}) copy-start(bf16[3,1024,384]{2,1,0:T(8,128)(2,1)} %param.9) | copy-start | bytes 7077892
  37.3 4.5 %collective-permute-start = (bf16[8,136,384]{2,1,0:T(8,128)(2,1)S(1)}, bf16[8,136,384]{2,1,0:T(8,128)(2,1)}, u32[]{:S(2)}, u32[]{:S(2)}) collective-permute-start(bf16[8,136,384]{2,1,0:T(8,128)(2,1)S(1)} %all_to_all.20.own), channel_id=1, source_target_pairs={{0,16},{16,0},{1,17},{17,1},{2,18},{18,2},{3,19},{19,3},{4,20},{20... | collective-permute-start | bytes 2506760 | tf_op jit(solution)/shard_map/ppermute | solution.py:38
  39.8 13.4 %copy-start.4 = (f32[384]{0:T(512)S(1)}, f32[384]{0:T(512)}, u32[]{:S(2)}) copy-start(f32[384]{0:T(512)} %param.13) | copy-start | bytes 4612
  39.8 13.4 %copy-start.3 = (f32[3,384]{1,0:T(4,128)S(1)}, f32[3,384]{1,0:T(4,128)}, u32[]{:S(2)}) copy-start(f32[3,384]{1,0:T(4,128)} %param.12) | copy-start | bytes 13828
  46.4 20.3 %all-to-all-start.1 = ((bf16[16,64,384]{2,1,0:T(8,128)(2,1)}), bf16[16,64,384]{2,1,0:T(8,128)(2,1)S(1)}, u32[]{:S(2)}, u32[]{:S(2)}) async-start(bf16[16,64,384]{2,1,0:T(8,128)(2,1)} %bitcast.64), calls=%async_computation.1 | async-start | bytes 1572864 | tf_op jit(solution)/shard_map/all_to_all | solution.py:34
  93.6 25.3 %collective-permute-start.2 = (bf16[32,72,384]{2,1,0:T(8,128)(2,1)}, bf16[32,72,384]{2,1,0:T(8,128)(2,1)}, u32[]{:S(2)}, u32[]{:S(2)}) collective-permute-start(bf16[32,72,384]{2,1,0:T(8,128)(2,1)} %all_to_all.21.y), channel_id=1, source_target_pairs={{0,16},{16,0},{1,17},{17,1},{2,18},{18,2},{3,19},{19,3},{4,20},{20... | collective-permute-start | bytes 5308424 | tf_op jit(solution)/shard_map/ppermute | solution.py:38
  99.4 11.0 %collective-permute-start.1 = (bf16[512,384]{1,0:T(8,128)(2,1)}, bf16[512,384]{1,0:T(8,128)(2,1)}, u32[]{:S(2)}, u32[]{:S(2)}) collective-permute-start(bf16[512,384]{1,0:T(8,128)(2,1)} %get-tuple-element.20), channel_id=1, source_target_pairs={{0,32},{16,48},{32,0},{48,16},{1,33},{17,49},{33,1},{49,17},{2,34}... | collective-permute-start | bytes 1179656 | tf_op jit(solution)/shard_map/ppermute | solution.py:235
  99.9 13.4 %collective-permute-start.3 = (bf16[512,384]{1,0:T(8,128)(2,1)}, bf16[512,384]{1,0:T(8,128)(2,1)S(1)}, u32[]{:S(2)}, u32[]{:S(2)}) collective-permute-start(bf16[512,384]{1,0:T(8,128)(2,1)} %get-tuple-element.19), channel_id=1, source_target_pairs={{0,16},{16,0},{32,48},{48,32},{1,17},{17,1},{33,49},{49,33},{2,18}... | collective-permute-start | bytes 1179656 | tf_op jit(solution)/shard_map/ppermute | solution.py:235
  100.1 18.7 %collective-permute-start.4 = (bf16[512,384]{1,0:T(8,128)(2,1)}, bf16[512,384]{1,0:T(8,128)(2,1)S(1)}, u32[]{:S(2)}, u32[]{:S(2)}) collective-permute-start(bf16[512,384]{1,0:T(8,128)(2,1)} %get-tuple-element.18), channel_id=1, source_target_pairs={{0,48},{16,32},{32,16},{48,0},{1,49},{17,33},{33,17},{49,1},{2,50}... | collective-permute-start | bytes 1179656 | tf_op jit(solution)/shard_map/ppermute | solution.py:235
  113.2 8.5 %copy-start.2 = (f32[16,8,128]{2,1,0:T(8,128)S(1)}, f32[16,8,128]{2,1,0:T(8,128)}, u32[]{:S(2)}) copy-start(f32[16,8,128]{2,1,0:T(8,128)} %get-tuple-element.8) | copy-start | bytes 196612
  120.8 0.8 copy-start.1
  124.3 15.0 %collective-permute-start.5 = (f16[264,512]{1,0:T(8,128)(2,1)S(1)}, f16[264,512]{1,0:T(8,128)(2,1)}, u32[]{:S(2)}, u32[]{:S(2)}) collective-permute-start(f16[264,512]{1,0:T(8,128)(2,1)S(1)} %convert_element_type.24), channel_id=1, source_target_pairs={{0,128},{64,192},{128,0},{192,64},{1,129},{65,193},{129,1},{193,65... | collective-permute-start | bytes 811016 | tf_op jit(solution)/shard_map/ppermute | solution.py:272
  128.2 17.9 %collective-permute-start.6 = (f16[264,512]{1,0:T(8,128)(2,1)}, f16[264,512]{1,0:T(8,128)(2,1)}, u32[]{:S(2)}, u32[]{:S(2)}) collective-permute-start(f16[264,512]{1,0:T(8,128)(2,1)} %convert_element_type.26), channel_id=1, source_target_pairs={{0,64},{64,128},{128,192},{192,0},{1,65},{65,129},{129,193},{193,1... | collective-permute-start | bytes 811016 | tf_op jit(solution)/shard_map/ppermute | solution.py:272
  131.9 19.9 %collective-permute-start.7 = (f16[264,512]{1,0:T(8,128)(2,1)S(1)}, f16[264,512]{1,0:T(8,128)(2,1)S(1)}, u32[]{:S(2)}, u32[]{:S(2)}) collective-permute-start(f16[264,512]{1,0:T(8,128)(2,1)S(1)} %convert_element_type.28), channel_id=1, source_target_pairs={{0,192},{64,0},{128,64},{192,128},{1,193},{65,1},{129,65},{193,129... | collective-permute-start | bytes 811016 | tf_op jit(solution)/shard_map/ppermute | solution.py:272
  154.4 15.2 %all-to-all-start.3 = ((f32[64,8,128]{2,1,0:T(8,128)}), f32[64,8,128]{2,1,0:T(8,128)S(1)}, u32[]{:S(2)}, u32[]{:S(2)}) async-start(f32[64,8,128]{2,1,0:T(8,128)} %stats.1), calls=%async_computation.3 | async-start | bytes 524288 | tf_op jit(solution)/shard_map/all_to_all | solution.py:34
  169.6 6.4 %collective-permute-start.8 = (f32[8,128]{1,0:T(8,128)S(1)}, f32[8,128]{1,0:T(8,128)S(1)}, u32[]{:S(2)}, u32[]{:S(2)}) collective-permute-start(f32[8,128]{1,0:T(8,128)S(1)} %reduce_sum.48), channel_id=1, source_target_pairs={{0,64},{64,128},{128,192},{192,0},{1,65},{65,129},{129,193},{193,1... | collective-permute-start | bytes 12296 | tf_op jit(solution)/shard_map/ppermute | solution.py:303
  171.3 6.4 %collective-permute-start.9 = (f32[8,128]{1,0:T(8,128)S(1)}, f32[8,128]{1,0:T(8,128)S(1)}, u32[]{:S(2)}, u32[]{:S(2)}) collective-permute-start(f32[8,128]{1,0:T(8,128)S(1)} %reduce_sum.48), channel_id=1, source_target_pairs={{0,128},{64,192},{128,0},{192,64},{1,129},{65,193},{129,1},{193,65... | collective-permute-start | bytes 12296 | tf_op jit(solution)/shard_map/ppermute | solution.py:303
  173.9 3.8 %collective-permute-start.10 = (f32[8,128]{1,0:T(8,128)S(1)}, f32[8,128]{1,0:T(8,128)S(1)}, u32[]{:S(2)}, u32[]{:S(2)}) collective-permute-start(f32[8,128]{1,0:T(8,128)S(1)} %reduce_sum.48), channel_id=1, source_target_pairs={{0,192},{64,0},{128,64},{192,128},{1,193},{65,1},{129,65},{193,129... | collective-permute-start | bytes 12296 | tf_op jit(solution)/shard_map/ppermute | solution.py:303

commit v5 on v4

--- a/solution.py
+++ b/solution.py
@@ -21,6 +21,7 @@
 NT = (((1,), (1,)), ((), ()))
 TN = (((0,), (0,)), ((), ()))
 INFO = 128
+OFFSETS = (0, -2, 2, -1, 1, -3, 3, -4)
 SHIFT = 16.0
 SCALE = 262144.0
 LARGE = 16.0
@@ -34,6 +35,10 @@
     return lax.all_to_all(value, axes, split_axis=0, concat_axis=0, tiled=True)
 
 
+def shifted(value, by):
+    return lax.ppermute(value, Z, [(j, (j + by) % 8) for j in range(8)])
+
+
 def swap_cores(value):
     return lax.ppermute(value, "c", [(0, 1), (1, 0)])
 
@@ -55,36 +60,38 @@
 LIMIT = pltpu.CompilerParams(vmem_limit_bytes=24 * 1024 * 1024)
 
 
-def translate_kernel(flags, own, other, matrices, out, info, translator, arrived):
-    fetch = pltpu.make_async_copy(matrices, translator, arrived)
-    fetch.start()
+def translate_kernel(flags, *refs):
+    own, other = refs[:8], refs[8:16]
+    translator, out, info = refs[16:]
     low_core = flags[0] == 0
     keep = flags[1].astype(F32)
+    chips = [lax.rem(flags[4] + offset + 8, 8) for offset in OFFSETS]
     lane = lax.broadcasted_iota(jnp.int32, (CAP, ROWS), 1).astype(F32)
     slot = lax.broadcasted_iota(jnp.int32, (CAP, ROWS), 0).astype(F32)
-    base = jnp.zeros((1, 1), F32)
+    counts_own = [ref[INFO + 2 : INFO + 3, 0:1].astype(F32) for ref in own]
+    counts_other = [ref[INFO + 2 : INFO + 3, 0:1].astype(F32) for ref in other]
     pick_own, pick_other = [], []
     for k in range(8):
-        count_own = own[k, INFO + 2 : INFO + 3, 0:1].astype(F32)
-        count_other = other[k, INFO + 2 : INFO + 3, 0:1].astype(F32)
-        start_own = base + jnp.where(low_core, 0.0, count_other)
-        start_other = base + jnp.where(low_core, count_own, 0.0)
-        hit_own = (lane == start_own + slot) & (slot < count_own)
-        hit_other = (lane == start_other + slot) & (slot < count_other)
+        base = jnp.zeros((1, 1), F32)
+        for j in range(8):
+            if j != k:
+                base = base + jnp.where(chips[j] < chips[k], counts_own[j] + counts_other[j], 0.0)
+        start_own = base + jnp.where(low_core, 0.0, counts_other[k])
+        start_other = base + jnp.where(low_core, counts_own[k], 0.0)
+        hit_own = (lane == start_own + slot) & (slot < counts_own[k])
+        hit_other = (lane == start_other + slot) & (slot < counts_other[k])
         pick_own.append(jnp.where(hit_own, 1.0, 0.0).astype(BF16))
         pick_other.append(jnp.where(hit_other, 1.0, 0.0).astype(BF16))
-        base = base + count_own + count_other
-        a = own[k, INFO : INFO + 8, 0:128].astype(F32)
-        b = other[k, INFO : INFO + 8, 0:128].astype(F32)
-        info[2 * k] = jnp.where(low_core, a, b)
-        info[2 * k + 1] = jnp.where(low_core, b, a)
+        a = own[k][INFO : INFO + 8, 0:128].astype(F32)
+        b = other[k][INFO : INFO + 8, 0:128].astype(F32)
+        info[2 * chips[k]] = jnp.where(low_core, a, b)
+        info[2 * chips[k] + 1] = jnp.where(low_core, b, a)
     pick_own = jnp.concatenate(pick_own, axis=0)
     pick_other = jnp.concatenate(pick_other, axis=0)
-    fetch.wait()
     for layer in range(LAYERS + 1):
         low = layer * CAP
-        a = own[:, low : low + CAP, :].reshape(ROWS, -1)
-        b = other[:, low : low + CAP, :].reshape(ROWS, -1)
+        a = jnp.concatenate([ref[low : low + CAP, :] for ref in own], axis=0)
+        b = jnp.concatenate([ref[low : low + CAP, :] for ref in other], axis=0)
         rows = lax.dot_general(pick_own, a, TN, preferred_element_type=F32)
         rows = rows + lax.dot_general(pick_other, b, TN, preferred_element_type=F32)
         part = rows * keep
@@ -213,19 +220,22 @@
         ],
         axis=0,
     )
-    own = exchange(jnp.broadcast_to(local[None], (8, *local.shape)), Z)
-    other = swap_cores(own)
-
-    flags = jnp.stack([c, (seq == v).astype(jnp.int32), quarter // 2, zq])
+    back2, fore2, back1, fore1 = [shifted(local, by) for by in (2, -2, 1, -1)]
+    own = [local, back2, fore2, back1, fore1]
+    other = [swap_cores(chunk) for chunk in own]
+    third = [shifted(back2, 1), shifted(fore2, -1), shifted(back2, 2)]
+    own += third
+    other += [swap_cores(chunk) for chunk in third]
+
+    flags = jnp.stack([c, (seq == v).astype(jnp.int32), quarter // 2, zq, seq // 2])
     parts, every_info = pl.pallas_call(
         translate_kernel,
         out_shape=(far((16, 4, 16, width), BF16), far((16, 8, 128), F32)),
-        in_specs=[SCALARS, VECTORS, VECTORS, pl.BlockSpec(memory_space=pltpu.HBM)],
+        in_specs=[SCALARS] + [VECTORS] * 17,
         out_specs=(VECTORS, VECTORS),
-        scratch_shapes=[pltpu.VMEM(translator.shape, BF16), pltpu.SemaphoreType.DMA(())],
         compiler_params=LIMIT,
         name="translate",
-    )(flags, near(own), near(other), pltpu.with_memory_space_constraint(translator, pltpu.HBM))
+    )(flags, *[near(chunk) for chunk in own + other], near(translator))
     arrived = exchange(parts.reshape(16, 64, width), VOCAB)
     fours = unembed.reshape(4, part, width)
     quarters = []

time: 181 us -> 176 us (0.972)
  blocking collectives: 57.8 us -> 26.3 us
  starting transfers between devices: 31.6 us -> 55.8 us
  local copies, waits for them, and re-layouts: 7.75 us -> 13.9 us
    all_to_all x2 -> x1, blocking collectives: 57.8 us -> 26.3 us  [exchange(): return lax.all_to_all(value, axes, split_axis=0, concat_axis=0, tiled=True)]
    ppermute x0 -> x7, starting transfers between devices: none -> 13.4 us  [shifted(): return lax.ppermute(value, Z, [(j, (j + by) % 8) for j in range(8)])]
    unnamed x11 -> x29, local copies, waits for them, and re-layouts: 1.42 us -> 7.53 us
    ppermute x2 -> x9, starting transfers between devices: 5.82 us -> 11.8 us  [swap_cores(): return lax.ppermute(value, 'c', [(0, 1), (1, 0)])]
    ppermute x3, starting transfers between devices: 4.83 us -> 9.27 us  [body(): chunk = lax.ppermute(chunk, 'zq', [(j, (j + k) % 4) for j in range(4)])]
    ppermute x3, waiting for transfers between devices: 17.5 us -> 14.2 us  [body(): chunk = lax.ppermute(chunk, 'zq', [(j, (j + k) % 4) for j in range(4)])]
  transfers between devices with their start and end apart: 13 -> 27, of which waited for: 9 -> 12; matrix products, arithmetic and copies ran while one was open for 3% -> 3% of each run, Pallas kernels for 4% -> 4%
where the time goes in v5:
time: 176 us
  starting transfers between devices  55.8 us (32%)
  waiting for transfers between devices  55.5 us (32%)
  blocking collectives  26.3 us (15%)
  Pallas kernels  16 us (9%)
  local copies, waits for them, and re-layouts  13.9 us (8%)
  other arithmetic  6.48 us (4%)
    all_to_all x1, blocking collectives, exchange(): return lax.all_to_all(value, axes, split_axis=0, concat_axis=0, tiled=True)  26.3 us
    all_to_all x2, waiting for transfers between devices, exchange(): return lax.all_to_all(value, axes, split_axis=0, concat_axis=0, tiled=True)  21.3 us
    ppermute x3, waiting for transfers between devices, body(): block = lax.ppermute(block, ('zp', 'c'), [(j, j ^ k) for j in range(4)])  14.8 us
    ppermute x3, waiting for transfers between devices, body(): chunk = lax.ppermute(chunk, 'zq', [(j, (j + k) % 4) for j in range(4)])  14.2 us
    all_to_all x2, starting transfers between devices, exchange(): return lax.all_to_all(value, axes, split_axis=0, concat_axis=0, tiled=True)  14 us
    ppermute x7, starting transfers between devices, shifted(): return lax.ppermute(value, Z, [(j, (j + by) % 8) for j in range(8)])  13.4 us
    ppermute x9, starting transfers between devices, swap_cores(): return lax.ppermute(value, 'c', [(0, 1), (1, 0)])  11.8 us
    ppermute x3, starting transfers between devices, body(): chunk = lax.ppermute(chunk, 'zq', [(j, (j + k) % 4) for j in range(4)])  9.27 us
  transfers between devices with their start and end apart: 27, of which 12 were waited for; matrix products, arithmetic and copies ran while one was open for 3% of the time, Pallas kernels for 4%

profile of v5, /device:TPU:1, one launch (start us, length us, event | category | flops | bytes accessed | tf_op | source)
XLA Modules:
  0.0 175.7 jit_solution(9715631018645058045)
XLA Ops:
  5.9 3.9 %collective-permute-start = (bf16[136,384]{1,0:T(8,128)(2,1)S(1)}, bf16[136,384]{1,0:T(8,128)(2,1)S(1)}, u32[]{:S(2)}, u32[]{:S(2)}) collective-permute-start(bf16[136,384]{1,0:T(8,128)(2,1)S(1)} %fusion.1.refs_0_), channel_id=1, source_target_pairs={{0,64},{32,96},{64,128},{96,160},{128,192},{160,224},{192,0},{224,... | collective-permute-start | bytes 313352 | tf_op jit(solution)/shard_map/ppermute | solution.py:39
  9.8 3.1 %collective-permute-start.1 = (bf16[136,384]{1,0:T(8,128)(2,1)S(1)}, bf16[136,384]{1,0:T(8,128)(2,1)S(1)}, u32[]{:S(2)}, u32[]{:S(2)}) collective-permute-start(bf16[136,384]{1,0:T(8,128)(2,1)S(1)} %fusion.1.refs_0_), channel_id=1, source_target_pairs={{0,192},{32,224},{64,0},{96,32},{128,64},{160,96},{192,128},{224,1... | collective-permute-start | bytes 313352 | tf_op jit(solution)/shard_map/ppermute | solution.py:39
  19.3 2.1 %collective-permute-start.6 = (bf16[136,384]{1,0:T(8,128)(2,1)S(1)}, bf16[136,384]{1,0:T(8,128)(2,1)}, u32[]{:S(2)}, u32[]{:S(2)}) collective-permute-start(bf16[136,384]{1,0:T(8,128)(2,1)S(1)} %collective-permute-done.refs_1_), channel_id=1, source_target_pairs={{0,64},{32,96},{64,128},{96,160},{128,192},{160,224},{192,0},{224,... | collective-permute-start | bytes 313352 | tf_op jit(solution)/shard_map/ppermute | solution.py:39
  21.4 3.5 %collective-permute-start.8 = (bf16[136,384]{1,0:T(8,128)(2,1)S(1)}, bf16[136,384]{1,0:T(8,128)(2,1)S(1)}, u32[]{:S(2)}, u32[]{:S(2)}) collective-permute-start(bf16[136,384]{1,0:T(8,128)(2,1)S(1)} %collective-permute-done.refs_1_), channel_id=1, source_target_pairs={{0,16},{16,0},{1,17},{17,1},{2,18},{18,2},{3,19},{19,3},{4,20},{20... | collective-permute-start | bytes 313352 | tf_op jit(solution)/shard_map/ppermute | solution.py:43
  36.2 3.6 %translate.1 = (bf16[16,4,16,384]{3,2,1,0:T(8,128)(2,1)}, f32[16,8,128]{2,1,0:T(8,128)}) custom-call(s32[5]{0:T(128)S(1)} %stack.42.flags, bf16[136,384]{1,0:T(8,128)(2,1)S(1)} %fusion.1.refs_0_, bf16[136,384]{1,0:T(8,128)(2,1)S(1)} %collective-permute-done.refs_1_, bf16[136,384]{1,0:T(8,128)(2,1)S(1)} %copy-done.4, ...), custom_call_target="tpu_custom_call" | custom-call | tf_op jit(solution)/shard_map/translate/pallas_call | solution.py:231
  39.9 6.8 %all-to-all-start = ((bf16[16,64,384]{2,1,0:T(8,128)(2,1)}), bf16[16,64,384]{2,1,0:T(8,128)(2,1)S(1)}, u32[]{:S(2)}, u32[]{:S(2)}) async-start(bf16[16,64,384]{2,1,0:T(8,128)(2,1)} %bitcast.65), calls=%async_computation | async-start | bytes 1572864 | tf_op jit(solution)/shard_map/all_to_all | solution.py:35
  46.7 13.5 %all-to-all-done.parts = bf16[16,64,384]{2,1,0:T(8,128)(2,1)S(1)} async-done(((bf16[16,64,384]{2,1,0:T(8,128)(2,1)}), bf16[16,64,384]{2,1,0:T(8,128)(2,1)S(1)}, u32[]{:S(2)}, u32[]{:S(2)}) %all-to-all-start) | async-done | bytes 786464 | tf_op jit(solution)/shard_map/all_to_all | solution.py:35
  60.8 26.3 %all_to_all.15.y = bf16[32,72,384]{2,1,0:T(8,128)(2,1)} all-to-all(bf16[32,72,384]{2,1,0:T(8,128)(2,1)S(1)} %scale.1), channel_id=1, replica_groups=mesh['zq'=4,'zp'=2,'c'=2,'y'=4,'x'=4] {'zp','y','x'}, dimensions={0} | all-to-all | bytes 3538944 | tf_op jit(solution)/shard_map/all_to_all | solution.py:35
  87.1 3.4 %collective-permute-start.16 = (bf16[32,72,384]{2,1,0:T(8,128)(2,1)}, bf16[32,72,384]{2,1,0:T(8,128)(2,1)}, u32[]{:S(2)}, u32[]{:S(2)}) collective-permute-start(bf16[32,72,384]{2,1,0:T(8,128)(2,1)} %all_to_all.15.y), channel_id=1, source_target_pairs={{0,16},{16,0},{1,17},{17,1},{2,18},{18,2},{3,19},{19,3},{4,20},{20... | collective-permute-start | bytes 5308424 | tf_op jit(solution)/shard_map/ppermute | solution.py:43
  90.5 2.4 %dynamic-slice_bitcast_fusion = (bf16[512,384]{1,0:T(8,128)(2,1)}, bf16[512,384]{1,0:T(8,128)(2,1)}, bf16[512,384]{1,0:T(8,128)(2,1)}, bf16[512,384]{1,0:T(8,128)(2,1)S(1)}) fusion(bf16[4,512,384]{2,1,0:T(8,128)(2,1)} %bitcast.64, s32[]{:T(128)S(6)} %select_n.88, s32[]{:T(128)S(6)} %select_n.87, s32[]{:T(128)S(6)} %select_n.86, s32[]{:T(128)S(6)} %select_n.85), kind=kLoop, calls=%fused_computation.4 | loop fusion | bytes 3145744 | tf_op jit(solution)/shard_map/jit(dynamic_index_in_dim)/squeeze | solution.py:243
  94.8 9.1 %collective-permute-done.15.u_far = bf16[512,384]{1,0:T(8,128)(2,1)} collective-permute-done((bf16[512,384]{1,0:T(8,128)(2,1)}, bf16[512,384]{1,0:T(8,128)(2,1)}, u32[]{:S(2)}, u32[]{:S(2)}) %collective-permute-start.15) | collective-permute-done | bytes 393248 | tf_op jit(solution)/shard_map/ppermute | solution.py:245
  103.9 2.8 %own_logits.1.own_part = f32[4,264,512]{2,1,0:T(8,128)S(1)} custom-call(s32[5]{0:T(128)S(1)} %stack.42.flags, bf16[32,72,384]{2,1,0:T(8,128)(2,1)} %all_to_all.15.y, bf16[512,384]{1,0:T(8,128)(2,1)S(1)} %get-tuple-element.21.u_near, bf16[512,384]{1,0:T(8,128)(2,1)} %collective-permute-done.15.u_far), custom_call_target="tpu_custom_call" | custom-call | tf_op jit(solution)/shard_map/own_logits/pallas_call | solution.py:263
  106.7 5.7 %collective-permute-done.18.u_far = bf16[512,384]{1,0:T(8,128)(2,1)S(1)} collective-permute-done((bf16[512,384]{1,0:T(8,128)(2,1)}, bf16[512,384]{1,0:T(8,128)(2,1)S(1)}, u32[]{:S(2)}, u32[]{:S(2)}) %collective-permute-start.18) | collective-permute-done | bytes 393248 | tf_op jit(solution)/shard_map/ppermute | solution.py:245
  115.8 2.0 %shard_map.105 = f32[264,512]{1,0:T(8,128)S(1)} custom-call(s32[5]{0:T(128)S(1)} %stack.42.flags, f32[4,264,512]{2,1,0:T(8,128)S(1)} %own_logits.1.own_part, bf16[32,72,384]{2,1,0:T(8,128)(2,1)} %collective-permute-done.16.y_other, bf16[512,384]{1,0:T(8,128)(2,1)S(1)} %collective-permute-done.17.u_near, bf16[512,384]{1,0:T(8,128)(2,1)S(1)} %collective-permute-done.18.u_far), custom_call_target="tpu_custom_call" | custom-call | tf_op jit(solution)/shard_map/pallas_call | solution.py:273
  117.8 5.6 %collective-permute-start.19 = (f16[264,512]{1,0:T(8,128)(2,1)S(1)}, f16[264,512]{1,0:T(8,128)(2,1)}, u32[]{:S(2)}, u32[]{:S(2)}) collective-permute-start(f16[264,512]{1,0:T(8,128)(2,1)S(1)} %convert_element_type.24), channel_id=1, source_target_pairs={{0,128},{64,192},{128,0},{192,64},{1,129},{65,193},{129,1},{193,65... | collective-permute-start | bytes 811016 | tf_op jit(solution)/shard_map/ppermute | solution.py:282
  128.1 3.6 %collective-permute-start.21 = (f16[264,512]{1,0:T(8,128)(2,1)S(1)}, f16[264,512]{1,0:T(8,128)(2,1)S(1)}, u32[]{:S(2)}, u32[]{:S(2)}) collective-permute-start(f16[264,512]{1,0:T(8,128)(2,1)S(1)} %convert_element_type.28), channel_id=1, source_target_pairs={{0,192},{64,0},{128,64},{192,128},{1,193},{65,1},{129,65},{193,129... | collective-permute-start | bytes 811016 | tf_op jit(solution)/shard_map/ppermute | solution.py:282
  132.2 3.8 %collective-permute-done.19 = f16[264,512]{1,0:T(8,128)(2,1)} collective-permute-done((f16[264,512]{1,0:T(8,128)(2,1)S(1)}, f16[264,512]{1,0:T(8,128)(2,1)}, u32[]{:S(2)}, u32[]{:S(2)}) %collective-permute-start.19) | collective-permute-done | bytes 270368 | tf_op jit(solution)/shard_map/ppermute | solution.py:282
  135.9 6.3 %collective-permute-done.20 = f16[264,512]{1,0:T(8,128)(2,1)} collective-permute-done((f16[264,512]{1,0:T(8,128)(2,1)}, f16[264,512]{1,0:T(8,128)(2,1)}, u32[]{:S(2)}, u32[]{:S(2)}) %collective-permute-start.20) | collective-permute-done | bytes 270368 | tf_op jit(solution)/shard_map/ppermute | solution.py:282
  142.2 4.2 %collective-permute-done.21 = f16[264,512]{1,0:T(8,128)(2,1)S(1)} collective-permute-done((f16[264,512]{1,0:T(8,128)(2,1)S(1)}, f16[264,512]{1,0:T(8,128)(2,1)S(1)}, u32[]{:S(2)}, u32[]{:S(2)}) %collective-permute-start.21) | collective-permute-done | bytes 270368 | tf_op jit(solution)/shard_map/ppermute | solution.py:282
  148.9 7.2 %all-to-all-start.2 = ((f32[64,8,128]{2,1,0:T(8,128)}), f32[64,8,128]{2,1,0:T(8,128)S(1)}, u32[]{:S(2)}, u32[]{:S(2)}) async-start(f32[64,8,128]{2,1,0:T(8,128)} %stats.1), calls=%async_computation.2 | async-start | bytes 524288 | tf_op jit(solution)/shard_map/all_to_all | solution.py:35
  157.6 7.8 %all-to-all-done.2 = f32[64,8,128]{2,1,0:T(8,128)S(1)} async-done(((f32[64,8,128]{2,1,0:T(8,128)}), f32[64,8,128]{2,1,0:T(8,128)S(1)}, u32[]{:S(2)}, u32[]{:S(2)}) %all-to-all-start.2) | async-done | bytes 262176 | tf_op jit(solution)/shard_map/all_to_all | solution.py:35
  165.4 2.2 %collective-permute-start.22 = (f32[8,128]{1,0:T(8,128)S(1)}, f32[8,128]{1,0:T(8,128)S(1)}, u32[]{:S(2)}, u32[]{:S(2)}) collective-permute-start(f32[8,128]{1,0:T(8,128)S(1)} %reduce_sum.48), channel_id=1, source_target_pairs={{0,64},{64,128},{128,192},{192,0},{1,65},{65,129},{129,193},{193,1... | collective-permute-start | bytes 12296 | tf_op jit(solution)/shard_map/ppermute | solution.py:313
  168.4 2.5 %collective-permute-start.24 = (f32[8,128]{1,0:T(8,128)S(1)}, f32[8,128]{1,0:T(8,128)S(1)}, u32[]{:S(2)}, u32[]{:S(2)}) collective-permute-start(f32[8,128]{1,0:T(8,128)S(1)} %reduce_sum.48), channel_id=1, source_target_pairs={{0,192},{64,0},{128,64},{192,128},{1,193},{65,1},{129,65},{193,129... | collective-permute-start | bytes 12296 | tf_op jit(solution)/shard_map/ppermute | solution.py:313
  171.0 2.9 %collective-permute-done.23 = f32[8,128]{1,0:T(8,128)S(1)} collective-permute-done((f32[8,128]{1,0:T(8,128)S(1)}, f32[8,128]{1,0:T(8,128)S(1)}, u32[]{:S(2)}, u32[]{:S(2)}) %collective-permute-start.23) | collective-permute-done | bytes 4128 | tf_op jit(solution)/shard_map/ppermute | solution.py:313
  (114 shorter events, 39.8 us)
Async XLA Ops:
  5.9 11.2 %collective-permute-start = (bf16[136,384]{1,0:T(8,128)(2,1)S(1)}, bf16[136,384]{1,0:T(8,128)(2,1)S(1)}, u32[]{:S(2)}, u32[]{:S(2)}) collective-permute-start(bf16[136,384]{1,0:T(8,128)(2,1)S(1)} %fusion.1.refs_0_), channel_id=1, source_target_pairs={{0,64},{32,96},{64,128},{96,160},{128,192},{160,224},{192,0},{224,... | collective-permute-start | bytes 313352 | tf_op jit(solution)/shard_map/ppermute | solution.py:39
  9.8 9.5 %collective-permute-start.1 = (bf16[136,384]{1,0:T(8,128)(2,1)S(1)}, bf16[136,384]{1,0:T(8,128)(2,1)S(1)}, u32[]{:S(2)}, u32[]{:S(2)}) collective-permute-start(bf16[136,384]{1,0:T(8,128)(2,1)S(1)} %fusion.1.refs_0_), channel_id=1, source_target_pairs={{0,192},{32,224},{64,0},{96,32},{128,64},{160,96},{192,128},{224,1... | collective-permute-start | bytes 313352 | tf_op jit(solution)/shard_map/ppermute | solution.py:39
  12.9 8.5 %collective-permute-start.2 = (bf16[136,384]{1,0:T(8,128)(2,1)S(1)}, bf16[136,384]{1,0:T(8,128)(2,1)}, u32[]{:S(2)}, u32[]{:S(2)}) collective-permute-start(bf16[136,384]{1,0:T(8,128)(2,1)S(1)} %fusion.1.refs_0_), channel_id=1, source_target_pairs={{0,32},{32,64},{64,96},{96,128},{128,160},{160,192},{192,224},{224... | collective-permute-start | bytes 313352 | tf_op jit(solution)/shard_map/ppermute | solution.py:39
  13.6 7.8 %collective-permute-start.3 = (bf16[136,384]{1,0:T(8,128)(2,1)S(1)}, bf16[136,384]{1,0:T(8,128)(2,1)}, u32[]{:S(2)}, u32[]{:S(2)}) collective-permute-start(bf16[136,384]{1,0:T(8,128)(2,1)S(1)} %fusion.1.refs_0_), channel_id=1, source_target_pairs={{0,224},{32,0},{64,32},{96,64},{128,96},{160,128},{192,160},{224,1... | collective-permute-start | bytes 313352 | tf_op jit(solution)/shard_map/ppermute | solution.py:39
  15.6 9.3 %collective-permute-start.7 = (bf16[136,384]{1,0:T(8,128)(2,1)S(1)}, bf16[136,384]{1,0:T(8,128)(2,1)S(1)}, u32[]{:S(2)}, u32[]{:S(2)}) collective-permute-start(bf16[136,384]{1,0:T(8,128)(2,1)S(1)} %fusion.1.refs_0_), channel_id=1, source_target_pairs={{0,16},{16,0},{1,17},{17,1},{2,18},{18,2},{3,19},{19,3},{4,20},{20... | collective-permute-start | bytes 313352 | tf_op jit(solution)/shard_map/ppermute | solution.py:43
  17.1 9.1 %collective-permute-start.4 = (bf16[136,384]{1,0:T(8,128)(2,1)S(1)}, bf16[136,384]{1,0:T(8,128)(2,1)}, u32[]{:S(2)}, u32[]{:S(2)}) collective-permute-start(bf16[136,384]{1,0:T(8,128)(2,1)S(1)} %collective-permute-done.refs_1_), channel_id=1, source_target_pairs={{0,32},{32,64},{64,96},{96,128},{128,160},{160,192},{192,224},{224... | collective-permute-start | bytes 313352 | tf_op jit(solution)/shard_map/ppermute | solution.py:39
  19.3 7.9 %collective-permute-start.6 = (bf16[136,384]{1,0:T(8,128)(2,1)S(1)}, bf16[136,384]{1,0:T(8,128)(2,1)}, u32[]{:S(2)}, u32[]{:S(2)}) collective-permute-start(bf16[136,384]{1,0:T(8,128)(2,1)S(1)} %collective-permute-done.refs_1_), channel_id=1, source_target_pairs={{0,64},{32,96},{64,128},{96,160},{128,192},{160,224},{192,0},{224,... | collective-permute-start | bytes 313352 | tf_op jit(solution)/shard_map/ppermute | solution.py:39
  21.4 7.4 %collective-permute-start.5 = (bf16[136,384]{1,0:T(8,128)(2,1)S(1)}, bf16[136,384]{1,0:T(8,128)(2,1)}, u32[]{:S(2)}, u32[]{:S(2)}) collective-permute-start(bf16[136,384]{1,0:T(8,128)(2,1)S(1)} %collective-permute-done.1.refs_2_), channel_id=1, source_target_pairs={{0,224},{32,0},{64,32},{96,64},{128,96},{160,128},{192,160},{224,1... | collective-permute-start | bytes 313352 | tf_op jit(solution)/shard_map/ppermute | solution.py:39
  21.4 8.2 %collective-permute-start.8 = (bf16[136,384]{1,0:T(8,128)(2,1)S(1)}, bf16[136,384]{1,0:T(8,128)(2,1)S(1)}, u32[]{:S(2)}, u32[]{:S(2)}) collective-permute-start(bf16[136,384]{1,0:T(8,128)(2,1)S(1)} %collective-permute-done.refs_1_), channel_id=1, source_target_pairs={{0,16},{16,0},{1,17},{17,1},{2,18},{18,2},{3,19},{19,3},{4,20},{20... | collective-permute-start | bytes 313352 | tf_op jit(solution)/shard_map/ppermute | solution.py:43
  25.5 4.7 %collective-permute-start.9 = (bf16[136,384]{1,0:T(8,128)(2,1)S(1)}, bf16[136,384]{1,0:T(8,128)(2,1)S(1)}, u32[]{:S(2)}, u32[]{:S(2)}) collective-permute-start(bf16[136,384]{1,0:T(8,128)(2,1)S(1)} %collective-permute-done.1.refs_2_), channel_id=1, source_target_pairs={{0,16},{16,0},{1,17},{17,1},{2,18},{18,2},{3,19},{19,3},{4,20},{20... | collective-permute-start | bytes 313352 | tf_op jit(solution)/shard_map/ppermute | solution.py:43
  26.2 5.3 %collective-permute-start.10 = (bf16[136,384]{1,0:T(8,128)(2,1)}, bf16[136,384]{1,0:T(8,128)(2,1)}, u32[]{:S(2)}, u32[]{:S(2)}) collective-permute-start(bf16[136,384]{1,0:T(8,128)(2,1)} %collective-permute-done.2.refs_3_), channel_id=1, source_target_pairs={{0,16},{16,0},{1,17},{17,1},{2,18},{18,2},{3,19},{19,3},{4,20},{20... | collective-permute-start | bytes 313352 | tf_op jit(solution)/shard_map/ppermute | solution.py:43
  27.2 4.2 %collective-permute-start.11 = (bf16[136,384]{1,0:T(8,128)(2,1)}, bf16[136,384]{1,0:T(8,128)(2,1)}, u32[]{:S(2)}, u32[]{:S(2)}) collective-permute-start(bf16[136,384]{1,0:T(8,128)(2,1)} %collective-permute-done.3.refs_4_), channel_id=1, source_target_pairs={{0,16},{16,0},{1,17},{17,1},{2,18},{18,2},{3,19},{19,3},{4,20},{20... | collective-permute-start | bytes 313352 | tf_op jit(solution)/shard_map/ppermute | solution.py:43
  39.9 20.3 %all-to-all-start = ((bf16[16,64,384]{2,1,0:T(8,128)(2,1)}), bf16[16,64,384]{2,1,0:T(8,128)(2,1)S(1)}, u32[]{:S(2)}, u32[]{:S(2)}) async-start(bf16[16,64,384]{2,1,0:T(8,128)(2,1)} %bitcast.65), calls=%async_computation | async-start | bytes 1572864 | tf_op jit(solution)/shard_map/all_to_all | solution.py:35
  87.1 25.3 %collective-permute-start.16 = (bf16[32,72,384]{2,1,0:T(8,128)(2,1)}, bf16[32,72,384]{2,1,0:T(8,128)(2,1)}, u32[]{:S(2)}, u32[]{:S(2)}) collective-permute-start(bf16[32,72,384]{2,1,0:T(8,128)(2,1)} %all_to_all.15.y), channel_id=1, source_target_pairs={{0,16},{16,0},{1,17},{17,1},{2,18},{18,2},{3,19},{19,3},{4,20},{20... | collective-permute-start | bytes 5308424 | tf_op jit(solution)/shard_map/ppermute | solution.py:43
  92.9 11.0 %collective-permute-start.15 = (bf16[512,384]{1,0:T(8,128)(2,1)}, bf16[512,384]{1,0:T(8,128)(2,1)}, u32[]{:S(2)}, u32[]{:S(2)}) collective-permute-start(bf16[512,384]{1,0:T(8,128)(2,1)} %get-tuple-element.20), channel_id=1, source_target_pairs={{0,32},{16,48},{32,0},{48,16},{1,33},{17,49},{33,1},{49,17},{2,34}... | collective-permute-start | bytes 1179656 | tf_op jit(solution)/shard_map/ppermute | solution.py:245
  93.4 13.4 %collective-permute-start.17 = (bf16[512,384]{1,0:T(8,128)(2,1)}, bf16[512,384]{1,0:T(8,128)(2,1)S(1)}, u32[]{:S(2)}, u32[]{:S(2)}) collective-permute-start(bf16[512,384]{1,0:T(8,128)(2,1)} %get-tuple-element.19), channel_id=1, source_target_pairs={{0,16},{16,0},{32,48},{48,32},{1,17},{17,1},{33,49},{49,33},{2,18}... | collective-permute-start | bytes 1179656 | tf_op jit(solution)/shard_map/ppermute | solution.py:245
  93.7 18.7 %collective-permute-start.18 = (bf16[512,384]{1,0:T(8,128)(2,1)}, bf16[512,384]{1,0:T(8,128)(2,1)S(1)}, u32[]{:S(2)}, u32[]{:S(2)}) collective-permute-start(bf16[512,384]{1,0:T(8,128)(2,1)} %get-tuple-element.18), channel_id=1, source_target_pairs={{0,48},{16,32},{32,16},{48,0},{1,49},{17,33},{33,17},{49,1},{2,50}... | collective-permute-start | bytes 1179656 | tf_op jit(solution)/shard_map/ppermute | solution.py:245
  117.8 18.2 %collective-permute-start.19 = (f16[264,512]{1,0:T(8,128)(2,1)S(1)}, f16[264,512]{1,0:T(8,128)(2,1)}, u32[]{:S(2)}, u32[]{:S(2)}) collective-permute-start(f16[264,512]{1,0:T(8,128)(2,1)S(1)} %convert_element_type.24), channel_id=1, source_target_pairs={{0,128},{64,192},{128,0},{192,64},{1,129},{65,193},{129,1},{193,65... | collective-permute-start | bytes 811016 | tf_op jit(solution)/shard_map/ppermute | solution.py:282
  126.1 16.1 %collective-permute-start.20 = (f16[264,512]{1,0:T(8,128)(2,1)}, f16[264,512]{1,0:T(8,128)(2,1)}, u32[]{:S(2)}, u32[]{:S(2)}) collective-permute-start(f16[264,512]{1,0:T(8,128)(2,1)} %convert_element_type.26), channel_id=1, source_target_pairs={{0,64},{64,128},{128,192},{192,0},{1,65},{65,129},{129,193},{193,1... | collective-permute-start | bytes 811016 | tf_op jit(solution)/shard_map/ppermute | solution.py:282
  128.1 18.3 %collective-permute-start.21 = (f16[264,512]{1,0:T(8,128)(2,1)S(1)}, f16[264,512]{1,0:T(8,128)(2,1)S(1)}, u32[]{:S(2)}, u32[]{:S(2)}) collective-permute-start(f16[264,512]{1,0:T(8,128)(2,1)S(1)} %convert_element_type.28), channel_id=1, source_target_pairs={{0,192},{64,0},{128,64},{192,128},{1,193},{65,1},{129,65},{193,129... | collective-permute-start | bytes 811016 | tf_op jit(solution)/shard_map/ppermute | solution.py:282
  148.9 16.4 %all-to-all-start.2 = ((f32[64,8,128]{2,1,0:T(8,128)}), f32[64,8,128]{2,1,0:T(8,128)S(1)}, u32[]{:S(2)}, u32[]{:S(2)}) async-start(f32[64,8,128]{2,1,0:T(8,128)} %stats.1), calls=%async_computation.2 | async-start | bytes 524288 | tf_op jit(solution)/shard_map/all_to_all | solution.py:35
  165.4 5.6 %collective-permute-start.22 = (f32[8,128]{1,0:T(8,128)S(1)}, f32[8,128]{1,0:T(8,128)S(1)}, u32[]{:S(2)}, u32[]{:S(2)}) collective-permute-start(f32[8,128]{1,0:T(8,128)S(1)} %reduce_sum.48), channel_id=1, source_target_pairs={{0,64},{64,128},{128,192},{192,0},{1,65},{65,129},{129,193},{193,1... | collective-permute-start | bytes 12296 | tf_op jit(solution)/shard_map/ppermute | solution.py:313
  167.6 6.4 %collective-permute-start.23 = (f32[8,128]{1,0:T(8,128)S(1)}, f32[8,128]{1,0:T(8,128)S(1)}, u32[]{:S(2)}, u32[]{:S(2)}) collective-permute-start(f32[8,128]{1,0:T(8,128)S(1)} %reduce_sum.48), channel_id=1, source_target_pairs={{0,128},{64,192},{128,0},{192,64},{1,129},{65,193},{129,1},{193,65... | collective-permute-start | bytes 12296 | tf_op jit(solution)/shard_map/ppermute | solution.py:313
  168.4 5.5 %collective-permute-start.24 = (f32[8,128]{1,0:T(8,128)S(1)}, f32[8,128]{1,0:T(8,128)S(1)}, u32[]{:S(2)}, u32[]{:S(2)}) collective-permute-start(f32[8,128]{1,0:T(8,128)S(1)} %reduce_sum.48), channel_id=1, source_target_pairs={{0,192},{64,0},{128,64},{192,128},{1,193},{65,1},{129,65},{193,129... | collective-permute-start | bytes 12296 | tf_op jit(solution)/shard_map/ppermute | solution.py:313
  (17 other events, 86.6 us)

commit v6 on v5

--- a/solution.py
+++ b/solution.py
@@ -55,9 +55,40 @@
     return pltpu.with_memory_space_constraint(value, pltpu.VMEM)
 
 
+def held(value):
+    return pltpu.with_memory_space_constraint(value, pltpu.HBM)
+
+
 SCALARS = pl.BlockSpec(memory_space=pltpu.SMEM)
 VECTORS = pl.BlockSpec(memory_space=pltpu.VMEM)
 LIMIT = pltpu.CompilerParams(vmem_limit_bytes=24 * 1024 * 1024)
+
+
+def pick_kernel(picks, count, targets, probe, final_far, out, rows, final, arrived):
+    fetch = pltpu.make_async_copy(final_far, final, arrived)
+    fetch.start()
+    sub = lax.broadcasted_iota(jnp.int32, (16, out.shape[1]), 0)
+
+    def take(layer, k):
+        pick = jnp.clip(picks[0, k], 0, final.shape[0] - 1)
+        within = lax.rem(pick, 16)
+        group = pl.ds(pl.multiple_of(pick - within, 16), 16)
+        block = probe[layer, group, :] if layer < LAYERS else final[group, :]
+        row = jnp.sum(jnp.where(sub == within, block.astype(F32), 0.0), axis=0, keepdims=True)
+        rows[layer * CAP + k : layer * CAP + k + 1, :] = row
+
+    for k in range(CAP):
+        for layer in range(LAYERS):
+            take(layer, k)
+    fetch.wait()
+    for k in range(CAP):
+        take(LAYERS, k)
+    out[0:INFO] = rows[...].astype(BF16)
+    out[INFO : INFO + 8] = jnp.zeros((8, out.shape[1]), BF16)
+    line = lax.broadcasted_iota(jnp.int32, (8, CAP), 0)
+    wanted = jnp.broadcast_to(targets[...], (8, CAP))
+    value = jnp.where(line == 0, wanted >> 8, jnp.where(line == 1, wanted & 255, jnp.where(line == 2, count[0], 0)))
+    out[INFO : INFO + 8, 0:CAP] = value.astype(F32).astype(BF16)
 
 
 def translate_kernel(flags, *refs):
@@ -206,20 +237,20 @@
     seq = 4 * zq + quarter
     width = probe_states.shape[2]
     part = unembed.shape[0] // 4
-    picks = answer_rows[0]
-
-    info = jnp.concatenate(
-        [targets // 256, targets % 256, jnp.broadcast_to(answer_count[:, None], (1, CAP)), jnp.zeros((5, CAP), jnp.int32)]
-    )
-    info = jnp.pad(info, ((0, 0), (0, width - CAP))).astype(BF16)
-    local = jnp.concatenate(
-        [
-            jnp.take(probe_states, picks, axis=1, mode="clip").reshape(LAYERS * CAP, width),
-            jnp.take(final_states, picks, axis=0, mode="clip"),
-            info,
+
+    local = pl.pallas_call(
+        pick_kernel,
+        out_shape=whole((INFO + 8, width), BF16),
+        in_specs=[SCALARS] * 2 + [VECTORS] * 2 + [pl.BlockSpec(memory_space=pltpu.HBM)],
+        out_specs=VECTORS,
+        scratch_shapes=[
+            pltpu.VMEM((INFO, width), F32),
+            pltpu.VMEM(final_states.shape, BF16),
+            pltpu.SemaphoreType.DMA(()),
         ],
-        axis=0,
-    )
+        compiler_params=LIMIT,
+        name="pick",
+    )(answer_rows, answer_count, held(targets), near(probe_states), held(final_states))
     back2, fore2, back1, fore1 = [shifted(local, by) for by in (2, -2, 1, -1)]
     own = [local, back2, fore2, back1, fore1]
     other = [swap_cores(chunk) for chunk in own]
@@ -315,11 +346,11 @@
 
     table = every[:, :6].reshape(4, 2, 3, 2, 4, 16).transpose(2, 4, 0, 1, 3, 5).reshape(3, 4, 1, ROWS)
     chunk = (zq - jnp.arange(4, dtype=jnp.int32)) % 4
-    held = (chunk[:, None] * 64 + jnp.arange(64, dtype=jnp.int32)[None, :]).reshape(1, ROWS)
+    ids = (chunk[:, None] * 64 + jnp.arange(64, dtype=jnp.int32)[None, :]).reshape(1, ROWS)
     my_start = jnp.sum(jnp.where(order == seq, starts, 0))
     live = slots < answer_count[0]
     wanted = my_start + slots
-    mine = wanted[:, None] == held
+    mine = wanted[:, None] == ids
     mine = jnp.sum(jnp.where(mine[None, None], table, 0.0), axis=3)
     log_total = jnp.log(mine[0])
     logprob = mine[2] - log_total

time: 176 us -> 167 us (0.949)
  local copies, waits for them, and re-layouts: 13.9 us -> 7.53 us
  other arithmetic: 6.48 us -> 3 us
    unnamed x29 -> x15, local copies, waits for them, and re-layouts: 7.53 us -> 3.89 us
    gather x2 -> x0, local copies, waits for them, and re-layouts: 2.67 us -> none  [the longest x1 1.87 us: body(): jnp.take(final_states, picks, axis=0, mode='clip')]
    pallas_call x0 -> x1, Pallas kernels: none -> 2.08 us  [body(): pl.pallas_call(pick_kernel, out_shape=whole((INFO + 8, width), BF16), in_...]
  transfers between devices with their start and end apart: 27 -> 27, of which waited for: 12 -> 13; matrix products, arithmetic and copies ran while one was open for 3% -> 3% of each run, Pallas kernels for 4% -> 3%
where the time goes in v6:
time: 167 us
  waiting for transfers between devices  56.9 us (34%)
  starting transfers between devices  55.8 us (33%)
  blocking collectives  26.6 us (16%)
  Pallas kernels  15.3 us (9%)
  local copies, waits for them, and re-layouts  7.53 us (5%)
  other arithmetic  3 us (2%)
    all_to_all x1, blocking collectives, exchange(): return lax.all_to_all(value, axes, split_axis=0, concat_axis=0, tiled=True)  26.6 us
    all_to_all x2, waiting for transfers between devices, exchange(): return lax.all_to_all(value, axes, split_axis=0, concat_axis=0, tiled=True)  21.3 us
    ppermute x3, waiting for transfers between devices, body(): chunk = lax.ppermute(chunk, 'zq', [(j, (j + k) % 4) for j in range(4)])  15.5 us
    ppermute x3, waiting for transfers between devices, body(): block = lax.ppermute(block, ('zp', 'c'), [(j, j ^ k) for j in range(4)])  14.4 us
    all_to_all x2, starting transfers between devices, exchange(): return lax.all_to_all(value, axes, split_axis=0, concat_axis=0, tiled=True)  13.8 us
    ppermute x7, starting transfers between devices, shifted(): return lax.ppermute(value, Z, [(j, (j + by) % 8) for j in range(8)])  13.5 us
    ppermute x9, starting transfers between devices, swap_cores(): return lax.ppermute(value, 'c', [(0, 1), (1, 0)])  11.6 us
    ppermute x3, starting transfers between devices, body(): chunk = lax.ppermute(chunk, 'zq', [(j, (j + k) % 4) for j in range(4)])  9.42 us
  transfers between devices with their start and end apart: 27, of which 13 were waited for; matrix products, arithmetic and copies ran while one was open for 3% of the time, Pallas kernels for 3%

profile of v6, /device:TPU:1, one launch (start us, length us, event | category | flops | bytes accessed | tf_op | source)
XLA Modules:
  0.0 166.7 jit_solution(3404058096265713593)
XLA Ops:
  3.6 2.1 %pick.1.refs_0_ = bf16[136,384]{1,0:T(8,128)(2,1)S(1)} custom-call(s32[1,32]{1,0:T(1,128)S(1)} %copy-done.3, s32[1]{0:T(128)} %copy.33.count, s32[1,32]{1,0:T(1,128)} %targets.1, bf16[3,1024,384]{2,1,0:T(8,128)(2,1)S(1)} %copy-done, bf16[1024,384]{1,0:T(8,128)(2,1)} %final_far.1), custom_call_target="tpu_custom_call" | custom-call | tf_op jit(solution)/shard_map/pick/pallas_call | solution.py:241
  5.7 3.9 %collective-permute-start = (bf16[136,384]{1,0:T(8,128)(2,1)S(1)}, bf16[136,384]{1,0:T(8,128)(2,1)S(1)}, u32[]{:S(2)}, u32[]{:S(2)}) collective-permute-start(bf16[136,384]{1,0:T(8,128)(2,1)S(1)} %pick.1.refs_0_), channel_id=1, source_target_pairs={{0,64},{32,96},{64,128},{96,160},{128,192},{160,224},{192,0},{224,... | collective-permute-start | bytes 313352 | tf_op jit(solution)/shard_map/ppermute | solution.py:39
  9.6 3.1 %collective-permute-start.1 = (bf16[136,384]{1,0:T(8,128)(2,1)S(1)}, bf16[136,384]{1,0:T(8,128)(2,1)S(1)}, u32[]{:S(2)}, u32[]{:S(2)}) collective-permute-start(bf16[136,384]{1,0:T(8,128)(2,1)S(1)} %pick.1.refs_0_), channel_id=1, source_target_pairs={{0,192},{32,224},{64,0},{96,32},{128,64},{160,96},{192,128},{224,1... | collective-permute-start | bytes 313352 | tf_op jit(solution)/shard_map/ppermute | solution.py:39
  19.0 2.2 %collective-permute-start.6 = (bf16[136,384]{1,0:T(8,128)(2,1)S(1)}, bf16[136,384]{1,0:T(8,128)(2,1)S(1)}, u32[]{:S(2)}, u32[]{:S(2)}) collective-permute-start(bf16[136,384]{1,0:T(8,128)(2,1)S(1)} %collective-permute-done.refs_1_), channel_id=1, source_target_pairs={{0,64},{32,96},{64,128},{96,160},{128,192},{160,224},{192,0},{224,... | collective-permute-start | bytes 313352 | tf_op jit(solution)/shard_map/ppermute | solution.py:39
  21.2 3.4 %collective-permute-start.8 = (bf16[136,384]{1,0:T(8,128)(2,1)S(1)}, bf16[136,384]{1,0:T(8,128)(2,1)S(1)}, u32[]{:S(2)}, u32[]{:S(2)}) collective-permute-start(bf16[136,384]{1,0:T(8,128)(2,1)S(1)} %collective-permute-done.refs_1_), channel_id=1, source_target_pairs={{0,16},{16,0},{1,17},{17,1},{2,18},{18,2},{3,19},{19,3},{4,20},{20... | collective-permute-start | bytes 313352 | tf_op jit(solution)/shard_map/ppermute | solution.py:43
  30.7 2.9 %translate.1 = (bf16[16,4,16,384]{3,2,1,0:T(8,128)(2,1)}, f32[16,8,128]{2,1,0:T(8,128)}) custom-call(s32[5]{0:T(128)S(1)} %stack.42.flags, bf16[136,384]{1,0:T(8,128)(2,1)S(1)} %pick.1.refs_0_, bf16[136,384]{1,0:T(8,128)(2,1)S(1)} %collective-permute-done.refs_1_, bf16[136,384]{1,0:T(8,128)(2,1)S(1)} %collective-permute-done.1.refs_2_, ...), custom_call_target="tpu_custom_call" | custom-call | tf_op jit(solution)/shard_map/translate/pallas_call | solution.py:262
  33.6 6.8 %all-to-all-start = ((bf16[16,64,384]{2,1,0:T(8,128)(2,1)}), bf16[16,64,384]{2,1,0:T(8,128)(2,1)S(1)}, u32[]{:S(2)}, u32[]{:S(2)}) async-start(bf16[16,64,384]{2,1,0:T(8,128)(2,1)} %bitcast.59), calls=%async_computation | async-start | bytes 1572864 | tf_op jit(solution)/shard_map/all_to_all | solution.py:35
  40.4 13.5 %all-to-all-done.parts = bf16[16,64,384]{2,1,0:T(8,128)(2,1)S(1)} async-done(((bf16[16,64,384]{2,1,0:T(8,128)(2,1)}), bf16[16,64,384]{2,1,0:T(8,128)(2,1)S(1)}, u32[]{:S(2)}, u32[]{:S(2)}) %all-to-all-start) | async-done | bytes 786464 | tf_op jit(solution)/shard_map/all_to_all | solution.py:35
  54.5 26.6 %all_to_all.15.y = bf16[32,72,384]{2,1,0:T(8,128)(2,1)S(1)} all-to-all(bf16[32,72,384]{2,1,0:T(8,128)(2,1)S(1)} %scale.1), channel_id=1, replica_groups=mesh['zq'=4,'zp'=2,'c'=2,'y'=4,'x'=4] {'zp','y','x'}, dimensions={0} | all-to-all | bytes 3538944 | tf_op jit(solution)/shard_map/all_to_all | solution.py:35
  81.1 2.9 %collective-permute-start.16 = (bf16[32,72,384]{2,1,0:T(8,128)(2,1)S(1)}, bf16[32,72,384]{2,1,0:T(8,128)(2,1)S(1)}, u32[]{:S(2)}, u32[]{:S(2)}) collective-permute-start(bf16[32,72,384]{2,1,0:T(8,128)(2,1)S(1)} %all_to_all.15.y), channel_id=1, source_target_pairs={{0,16},{16,0},{1,17},{17,1},{2,18},{18,2},{3,19},{19,3},{4,20},{20... | collective-permute-start | bytes 5308424 | tf_op jit(solution)/shard_map/ppermute | solution.py:43
  84.0 2.5 %dynamic-slice_bitcast_fusion = (bf16[512,384]{1,0:T(8,128)(2,1)}, bf16[512,384]{1,0:T(8,128)(2,1)}, bf16[512,384]{1,0:T(8,128)(2,1)}, bf16[512,384]{1,0:T(8,128)(2,1)}) fusion(bf16[4,512,384]{2,1,0:T(8,128)(2,1)} %bitcast.58, s32[]{:T(128)S(6)} %select_n.75, s32[]{:T(128)S(6)} %select_n.74, s32[]{:T(128)S(6)} %select_n.73, s32[]{:T(128)S(6)} %select_n.72), kind=kLoop, calls=%fused_computation.2 | loop fusion | bytes 3145744 | tf_op jit(solution)/shard_map/jit(dynamic_index_in_dim)/squeeze | solution.py:274
  88.4 9.1 %collective-permute-done.15.u_far = bf16[512,384]{1,0:T(8,128)(2,1)} collective-permute-done((bf16[512,384]{1,0:T(8,128)(2,1)}, bf16[512,384]{1,0:T(8,128)(2,1)}, u32[]{:S(2)}, u32[]{:S(2)}) %collective-permute-start.15) | collective-permute-done | bytes 393248 | tf_op jit(solution)/shard_map/ppermute | solution.py:276
  98.5 2.3 %own_logits.1.own_part = f32[4,264,512]{2,1,0:T(8,128)S(1)} custom-call(s32[5]{0:T(128)S(1)} %stack.42.flags, bf16[32,72,384]{2,1,0:T(8,128)(2,1)S(1)} %all_to_all.15.y, bf16[512,384]{1,0:T(8,128)(2,1)S(1)} %copy-done.1, bf16[512,384]{1,0:T(8,128)(2,1)} %collective-permute-done.15.u_far), custom_call_target="tpu_custom_call" | custom-call | tf_op jit(solution)/shard_map/own_logits/pallas_call | solution.py:294
  100.8 5.3 %collective-permute-done.18.u_far = bf16[512,384]{1,0:T(8,128)(2,1)} collective-permute-done((bf16[512,384]{1,0:T(8,128)(2,1)}, bf16[512,384]{1,0:T(8,128)(2,1)}, u32[]{:S(2)}, u32[]{:S(2)}) %collective-permute-start.18) | collective-permute-done | bytes 393248 | tf_op jit(solution)/shard_map/ppermute | solution.py:276
  110.0 5.7 %collective-permute-start.19 = (f16[264,512]{1,0:T(8,128)(2,1)S(1)}, f16[264,512]{1,0:T(8,128)(2,1)S(1)}, u32[]{:S(2)}, u32[]{:S(2)}) collective-permute-start(f16[264,512]{1,0:T(8,128)(2,1)S(1)} %convert_element_type.23), channel_id=1, source_target_pairs={{0,128},{64,192},{128,0},{192,64},{1,129},{65,193},{129,1},{193,65... | collective-permute-start | bytes 811016 | tf_op jit(solution)/shard_map/ppermute | solution.py:313
  119.1 3.6 %collective-permute-start.21 = (f16[264,512]{1,0:T(8,128)(2,1)S(1)}, f16[264,512]{1,0:T(8,128)(2,1)S(1)}, u32[]{:S(2)}, u32[]{:S(2)}) collective-permute-start(f16[264,512]{1,0:T(8,128)(2,1)S(1)} %convert_element_type.27), channel_id=1, source_target_pairs={{0,192},{64,0},{128,64},{192,128},{1,193},{65,1},{129,65},{193,129... | collective-permute-start | bytes 811016 | tf_op jit(solution)/shard_map/ppermute | solution.py:313
  123.1 5.1 %collective-permute-done.19 = f16[264,512]{1,0:T(8,128)(2,1)S(1)} collective-permute-done((f16[264,512]{1,0:T(8,128)(2,1)S(1)}, f16[264,512]{1,0:T(8,128)(2,1)S(1)}, u32[]{:S(2)}, u32[]{:S(2)}) %collective-permute-start.19) | collective-permute-done | bytes 270368 | tf_op jit(solution)/shard_map/ppermute | solution.py:313
  128.3 6.1 %collective-permute-done.20 = f16[264,512]{1,0:T(8,128)(2,1)S(1)} collective-permute-done((f16[264,512]{1,0:T(8,128)(2,1)S(1)}, f16[264,512]{1,0:T(8,128)(2,1)S(1)}, u32[]{:S(2)}, u32[]{:S(2)}) %collective-permute-start.20) | collective-permute-done | bytes 270368 | tf_op jit(solution)/shard_map/ppermute | solution.py:313
  134.4 4.3 %collective-permute-done.21 = f16[264,512]{1,0:T(8,128)(2,1)S(1)} collective-permute-done((f16[264,512]{1,0:T(8,128)(2,1)S(1)}, f16[264,512]{1,0:T(8,128)(2,1)S(1)}, u32[]{:S(2)}, u32[]{:S(2)}) %collective-permute-start.21) | collective-permute-done | bytes 270368 | tf_op jit(solution)/shard_map/ppermute | solution.py:313
  140.0 7.1 %all-to-all-start.2 = ((f32[64,8,128]{2,1,0:T(8,128)}), f32[64,8,128]{2,1,0:T(8,128)S(1)}, u32[]{:S(2)}, u32[]{:S(2)}) async-start(f32[64,8,128]{2,1,0:T(8,128)} %stats.1), calls=%async_computation.2 | async-start | bytes 524288 | tf_op jit(solution)/shard_map/all_to_all | solution.py:35
  148.6 7.8 %all-to-all-done.2 = f32[64,8,128]{2,1,0:T(8,128)S(1)} async-done(((f32[64,8,128]{2,1,0:T(8,128)}), f32[64,8,128]{2,1,0:T(8,128)S(1)}, u32[]{:S(2)}, u32[]{:S(2)}) %all-to-all-start.2) | async-done | bytes 262176 | tf_op jit(solution)/shard_map/all_to_all | solution.py:35
  156.4 2.2 %collective-permute-start.22 = (f32[8,128]{1,0:T(8,128)S(1)}, f32[8,128]{1,0:T(8,128)S(1)}, u32[]{:S(2)}, u32[]{:S(2)}) collective-permute-start(f32[8,128]{1,0:T(8,128)S(1)} %reduce_sum.48), channel_id=1, source_target_pairs={{0,64},{64,128},{128,192},{192,0},{1,65},{65,129},{129,193},{193,1... | collective-permute-start | bytes 12296 | tf_op jit(solution)/shard_map/ppermute | solution.py:344
  159.5 2.4 %collective-permute-start.24 = (f32[8,128]{1,0:T(8,128)S(1)}, f32[8,128]{1,0:T(8,128)S(1)}, u32[]{:S(2)}, u32[]{:S(2)}) collective-permute-start(f32[8,128]{1,0:T(8,128)S(1)} %reduce_sum.48), channel_id=1, source_target_pairs={{0,192},{64,0},{128,64},{192,128},{1,193},{65,1},{129,65},{193,129... | collective-permute-start | bytes 12296 | tf_op jit(solution)/shard_map/ppermute | solution.py:344
  162.0 2.9 %collective-permute-done.23 = f32[8,128]{1,0:T(8,128)S(1)} collective-permute-done((f32[8,128]{1,0:T(8,128)S(1)}, f32[8,128]{1,0:T(8,128)S(1)}, u32[]{:S(2)}, u32[]{:S(2)}) %collective-permute-start.23) | collective-permute-done | bytes 4128 | tf_op jit(solution)/shard_map/ppermute | solution.py:344
  (92 shorter events, 31.3 us)
Async XLA Ops:
  5.7 11.2 %collective-permute-start = (bf16[136,384]{1,0:T(8,128)(2,1)S(1)}, bf16[136,384]{1,0:T(8,128)(2,1)S(1)}, u32[]{:S(2)}, u32[]{:S(2)}) collective-permute-start(bf16[136,384]{1,0:T(8,128)(2,1)S(1)} %pick.1.refs_0_), channel_id=1, source_target_pairs={{0,64},{32,96},{64,128},{96,160},{128,192},{160,224},{192,0},{224,... | collective-permute-start | bytes 313352 | tf_op jit(solution)/shard_map/ppermute | solution.py:39
  9.6 9.4 %collective-permute-start.1 = (bf16[136,384]{1,0:T(8,128)(2,1)S(1)}, bf16[136,384]{1,0:T(8,128)(2,1)S(1)}, u32[]{:S(2)}, u32[]{:S(2)}) collective-permute-start(bf16[136,384]{1,0:T(8,128)(2,1)S(1)} %pick.1.refs_0_), channel_id=1, source_target_pairs={{0,192},{32,224},{64,0},{96,32},{128,64},{160,96},{192,128},{224,1... | collective-permute-start | bytes 313352 | tf_op jit(solution)/shard_map/ppermute | solution.py:39
  12.7 8.5 %collective-permute-start.2 = (bf16[136,384]{1,0:T(8,128)(2,1)S(1)}, bf16[136,384]{1,0:T(8,128)(2,1)S(1)}, u32[]{:S(2)}, u32[]{:S(2)}) collective-permute-start(bf16[136,384]{1,0:T(8,128)(2,1)S(1)} %pick.1.refs_0_), channel_id=1, source_target_pairs={{0,32},{32,64},{64,96},{96,128},{128,160},{160,192},{192,224},{224... | collective-permute-start | bytes 313352 | tf_op jit(solution)/shard_map/ppermute | solution.py:39
  13.4 7.8 %collective-permute-start.3 = (bf16[136,384]{1,0:T(8,128)(2,1)S(1)}, bf16[136,384]{1,0:T(8,128)(2,1)S(1)}, u32[]{:S(2)}, u32[]{:S(2)}) collective-permute-start(bf16[136,384]{1,0:T(8,128)(2,1)S(1)} %pick.1.refs_0_), channel_id=1, source_target_pairs={{0,224},{32,0},{64,32},{96,64},{128,96},{160,128},{192,160},{224,1... | collective-permute-start | bytes 313352 | tf_op jit(solution)/shard_map/ppermute | solution.py:39
  15.4 9.3 %collective-permute-start.7 = (bf16[136,384]{1,0:T(8,128)(2,1)S(1)}, bf16[136,384]{1,0:T(8,128)(2,1)S(1)}, u32[]{:S(2)}, u32[]{:S(2)}) collective-permute-start(bf16[136,384]{1,0:T(8,128)(2,1)S(1)} %pick.1.refs_0_), channel_id=1, source_target_pairs={{0,16},{16,0},{1,17},{17,1},{2,18},{18,2},{3,19},{19,3},{4,20},{20... | collective-permute-start | bytes 313352 | tf_op jit(solution)/shard_map/ppermute | solution.py:43
  16.9 7.9 %collective-permute-start.4 = (bf16[136,384]{1,0:T(8,128)(2,1)S(1)}, bf16[136,384]{1,0:T(8,128)(2,1)S(1)}, u32[]{:S(2)}, u32[]{:S(2)}) collective-permute-start(bf16[136,384]{1,0:T(8,128)(2,1)S(1)} %collective-permute-done.refs_1_), channel_id=1, source_target_pairs={{0,32},{32,64},{64,96},{96,128},{128,160},{160,192},{192,224},{224... | collective-permute-start | bytes 313352 | tf_op jit(solution)/shard_map/ppermute | solution.py:39
  19.0 7.6 %collective-permute-start.6 = (bf16[136,384]{1,0:T(8,128)(2,1)S(1)}, bf16[136,384]{1,0:T(8,128)(2,1)S(1)}, u32[]{:S(2)}, u32[]{:S(2)}) collective-permute-start(bf16[136,384]{1,0:T(8,128)(2,1)S(1)} %collective-permute-done.refs_1_), channel_id=1, source_target_pairs={{0,64},{32,96},{64,128},{96,160},{128,192},{160,224},{192,0},{224,... | collective-permute-start | bytes 313352 | tf_op jit(solution)/shard_map/ppermute | solution.py:39
  21.2 7.3 %collective-permute-start.5 = (bf16[136,384]{1,0:T(8,128)(2,1)S(1)}, bf16[136,384]{1,0:T(8,128)(2,1)S(1)}, u32[]{:S(2)}, u32[]{:S(2)}) collective-permute-start(bf16[136,384]{1,0:T(8,128)(2,1)S(1)} %collective-permute-done.1.refs_2_), channel_id=1, source_target_pairs={{0,224},{32,0},{64,32},{96,64},{128,96},{160,128},{192,160},{224,1... | collective-permute-start | bytes 313352 | tf_op jit(solution)/shard_map/ppermute | solution.py:39
  21.2 8.0 %collective-permute-start.8 = (bf16[136,384]{1,0:T(8,128)(2,1)S(1)}, bf16[136,384]{1,0:T(8,128)(2,1)S(1)}, u32[]{:S(2)}, u32[]{:S(2)}) collective-permute-start(bf16[136,384]{1,0:T(8,128)(2,1)S(1)} %collective-permute-done.refs_1_), channel_id=1, source_target_pairs={{0,16},{16,0},{1,17},{17,1},{2,18},{18,2},{3,19},{19,3},{4,20},{20... | collective-permute-start | bytes 313352 | tf_op jit(solution)/shard_map/ppermute | solution.py:43
  24.7 4.6 %collective-permute-start.9 = (bf16[136,384]{1,0:T(8,128)(2,1)S(1)}, bf16[136,384]{1,0:T(8,128)(2,1)S(1)}, u32[]{:S(2)}, u32[]{:S(2)}) collective-permute-start(bf16[136,384]{1,0:T(8,128)(2,1)S(1)} %collective-permute-done.1.refs_2_), channel_id=1, source_target_pairs={{0,16},{16,0},{1,17},{17,1},{2,18},{18,2},{3,19},{19,3},{4,20},{20... | collective-permute-start | bytes 313352 | tf_op jit(solution)/shard_map/ppermute | solution.py:43
  24.8 5.1 %collective-permute-start.10 = (bf16[136,384]{1,0:T(8,128)(2,1)S(1)}, bf16[136,384]{1,0:T(8,128)(2,1)S(1)}, u32[]{:S(2)}, u32[]{:S(2)}) collective-permute-start(bf16[136,384]{1,0:T(8,128)(2,1)S(1)} %collective-permute-done.2.refs_3_), channel_id=1, source_target_pairs={{0,16},{16,0},{1,17},{17,1},{2,18},{18,2},{3,19},{19,3},{4,20},{20... | collective-permute-start | bytes 313352 | tf_op jit(solution)/shard_map/ppermute | solution.py:43
  26.6 3.3 %collective-permute-start.11 = (bf16[136,384]{1,0:T(8,128)(2,1)S(1)}, bf16[136,384]{1,0:T(8,128)(2,1)S(1)}, u32[]{:S(2)}, u32[]{:S(2)}) collective-permute-start(bf16[136,384]{1,0:T(8,128)(2,1)S(1)} %collective-permute-done.3.refs_4_), channel_id=1, source_target_pairs={{0,16},{16,0},{1,17},{17,1},{2,18},{18,2},{3,19},{19,3},{4,20},{20... | collective-permute-start | bytes 313352 | tf_op jit(solution)/shard_map/ppermute | solution.py:43
  33.6 20.3 %all-to-all-start = ((bf16[16,64,384]{2,1,0:T(8,128)(2,1)}), bf16[16,64,384]{2,1,0:T(8,128)(2,1)S(1)}, u32[]{:S(2)}, u32[]{:S(2)}) async-start(bf16[16,64,384]{2,1,0:T(8,128)(2,1)} %bitcast.59), calls=%async_computation | async-start | bytes 1572864 | tf_op jit(solution)/shard_map/all_to_all | solution.py:35
  81.1 25.0 %collective-permute-start.16 = (bf16[32,72,384]{2,1,0:T(8,128)(2,1)S(1)}, bf16[32,72,384]{2,1,0:T(8,128)(2,1)S(1)}, u32[]{:S(2)}, u32[]{:S(2)}) collective-permute-start(bf16[32,72,384]{2,1,0:T(8,128)(2,1)S(1)} %all_to_all.15.y), channel_id=1, source_target_pairs={{0,16},{16,0},{1,17},{17,1},{2,18},{18,2},{3,19},{19,3},{4,20},{20... | collective-permute-start | bytes 5308424 | tf_op jit(solution)/shard_map/ppermute | solution.py:43
  86.5 11.0 %collective-permute-start.15 = (bf16[512,384]{1,0:T(8,128)(2,1)}, bf16[512,384]{1,0:T(8,128)(2,1)}, u32[]{:S(2)}, u32[]{:S(2)}) collective-permute-start(bf16[512,384]{1,0:T(8,128)(2,1)} %get-tuple-element.20), channel_id=1, source_target_pairs={{0,32},{16,48},{32,0},{48,16},{1,33},{17,49},{33,1},{49,17},{2,34}... | collective-permute-start | bytes 1179656 | tf_op jit(solution)/shard_map/ppermute | solution.py:276
  87.1 13.7 %collective-permute-start.17 = (bf16[512,384]{1,0:T(8,128)(2,1)}, bf16[512,384]{1,0:T(8,128)(2,1)}, u32[]{:S(2)}, u32[]{:S(2)}) collective-permute-start(bf16[512,384]{1,0:T(8,128)(2,1)} %get-tuple-element.19), channel_id=1, source_target_pairs={{0,16},{16,0},{32,48},{48,32},{1,17},{17,1},{33,49},{49,33},{2,18}... | collective-permute-start | bytes 1179656 | tf_op jit(solution)/shard_map/ppermute | solution.py:276
  87.4 18.8 %collective-permute-start.18 = (bf16[512,384]{1,0:T(8,128)(2,1)}, bf16[512,384]{1,0:T(8,128)(2,1)}, u32[]{:S(2)}, u32[]{:S(2)}) collective-permute-start(bf16[512,384]{1,0:T(8,128)(2,1)} %get-tuple-element.18), channel_id=1, source_target_pairs={{0,48},{16,32},{32,16},{48,0},{1,49},{17,33},{33,17},{49,1},{2,50}... | collective-permute-start | bytes 1179656 | tf_op jit(solution)/shard_map/ppermute | solution.py:276
  110.0 18.3 %collective-permute-start.19 = (f16[264,512]{1,0:T(8,128)(2,1)S(1)}, f16[264,512]{1,0:T(8,128)(2,1)S(1)}, u32[]{:S(2)}, u32[]{:S(2)}) collective-permute-start(f16[264,512]{1,0:T(8,128)(2,1)S(1)} %convert_element_type.23), channel_id=1, source_target_pairs={{0,128},{64,192},{128,0},{192,64},{1,129},{65,193},{129,1},{193,65... | collective-permute-start | bytes 811016 | tf_op jit(solution)/shard_map/ppermute | solution.py:313
  117.3 17.1 %collective-permute-start.20 = (f16[264,512]{1,0:T(8,128)(2,1)S(1)}, f16[264,512]{1,0:T(8,128)(2,1)S(1)}, u32[]{:S(2)}, u32[]{:S(2)}) collective-permute-start(f16[264,512]{1,0:T(8,128)(2,1)S(1)} %convert_element_type.25), channel_id=1, source_target_pairs={{0,64},{64,128},{128,192},{192,0},{1,65},{65,129},{129,193},{193,1... | collective-permute-start | bytes 811016 | tf_op jit(solution)/shard_map/ppermute | solution.py:313
  119.1 19.6 %collective-permute-start.21 = (f16[264,512]{1,0:T(8,128)(2,1)S(1)}, f16[264,512]{1,0:T(8,128)(2,1)S(1)}, u32[]{:S(2)}, u32[]{:S(2)}) collective-permute-start(f16[264,512]{1,0:T(8,128)(2,1)S(1)} %convert_element_type.27), channel_id=1, source_target_pairs={{0,192},{64,0},{128,64},{192,128},{1,193},{65,1},{129,65},{193,129... | collective-permute-start | bytes 811016 | tf_op jit(solution)/shard_map/ppermute | solution.py:313
  140.0 16.3 %all-to-all-start.2 = ((f32[64,8,128]{2,1,0:T(8,128)}), f32[64,8,128]{2,1,0:T(8,128)S(1)}, u32[]{:S(2)}, u32[]{:S(2)}) async-start(f32[64,8,128]{2,1,0:T(8,128)} %stats.1), calls=%async_computation.2 | async-start | bytes 524288 | tf_op jit(solution)/shard_map/all_to_all | solution.py:35
  156.4 5.6 %collective-permute-start.22 = (f32[8,128]{1,0:T(8,128)S(1)}, f32[8,128]{1,0:T(8,128)S(1)}, u32[]{:S(2)}, u32[]{:S(2)}) collective-permute-start(f32[8,128]{1,0:T(8,128)S(1)} %reduce_sum.48), channel_id=1, source_target_pairs={{0,64},{64,128},{128,192},{192,0},{1,65},{65,129},{129,193},{193,1... | collective-permute-start | bytes 12296 | tf_op jit(solution)/shard_map/ppermute | solution.py:344
  158.6 6.4 %collective-permute-start.23 = (f32[8,128]{1,0:T(8,128)S(1)}, f32[8,128]{1,0:T(8,128)S(1)}, u32[]{:S(2)}, u32[]{:S(2)}) collective-permute-start(f32[8,128]{1,0:T(8,128)S(1)} %reduce_sum.48), channel_id=1, source_target_pairs={{0,128},{64,192},{128,0},{192,64},{1,129},{65,193},{129,1},{193,65... | collective-permute-start | bytes 12296 | tf_op jit(solution)/shard_map/ppermute | solution.py:344
  159.5 5.4 %collective-permute-start.24 = (f32[8,128]{1,0:T(8,128)S(1)}, f32[8,128]{1,0:T(8,128)S(1)}, u32[]{:S(2)}, u32[]{:S(2)}) collective-permute-start(f32[8,128]{1,0:T(8,128)S(1)} %reduce_sum.48), channel_id=1, source_target_pairs={{0,192},{64,0},{128,64},{192,128},{1,193},{65,1},{129,65},{193,129... | collective-permute-start | bytes 12296 | tf_op jit(solution)/shard_map/ppermute | solution.py:344
  (10 other events, 62.9 us)

commit v7 on v6

--- a/solution.py
+++ b/solution.py
@@ -20,7 +20,7 @@
 BF16 = jnp.bfloat16
 NT = (((1,), (1,)), ((), ()))
 TN = (((0,), (0,)), ((), ()))
-INFO = 128
+INFO = 96
 OFFSETS = (0, -2, 2, -1, 1, -3, 3, -4)
 SHIFT = 16.0
 SCALE = 262144.0
@@ -64,7 +64,7 @@
 LIMIT = pltpu.CompilerParams(vmem_limit_bytes=24 * 1024 * 1024)
 
 
-def pick_kernel(picks, count, targets, probe, final_far, out, rows, final, arrived):
+def pick_kernel(picks, count, targets, probe, final_far, out, last, rows, final, arrived):
     fetch = pltpu.make_async_copy(final_far, final, arrived)
     fetch.start()
     sub = lax.broadcasted_iota(jnp.int32, (16, out.shape[1]), 0)
@@ -83,7 +83,8 @@
     fetch.wait()
     for k in range(CAP):
         take(LAYERS, k)
-    out[0:INFO] = rows[...].astype(BF16)
+    out[0:INFO] = rows[0:INFO].astype(BF16)
+    last[...] = rows[INFO : INFO + CAP].astype(BF16)
     out[INFO : INFO + 8] = jnp.zeros((8, out.shape[1]), BF16)
     line = lax.broadcasted_iota(jnp.int32, (8, CAP), 0)
     wanted = jnp.broadcast_to(targets[...], (8, CAP))
@@ -93,7 +94,7 @@
 
 def translate_kernel(flags, *refs):
     own, other = refs[:8], refs[8:16]
-    translator, out, info = refs[16:]
+    final, translator, out, info = refs[16:]
     low_core = flags[0] == 0
     keep = flags[1].astype(F32)
     chips = [lax.rem(flags[4] + offset + 8, 8) for offset in OFFSETS]
@@ -101,6 +102,13 @@
     slot = lax.broadcasted_iota(jnp.int32, (CAP, ROWS), 0).astype(F32)
     counts_own = [ref[INFO + 2 : INFO + 3, 0:1].astype(F32) for ref in own]
     counts_other = [ref[INFO + 2 : INFO + 3, 0:1].astype(F32) for ref in other]
+    start = jnp.zeros((1, 1), F32)
+    count = jnp.zeros((1, 1), F32)
+    for k in range(8):
+        for seq, value in ((2 * chips[k] + flags[0], counts_own[k]), (2 * chips[k] + 1 - flags[0], counts_other[k])):
+            start = start + jnp.where(seq < flags[5], value, 0.0)
+            count = count + jnp.where(seq == flags[5], value, 0.0)
+    pick_final = jnp.where((lane == start + slot) & (slot < count), 1.0, 0.0).astype(BF16)
     pick_own, pick_other = [], []
     for k in range(8):
         base = jnp.zeros((1, 1), F32)
@@ -119,16 +127,16 @@
         info[2 * chips[k] + 1] = jnp.where(low_core, b, a)
     pick_own = jnp.concatenate(pick_own, axis=0)
     pick_other = jnp.concatenate(pick_other, axis=0)
-    for layer in range(LAYERS + 1):
+    for layer in range(LAYERS):
         low = layer * CAP
         a = jnp.concatenate([ref[low : low + CAP, :] for ref in own], axis=0)
         b = jnp.concatenate([ref[low : low + CAP, :] for ref in other], axis=0)
         rows = lax.dot_general(pick_own, a, TN, preferred_element_type=F32)
         rows = rows + lax.dot_general(pick_other, b, TN, preferred_element_type=F32)
-        part = rows * keep
-        if layer < LAYERS:
-            part = part + dot(rows.astype(BF16), translator[layer])
+        part = rows * keep + dot(rows.astype(BF16), translator[layer])
         out[:, layer] = part.astype(BF16).reshape(16, 16, -1)
+    rows = lax.dot_general(pick_final, final[...], TN, preferred_element_type=F32)
+    out[:, LAYERS] = rows.astype(BF16).reshape(16, 16, -1)
 
 
 def high_low(value):
@@ -238,13 +246,13 @@
     width = probe_states.shape[2]
     part = unembed.shape[0] // 4
 
-    local = pl.pallas_call(
+    local, last = pl.pallas_call(
         pick_kernel,
-        out_shape=whole((INFO + 8, width), BF16),
+        out_shape=(whole((INFO + 8, width), BF16), whole((CAP, width), BF16)),
         in_specs=[SCALARS] * 2 + [VECTORS] * 2 + [pl.BlockSpec(memory_space=pltpu.HBM)],
-        out_specs=VECTORS,
+        out_specs=(VECTORS, VECTORS),
         scratch_shapes=[
-            pltpu.VMEM((INFO, width), F32),
+            pltpu.VMEM((INFO + CAP, width), F32),
             pltpu.VMEM(final_states.shape, BF16),
             pltpu.SemaphoreType.DMA(()),
         ],
@@ -253,20 +261,23 @@
     )(answer_rows, answer_count, held(targets), near(probe_states), held(final_states))
     back2, fore2, back1, fore1 = [shifted(local, by) for by in (2, -2, 1, -1)]
     own = [local, back2, fore2, back1, fore1]
-    other = [swap_cores(chunk) for chunk in own]
+    other = [swap_cores(chunk) for chunk in own[1:]]
+    other = [swap_cores(local)] + other
+    turned = [(a * 16 + b, b * 16 + a) for a in range(16) for b in range(16)]
+    last = lax.ppermute(last, (*SEQ, *VOCAB), turned)
     third = [shifted(back2, 1), shifted(fore2, -1), shifted(back2, 2)]
     own += third
     other += [swap_cores(chunk) for chunk in third]
 
-    flags = jnp.stack([c, (seq == v).astype(jnp.int32), quarter // 2, zq, seq // 2])
+    flags = jnp.stack([c, (seq == v).astype(jnp.int32), quarter // 2, zq, seq // 2, v])
     parts, every_info = pl.pallas_call(
         translate_kernel,
         out_shape=(far((16, 4, 16, width), BF16), far((16, 8, 128), F32)),
-        in_specs=[SCALARS] + [VECTORS] * 17,
+        in_specs=[SCALARS] + [VECTORS] * 18,
         out_specs=(VECTORS, VECTORS),
         compiler_params=LIMIT,
         name="translate",
-    )(flags, *[near(chunk) for chunk in own + other], near(translator))
+    )(flags, *[near(chunk) for chunk in own + other], near(last), near(translator))
     arrived = exchange(parts.reshape(16, 64, width), VOCAB)
     fours = unembed.reshape(4, part, width)
     quarters = []

time: 167 us -> 170 us (1.018)
    ppermute x0 -> x1, starting transfers between devices: none -> 4.5 us  [body(): last = lax.ppermute(last, (*SEQ, *VOCAB), turned)]
    ppermute x9, starting transfers between devices: 11.6 us -> 8.78 us  [swap_cores(): return lax.ppermute(value, 'c', [(0, 1), (1, 0)])]
    ppermute x3, waiting for transfers between devices: 15.5 us -> 17.8 us  [body(): chunk = lax.ppermute(chunk, 'zq', [(j, (j + k) % 4) for j in range(4)])]
    ppermute x3, starting transfers between devices: 9.42 us -> 7.25 us  [body(): chunk = lax.ppermute(chunk, 'zq', [(j, (j + k) % 4) for j in range(4)])]
  transfers between devices with their start and end apart: 27 -> 28, of which waited for: 13 -> 13; matrix products, arithmetic and copies ran while one was open for 3% -> 3% of each run, Pallas kernels for 3% -> 3%
where the time goes in v7:
time: 170 us; the launch traced here: 169 us
  waiting for transfers between devices  57.4 us (34%)
  starting transfers between devices  57.2 us (34%)
  blocking collectives  27.2 us (16%)
  Pallas kernels  15.3 us (9%)
  local copies, waits for them, and re-layouts  7.53 us (4%)
  other arithmetic  3 us (2%)
    all_to_all x1, blocking collectives, exchange(): return lax.all_to_all(value, axes, split_axis=0, concat_axis=0, tiled=True)  27.2 us
    all_to_all x2, waiting for transfers between devices, exchange(): return lax.all_to_all(value, axes, split_axis=0, concat_axis=0, tiled=True)  21.4 us
    ppermute x3, waiting for transfers between devices, body(): chunk = lax.ppermute(chunk, 'zq', [(j, (j + k) % 4) for j in range(4)])  17.8 us
    ppermute x3, waiting for transfers between devices, body(): block = lax.ppermute(block, ('zp', 'c'), [(j, j ^ k) for j in range(4)])  14.4 us
    ppermute x7, starting transfers between devices, shifted(): return lax.ppermute(value, Z, [(j, (j + by) % 8) for j in range(8)])  14.2 us
    all_to_all x2, starting transfers between devices, exchange(): return lax.all_to_all(value, axes, split_axis=0, concat_axis=0, tiled=True)  14 us
    ppermute x9, starting transfers between devices, swap_cores(): return lax.ppermute(value, 'c', [(0, 1), (1, 0)])  8.78 us
    ppermute x3, starting transfers between devices, body(): chunk = lax.ppermute(chunk, 'zq', [(j, (j + k) % 4) for j in range(4)])  7.25 us
  transfers between devices with their start and end apart: 28, of which 13 were waited for; matrix products, arithmetic and copies ran while one was open for 3% of the time, Pallas kernels for 3%

profile of v7, /device:TPU:1, one launch (start us, length us, event | category | flops | bytes accessed | tf_op | source)
XLA Modules:
  0.0 169.1 jit_solution(5667347053003857604)
XLA Ops:
  3.6 2.1 %pick.1 = (bf16[104,384]{1,0:T(8,128)(2,1)S(1)}, bf16[32,384]{1,0:T(8,128)(2,1)S(1)}) custom-call(s32[1,32]{1,0:T(1,128)S(1)} %copy-done.3, s32[1]{0:T(128)} %copy.33.count, s32[1,32]{1,0:T(1,128)} %targets.1, bf16[3,1024,384]{2,1,0:T(8,128)(2,1)S(1)} %copy-done, bf16[1024,384]{1,0:T(8,128)(2,1)} %final_far.1), custom_call_target="tpu_custom_call" | custom-call | tf_op jit(solution)/shard_map/pick/pallas_call | solution.py:249
  5.7 4.5 %collective-permute-start.15 = (bf16[32,384]{1,0:T(8,128)(2,1)S(1)}, bf16[32,384]{1,0:T(8,128)(2,1)S(1)}, u32[]{:S(2)}, u32[]{:S(2)}) collective-permute-start(bf16[32,384]{1,0:T(8,128)(2,1)S(1)} %get-tuple-element.9), channel_id=1, source_target_pairs={{0,0},{1,16},{2,32},{3,48},{4,64},{5,80},{6,96},{7,112},{8,128},{9... | collective-permute-start | bytes 73736 | tf_op jit(solution)/shard_map/ppermute | solution.py:267
  10.2 3.2 %collective-permute-start = (bf16[104,384]{1,0:T(8,128)(2,1)S(1)}, bf16[104,384]{1,0:T(8,128)(2,1)S(1)}, u32[]{:S(2)}, u32[]{:S(2)}) collective-permute-start(bf16[104,384]{1,0:T(8,128)(2,1)S(1)} %get-tuple-element.8.refs_0_), channel_id=1, source_target_pairs={{0,64},{32,96},{64,128},{96,160},{128,192},{160,224},{192,0},{224,... | collective-permute-start | bytes 239624 | tf_op jit(solution)/shard_map/ppermute | solution.py:39
  13.4 2.7 %collective-permute-start.1 = (bf16[104,384]{1,0:T(8,128)(2,1)S(1)}, bf16[104,384]{1,0:T(8,128)(2,1)S(1)}, u32[]{:S(2)}, u32[]{:S(2)}) collective-permute-start(bf16[104,384]{1,0:T(8,128)(2,1)S(1)} %get-tuple-element.8.refs_0_), channel_id=1, source_target_pairs={{0,192},{32,224},{64,0},{96,32},{128,64},{160,96},{192,128},{224,1... | collective-permute-start | bytes 239624 | tf_op jit(solution)/shard_map/ppermute | solution.py:39
  20.3 3.2 %collective-permute-start.4 = (bf16[104,384]{1,0:T(8,128)(2,1)S(1)}, bf16[104,384]{1,0:T(8,128)(2,1)S(1)}, u32[]{:S(2)}, u32[]{:S(2)}) collective-permute-start(bf16[104,384]{1,0:T(8,128)(2,1)S(1)} %collective-permute-done.refs_1_), channel_id=1, source_target_pairs={{0,32},{32,64},{64,96},{96,128},{128,160},{160,192},{192,224},{224... | collective-permute-start | bytes 239624 | tf_op jit(solution)/shard_map/ppermute | solution.py:39
  23.4 2.0 %collective-permute-start.6 = (bf16[104,384]{1,0:T(8,128)(2,1)S(1)}, bf16[104,384]{1,0:T(8,128)(2,1)S(1)}, u32[]{:S(2)}, u32[]{:S(2)}) collective-permute-start(bf16[104,384]{1,0:T(8,128)(2,1)S(1)} %collective-permute-done.refs_1_), channel_id=1, source_target_pairs={{0,64},{32,96},{64,128},{96,160},{128,192},{160,224},{192,0},{224,... | collective-permute-start | bytes 239624 | tf_op jit(solution)/shard_map/ppermute | solution.py:39
  32.8 2.8 %translate.1 = (bf16[16,4,16,384]{3,2,1,0:T(8,128)(2,1)}, f32[16,8,128]{2,1,0:T(8,128)}) custom-call(s32[6]{0:T(128)S(1)} %stack.46.flags, bf16[104,384]{1,0:T(8,128)(2,1)S(1)} %get-tuple-element.8.refs_0_, bf16[104,384]{1,0:T(8,128)(2,1)S(1)} %collective-permute-done.refs_1_, bf16[104,384]{1,0:T(8,128)(2,1)S(1)} %collective-permute-done.1.refs_2_, ...), custom_call_target="tpu_custom_call" | custom-call | tf_op jit(solution)/shard_map/translate/pallas_call | solution.py:273
  35.6 8.5 %all-to-all-start = ((bf16[16,64,384]{2,1,0:T(8,128)(2,1)}), bf16[16,64,384]{2,1,0:T(8,128)(2,1)S(1)}, u32[]{:S(2)}, u32[]{:S(2)}) async-start(bf16[16,64,384]{2,1,0:T(8,128)(2,1)} %bitcast.60), calls=%async_computation | async-start | bytes 1572864 | tf_op jit(solution)/shard_map/all_to_all | solution.py:35
  44.1 13.7 %all-to-all-done.parts = bf16[16,64,384]{2,1,0:T(8,128)(2,1)S(1)} async-done(((bf16[16,64,384]{2,1,0:T(8,128)(2,1)}), bf16[16,64,384]{2,1,0:T(8,128)(2,1)S(1)}, u32[]{:S(2)}, u32[]{:S(2)}) %all-to-all-start) | async-done | bytes 786464 | tf_op jit(solution)/shard_map/all_to_all | solution.py:35
  58.4 27.2 %all_to_all.15.y = bf16[32,72,384]{2,1,0:T(8,128)(2,1)S(1)} all-to-all(bf16[32,72,384]{2,1,0:T(8,128)(2,1)S(1)} %scale.1), channel_id=1, replica_groups=mesh['zq'=4,'zp'=2,'c'=2,'y'=4,'x'=4] {'zp','y','x'}, dimensions={0} | all-to-all | bytes 3538944 | tf_op jit(solution)/shard_map/all_to_all | solution.py:35
  85.6 2.9 %collective-permute-start.17 = (bf16[32,72,384]{2,1,0:T(8,128)(2,1)S(1)}, bf16[32,72,384]{2,1,0:T(8,128)(2,1)S(1)}, u32[]{:S(2)}, u32[]{:S(2)}) collective-permute-start(bf16[32,72,384]{2,1,0:T(8,128)(2,1)S(1)} %all_to_all.15.y), channel_id=1, source_target_pairs={{0,16},{16,0},{1,17},{17,1},{2,18},{18,2},{3,19},{19,3},{4,20},{20... | collective-permute-start | bytes 5308424 | tf_op jit(solution)/shard_map/ppermute | solution.py:43
  88.5 2.5 %dynamic-slice_bitcast_fusion = (bf16[512,384]{1,0:T(8,128)(2,1)}, bf16[512,384]{1,0:T(8,128)(2,1)}, bf16[512,384]{1,0:T(8,128)(2,1)}, bf16[512,384]{1,0:T(8,128)(2,1)}) fusion(bf16[4,512,384]{2,1,0:T(8,128)(2,1)} %bitcast.59, s32[]{:T(128)S(6)} %select_n.75, s32[]{:T(128)S(6)} %select_n.74, s32[]{:T(128)S(6)} %select_n.73, s32[]{:T(128)S(6)} %select_n.72), kind=kLoop, calls=%fused_computation.2 | loop fusion | bytes 3145744 | tf_op jit(solution)/shard_map/jit(dynamic_index_in_dim)/squeeze | solution.py:285
  92.9 9.1 %collective-permute-done.16.u_far = bf16[512,384]{1,0:T(8,128)(2,1)} collective-permute-done((bf16[512,384]{1,0:T(8,128)(2,1)}, bf16[512,384]{1,0:T(8,128)(2,1)}, u32[]{:S(2)}, u32[]{:S(2)}) %collective-permute-start.16) | collective-permute-done | bytes 393248 | tf_op jit(solution)/shard_map/ppermute | solution.py:287
  103.0 2.3 %own_logits.1.own_part = f32[4,264,512]{2,1,0:T(8,128)S(1)} custom-call(s32[6]{0:T(128)S(1)} %stack.46.flags, bf16[32,72,384]{2,1,0:T(8,128)(2,1)S(1)} %all_to_all.15.y, bf16[512,384]{1,0:T(8,128)(2,1)S(1)} %copy-done.1, bf16[512,384]{1,0:T(8,128)(2,1)} %collective-permute-done.16.u_far), custom_call_target="tpu_custom_call" | custom-call | tf_op jit(solution)/shard_map/own_logits/pallas_call | solution.py:305
  105.3 5.3 %collective-permute-done.19.u_far = bf16[512,384]{1,0:T(8,128)(2,1)} collective-permute-done((bf16[512,384]{1,0:T(8,128)(2,1)}, bf16[512,384]{1,0:T(8,128)(2,1)}, u32[]{:S(2)}, u32[]{:S(2)}) %collective-permute-start.19) | collective-permute-done | bytes 393248 | tf_op jit(solution)/shard_map/ppermute | solution.py:287
  114.5 3.5 %collective-permute-start.20 = (f16[264,512]{1,0:T(8,128)(2,1)S(1)}, f16[264,512]{1,0:T(8,128)(2,1)S(1)}, u32[]{:S(2)}, u32[]{:S(2)}) collective-permute-start(f16[264,512]{1,0:T(8,128)(2,1)S(1)} %convert_element_type.23), channel_id=1, source_target_pairs={{0,128},{64,192},{128,0},{192,64},{1,129},{65,193},{129,1},{193,65... | collective-permute-start | bytes 811016 | tf_op jit(solution)/shard_map/ppermute | solution.py:324
  121.9 3.1 %collective-permute-start.22 = (f16[264,512]{1,0:T(8,128)(2,1)S(1)}, f16[264,512]{1,0:T(8,128)(2,1)S(1)}, u32[]{:S(2)}, u32[]{:S(2)}) collective-permute-start(f16[264,512]{1,0:T(8,128)(2,1)S(1)} %convert_element_type.27), channel_id=1, source_target_pairs={{0,192},{64,0},{128,64},{192,128},{1,193},{65,1},{129,65},{193,129... | collective-permute-start | bytes 811016 | tf_op jit(solution)/shard_map/ppermute | solution.py:324
  125.4 6.4 %collective-permute-done.20 = f16[264,512]{1,0:T(8,128)(2,1)S(1)} collective-permute-done((f16[264,512]{1,0:T(8,128)(2,1)S(1)}, f16[264,512]{1,0:T(8,128)(2,1)S(1)}, u32[]{:S(2)}, u32[]{:S(2)}) %collective-permute-start.20) | collective-permute-done | bytes 270368 | tf_op jit(solution)/shard_map/ppermute | solution.py:324
  131.8 5.0 %collective-permute-done.21 = f16[264,512]{1,0:T(8,128)(2,1)S(1)} collective-permute-done((f16[264,512]{1,0:T(8,128)(2,1)S(1)}, f16[264,512]{1,0:T(8,128)(2,1)S(1)}, u32[]{:S(2)}, u32[]{:S(2)}) %collective-permute-start.21) | collective-permute-done | bytes 270368 | tf_op jit(solution)/shard_map/ppermute | solution.py:324
  136.9 6.4 %collective-permute-done.22 = f16[264,512]{1,0:T(8,128)(2,1)S(1)} collective-permute-done((f16[264,512]{1,0:T(8,128)(2,1)S(1)}, f16[264,512]{1,0:T(8,128)(2,1)S(1)}, u32[]{:S(2)}, u32[]{:S(2)}) %collective-permute-start.22) | collective-permute-done | bytes 270368 | tf_op jit(solution)/shard_map/ppermute | solution.py:324
  144.6 5.5 %all-to-all-start.2 = ((f32[64,8,128]{2,1,0:T(8,128)}), f32[64,8,128]{2,1,0:T(8,128)S(1)}, u32[]{:S(2)}, u32[]{:S(2)}) async-start(f32[64,8,128]{2,1,0:T(8,128)} %stats.1), calls=%async_computation.2 | async-start | bytes 524288 | tf_op jit(solution)/shard_map/all_to_all | solution.py:35
  151.5 7.8 %all-to-all-done.2 = f32[64,8,128]{2,1,0:T(8,128)S(1)} async-done(((f32[64,8,128]{2,1,0:T(8,128)}), f32[64,8,128]{2,1,0:T(8,128)S(1)}, u32[]{:S(2)}, u32[]{:S(2)}) %all-to-all-start.2) | async-done | bytes 262176 | tf_op jit(solution)/shard_map/all_to_all | solution.py:35
  161.0 2.7 %collective-permute-start.24 = (f32[8,128]{1,0:T(8,128)S(1)}, f32[8,128]{1,0:T(8,128)S(1)}, u32[]{:S(2)}, u32[]{:S(2)}) collective-permute-start(f32[8,128]{1,0:T(8,128)S(1)} %reduce_sum.48), channel_id=1, source_target_pairs={{0,128},{64,192},{128,0},{192,64},{1,129},{65,193},{129,1},{193,65... | collective-permute-start | bytes 12296 | tf_op jit(solution)/shard_map/ppermute | solution.py:355
  163.7 2.3 %collective-permute-start.25 = (f32[8,128]{1,0:T(8,128)S(1)}, f32[8,128]{1,0:T(8,128)S(1)}, u32[]{:S(2)}, u32[]{:S(2)}) collective-permute-start(f32[8,128]{1,0:T(8,128)S(1)} %reduce_sum.48), channel_id=1, source_target_pairs={{0,192},{64,0},{128,64},{192,128},{1,193},{65,1},{129,65},{193,129... | collective-permute-start | bytes 12296 | tf_op jit(solution)/shard_map/ppermute | solution.py:355
  (94 shorter events, 32.9 us)
Async XLA Ops:
  5.7 13.1 %collective-permute-start.15 = (bf16[32,384]{1,0:T(8,128)(2,1)S(1)}, bf16[32,384]{1,0:T(8,128)(2,1)S(1)}, u32[]{:S(2)}, u32[]{:S(2)}) collective-permute-start(bf16[32,384]{1,0:T(8,128)(2,1)S(1)} %get-tuple-element.9), channel_id=1, source_target_pairs={{0,0},{1,16},{2,32},{3,48},{4,64},{5,80},{6,96},{7,112},{8,128},{9... | collective-permute-start | bytes 73736 | tf_op jit(solution)/shard_map/ppermute | solution.py:267
  10.2 10.1 %collective-permute-start = (bf16[104,384]{1,0:T(8,128)(2,1)S(1)}, bf16[104,384]{1,0:T(8,128)(2,1)S(1)}, u32[]{:S(2)}, u32[]{:S(2)}) collective-permute-start(bf16[104,384]{1,0:T(8,128)(2,1)S(1)} %get-tuple-element.8.refs_0_), channel_id=1, source_target_pairs={{0,64},{32,96},{64,128},{96,160},{128,192},{160,224},{192,0},{224,... | collective-permute-start | bytes 239624 | tf_op jit(solution)/shard_map/ppermute | solution.py:39
  13.4 10.1 %collective-permute-start.1 = (bf16[104,384]{1,0:T(8,128)(2,1)S(1)}, bf16[104,384]{1,0:T(8,128)(2,1)S(1)}, u32[]{:S(2)}, u32[]{:S(2)}) collective-permute-start(bf16[104,384]{1,0:T(8,128)(2,1)S(1)} %get-tuple-element.8.refs_0_), channel_id=1, source_target_pairs={{0,192},{32,224},{64,0},{96,32},{128,64},{160,96},{192,128},{224,1... | collective-permute-start | bytes 239624 | tf_op jit(solution)/shard_map/ppermute | solution.py:39
  16.1 9.4 %collective-permute-start.2 = (bf16[104,384]{1,0:T(8,128)(2,1)S(1)}, bf16[104,384]{1,0:T(8,128)(2,1)S(1)}, u32[]{:S(2)}, u32[]{:S(2)}) collective-permute-start(bf16[104,384]{1,0:T(8,128)(2,1)S(1)} %get-tuple-element.8.refs_0_), channel_id=1, source_target_pairs={{0,32},{32,64},{64,96},{96,128},{128,160},{160,192},{192,224},{224... | collective-permute-start | bytes 239624 | tf_op jit(solution)/shard_map/ppermute | solution.py:39
  17.7 8.2 %collective-permute-start.3 = (bf16[104,384]{1,0:T(8,128)(2,1)S(1)}, bf16[104,384]{1,0:T(8,128)(2,1)S(1)}, u32[]{:S(2)}, u32[]{:S(2)}) collective-permute-start(bf16[104,384]{1,0:T(8,128)(2,1)S(1)} %get-tuple-element.8.refs_0_), channel_id=1, source_target_pairs={{0,224},{32,0},{64,32},{96,64},{128,96},{160,128},{192,160},{224,1... | collective-permute-start | bytes 239624 | tf_op jit(solution)/shard_map/ppermute | solution.py:39
  18.8 8.2 %collective-permute-start.7 = (bf16[104,384]{1,0:T(8,128)(2,1)S(1)}, bf16[104,384]{1,0:T(8,128)(2,1)S(1)}, u32[]{:S(2)}, u32[]{:S(2)}) collective-permute-start(bf16[104,384]{1,0:T(8,128)(2,1)S(1)} %get-tuple-element.8.refs_0_), channel_id=1, source_target_pairs={{0,16},{16,0},{1,17},{17,1},{2,18},{18,2},{3,19},{19,3},{4,20},{20... | collective-permute-start | bytes 239624 | tf_op jit(solution)/shard_map/ppermute | solution.py:43
  20.3 6.8 %collective-permute-start.4 = (bf16[104,384]{1,0:T(8,128)(2,1)S(1)}, bf16[104,384]{1,0:T(8,128)(2,1)S(1)}, u32[]{:S(2)}, u32[]{:S(2)}) collective-permute-start(bf16[104,384]{1,0:T(8,128)(2,1)S(1)} %collective-permute-done.refs_1_), channel_id=1, source_target_pairs={{0,32},{32,64},{64,96},{96,128},{128,160},{160,192},{192,224},{224... | collective-permute-start | bytes 239624 | tf_op jit(solution)/shard_map/ppermute | solution.py:39
  23.4 5.6 %collective-permute-start.6 = (bf16[104,384]{1,0:T(8,128)(2,1)S(1)}, bf16[104,384]{1,0:T(8,128)(2,1)S(1)}, u32[]{:S(2)}, u32[]{:S(2)}) collective-permute-start(bf16[104,384]{1,0:T(8,128)(2,1)S(1)} %collective-permute-done.refs_1_), channel_id=1, source_target_pairs={{0,64},{32,96},{64,128},{96,160},{128,192},{160,224},{192,0},{224,... | collective-permute-start | bytes 239624 | tf_op jit(solution)/shard_map/ppermute | solution.py:39
  25.5 5.5 %collective-permute-start.5 = (bf16[104,384]{1,0:T(8,128)(2,1)S(1)}, bf16[104,384]{1,0:T(8,128)(2,1)S(1)}, u32[]{:S(2)}, u32[]{:S(2)}) collective-permute-start(bf16[104,384]{1,0:T(8,128)(2,1)S(1)} %collective-permute-done.1.refs_2_), channel_id=1, source_target_pairs={{0,224},{32,0},{64,32},{96,64},{128,96},{160,128},{192,160},{224,1... | collective-permute-start | bytes 239624 | tf_op jit(solution)/shard_map/ppermute | solution.py:39
  25.8 5.2 %collective-permute-start.8 = (bf16[104,384]{1,0:T(8,128)(2,1)S(1)}, bf16[104,384]{1,0:T(8,128)(2,1)S(1)}, u32[]{:S(2)}, u32[]{:S(2)}) collective-permute-start(bf16[104,384]{1,0:T(8,128)(2,1)S(1)} %collective-permute-done.refs_1_), channel_id=1, source_target_pairs={{0,16},{16,0},{1,17},{17,1},{2,18},{18,2},{3,19},{19,3},{4,20},{20... | collective-permute-start | bytes 239624 | tf_op jit(solution)/shard_map/ppermute | solution.py:43
  27.0 4.6 %collective-permute-start.9 = (bf16[104,384]{1,0:T(8,128)(2,1)S(1)}, bf16[104,384]{1,0:T(8,128)(2,1)S(1)}, u32[]{:S(2)}, u32[]{:S(2)}) collective-permute-start(bf16[104,384]{1,0:T(8,128)(2,1)S(1)} %collective-permute-done.1.refs_2_), channel_id=1, source_target_pairs={{0,16},{16,0},{1,17},{17,1},{2,18},{18,2},{3,19},{19,3},{4,20},{20... | collective-permute-start | bytes 239624 | tf_op jit(solution)/shard_map/ppermute | solution.py:43
  27.1 4.6 %collective-permute-start.10 = (bf16[104,384]{1,0:T(8,128)(2,1)S(1)}, bf16[104,384]{1,0:T(8,128)(2,1)S(1)}, u32[]{:S(2)}, u32[]{:S(2)}) collective-permute-start(bf16[104,384]{1,0:T(8,128)(2,1)S(1)} %collective-permute-done.2.refs_3_), channel_id=1, source_target_pairs={{0,16},{16,0},{1,17},{17,1},{2,18},{18,2},{3,19},{19,3},{4,20},{20... | collective-permute-start | bytes 239624 | tf_op jit(solution)/shard_map/ppermute | solution.py:43
  35.6 22.2 %all-to-all-start = ((bf16[16,64,384]{2,1,0:T(8,128)(2,1)}), bf16[16,64,384]{2,1,0:T(8,128)(2,1)S(1)}, u32[]{:S(2)}, u32[]{:S(2)}) async-start(bf16[16,64,384]{2,1,0:T(8,128)(2,1)} %bitcast.60), calls=%async_computation | async-start | bytes 1572864 | tf_op jit(solution)/shard_map/all_to_all | solution.py:35
  85.6 25.0 %collective-permute-start.17 = (bf16[32,72,384]{2,1,0:T(8,128)(2,1)S(1)}, bf16[32,72,384]{2,1,0:T(8,128)(2,1)S(1)}, u32[]{:S(2)}, u32[]{:S(2)}) collective-permute-start(bf16[32,72,384]{2,1,0:T(8,128)(2,1)S(1)} %all_to_all.15.y), channel_id=1, source_target_pairs={{0,16},{16,0},{1,17},{17,1},{2,18},{18,2},{3,19},{19,3},{4,20},{20... | collective-permute-start | bytes 5308424 | tf_op jit(solution)/shard_map/ppermute | solution.py:43
  91.0 11.0 %collective-permute-start.16 = (bf16[512,384]{1,0:T(8,128)(2,1)}, bf16[512,384]{1,0:T(8,128)(2,1)}, u32[]{:S(2)}, u32[]{:S(2)}) collective-permute-start(bf16[512,384]{1,0:T(8,128)(2,1)} %get-tuple-element.24), channel_id=1, source_target_pairs={{0,32},{16,48},{32,0},{48,16},{1,33},{17,49},{33,1},{49,17},{2,34}... | collective-permute-start | bytes 1179656 | tf_op jit(solution)/shard_map/ppermute | solution.py:287
  91.6 13.7 %collective-permute-start.18 = (bf16[512,384]{1,0:T(8,128)(2,1)}, bf16[512,384]{1,0:T(8,128)(2,1)}, u32[]{:S(2)}, u32[]{:S(2)}) collective-permute-start(bf16[512,384]{1,0:T(8,128)(2,1)} %get-tuple-element.23), channel_id=1, source_target_pairs={{0,16},{16,0},{32,48},{48,32},{1,17},{17,1},{33,49},{49,33},{2,18}... | collective-permute-start | bytes 1179656 | tf_op jit(solution)/shard_map/ppermute | solution.py:287
  91.9 18.8 %collective-permute-start.19 = (bf16[512,384]{1,0:T(8,128)(2,1)}, bf16[512,384]{1,0:T(8,128)(2,1)}, u32[]{:S(2)}, u32[]{:S(2)}) collective-permute-start(bf16[512,384]{1,0:T(8,128)(2,1)} %get-tuple-element.22), channel_id=1, source_target_pairs={{0,48},{16,32},{32,16},{48,0},{1,49},{17,33},{33,17},{49,1},{2,50}... | collective-permute-start | bytes 1179656 | tf_op jit(solution)/shard_map/ppermute | solution.py:287
  114.5 17.3 %collective-permute-start.20 = (f16[264,512]{1,0:T(8,128)(2,1)S(1)}, f16[264,512]{1,0:T(8,128)(2,1)S(1)}, u32[]{:S(2)}, u32[]{:S(2)}) collective-permute-start(f16[264,512]{1,0:T(8,128)(2,1)S(1)} %convert_element_type.23), channel_id=1, source_target_pairs={{0,128},{64,192},{128,0},{192,64},{1,129},{65,193},{129,1},{193,65... | collective-permute-start | bytes 811016 | tf_op jit(solution)/shard_map/ppermute | solution.py:324
  119.6 17.2 %collective-permute-start.21 = (f16[264,512]{1,0:T(8,128)(2,1)S(1)}, f16[264,512]{1,0:T(8,128)(2,1)S(1)}, u32[]{:S(2)}, u32[]{:S(2)}) collective-permute-start(f16[264,512]{1,0:T(8,128)(2,1)S(1)} %convert_element_type.25), channel_id=1, source_target_pairs={{0,64},{64,128},{128,192},{192,0},{1,65},{65,129},{129,193},{193,1... | collective-permute-start | bytes 811016 | tf_op jit(solution)/shard_map/ppermute | solution.py:324
  121.9 21.3 %collective-permute-start.22 = (f16[264,512]{1,0:T(8,128)(2,1)S(1)}, f16[264,512]{1,0:T(8,128)(2,1)S(1)}, u32[]{:S(2)}, u32[]{:S(2)}) collective-permute-start(f16[264,512]{1,0:T(8,128)(2,1)S(1)} %convert_element_type.27), channel_id=1, source_target_pairs={{0,192},{64,0},{128,64},{192,128},{1,193},{65,1},{129,65},{193,129... | collective-permute-start | bytes 811016 | tf_op jit(solution)/shard_map/ppermute | solution.py:324
  144.6 14.7 %all-to-all-start.2 = ((f32[64,8,128]{2,1,0:T(8,128)}), f32[64,8,128]{2,1,0:T(8,128)S(1)}, u32[]{:S(2)}, u32[]{:S(2)}) async-start(f32[64,8,128]{2,1,0:T(8,128)} %stats.1), calls=%async_computation.2 | async-start | bytes 524288 | tf_op jit(solution)/shard_map/all_to_all | solution.py:35
  159.4 6.7 %collective-permute-start.23 = (f32[8,128]{1,0:T(8,128)S(1)}, f32[8,128]{1,0:T(8,128)S(1)}, u32[]{:S(2)}, u32[]{:S(2)}) collective-permute-start(f32[8,128]{1,0:T(8,128)S(1)} %reduce_sum.48), channel_id=1, source_target_pairs={{0,64},{64,128},{128,192},{192,0},{1,65},{65,129},{129,193},{193,1... | collective-permute-start | bytes 12296 | tf_op jit(solution)/shard_map/ppermute | solution.py:355
  161.0 6.4 %collective-permute-start.24 = (f32[8,128]{1,0:T(8,128)S(1)}, f32[8,128]{1,0:T(8,128)S(1)}, u32[]{:S(2)}, u32[]{:S(2)}) collective-permute-start(f32[8,128]{1,0:T(8,128)S(1)} %reduce_sum.48), channel_id=1, source_target_pairs={{0,128},{64,192},{128,0},{192,64},{1,129},{65,193},{129,1},{193,65... | collective-permute-start | bytes 12296 | tf_op jit(solution)/shard_map/ppermute | solution.py:355
  163.7 3.7 %collective-permute-start.25 = (f32[8,128]{1,0:T(8,128)S(1)}, f32[8,128]{1,0:T(8,128)S(1)}, u32[]{:S(2)}, u32[]{:S(2)}) collective-permute-start(f32[8,128]{1,0:T(8,128)S(1)} %reduce_sum.48), channel_id=1, source_target_pairs={{0,192},{64,0},{128,64},{192,128},{1,193},{65,1},{129,65},{193,129... | collective-permute-start | bytes 12296 | tf_op jit(solution)/shard_map/ppermute | solution.py:355
  (11 other events, 71.1 us)

commit v8 on v6

--- a/solution.py
+++ b/solution.py
@@ -64,25 +64,21 @@
 LIMIT = pltpu.CompilerParams(vmem_limit_bytes=24 * 1024 * 1024)
 
 
-def pick_kernel(picks, count, targets, probe, final_far, out, rows, final, arrived):
-    fetch = pltpu.make_async_copy(final_far, final, arrived)
-    fetch.start()
+def pick_kernel(picks, count, targets, probe_far, final_far, out, rows, probe, final, arrived):
+    copies = [pltpu.make_async_copy(probe_far.at[k], probe.at[k], arrived.at[k]) for k in range(LAYERS)]
+    copies.append(pltpu.make_async_copy(final_far, final, arrived.at[LAYERS]))
+    for copy in copies:
+        copy.start()
     sub = lax.broadcasted_iota(jnp.int32, (16, out.shape[1]), 0)
-
-    def take(layer, k):
-        pick = jnp.clip(picks[0, k], 0, final.shape[0] - 1)
-        within = lax.rem(pick, 16)
-        group = pl.ds(pl.multiple_of(pick - within, 16), 16)
-        block = probe[layer, group, :] if layer < LAYERS else final[group, :]
-        row = jnp.sum(jnp.where(sub == within, block.astype(F32), 0.0), axis=0, keepdims=True)
-        rows[layer * CAP + k : layer * CAP + k + 1, :] = row
-
-    for k in range(CAP):
-        for layer in range(LAYERS):
-            take(layer, k)
-    fetch.wait()
-    for k in range(CAP):
-        take(LAYERS, k)
+    for layer in range(LAYERS + 1):
+        copies[layer].wait()
+        for k in range(CAP):
+            pick = jnp.clip(picks[0, k], 0, final.shape[0] - 1)
+            within = lax.rem(pick, 16)
+            group = pl.ds(pl.multiple_of(pick - within, 16), 16)
+            block = probe[layer, group, :] if layer < LAYERS else final[group, :]
+            row = jnp.sum(jnp.where(sub == within, block.astype(F32), 0.0), axis=0, keepdims=True)
+            rows[layer * CAP + k : layer * CAP + k + 1, :] = row
     out[0:INFO] = rows[...].astype(BF16)
     out[INFO : INFO + 8] = jnp.zeros((8, out.shape[1]), BF16)
     line = lax.broadcasted_iota(jnp.int32, (8, CAP), 0)
@@ -214,9 +210,7 @@
     for h in range(2):
         for k, value in enumerate((total, cross, picked)):
             table = jnp.where(lane == 3 * h + k, value[128 * h : 128 * h + 128], table)
-    rows = table.T[:8]
-    for k in range(64):
-        out[k] = rows
+    out[...] = table.T[:8]
 
 
 def body(
@@ -241,16 +235,17 @@
     local = pl.pallas_call(
         pick_kernel,
         out_shape=whole((INFO + 8, width), BF16),
-        in_specs=[SCALARS] * 2 + [VECTORS] * 2 + [pl.BlockSpec(memory_space=pltpu.HBM)],
+        in_specs=[SCALARS] * 2 + [VECTORS] + [pl.BlockSpec(memory_space=pltpu.HBM)] * 2,
         out_specs=VECTORS,
         scratch_shapes=[
             pltpu.VMEM((INFO, width), F32),
+            pltpu.VMEM(probe_states.shape, BF16),
             pltpu.VMEM(final_states.shape, BF16),
-            pltpu.SemaphoreType.DMA(()),
+            pltpu.SemaphoreType.DMA((LAYERS + 1,)),
         ],
         compiler_params=LIMIT,
         name="pick",
-    )(answer_rows, answer_count, held(targets), near(probe_states), held(final_states))
+    )(answer_rows, answer_count, held(targets), held(probe_states), held(final_states))
     back2, fore2, back1, fore1 = [shifted(local, by) for by in (2, -2, 1, -1)]
     own = [local, back2, fore2, back1, fore1]
     other = [swap_cores(chunk) for chunk in own]
@@ -290,7 +285,7 @@
     y_other = swap_cores(y_own)
 
     quarters = [near(block) for block in quarters]
-    y_own, y_other = near(y_own), near(y_other)
+    y_own, y_other = held(y_own), near(y_other)
     own_part = pl.pallas_call(
         own_kernel,
         out_shape=whole((4, 264, part), F32),
@@ -332,13 +327,14 @@
     item_targets = jnp.broadcast_to(local_targets.reshape(4, 1, 16), (4, 4, 16)).reshape(256, 1)
     stats = pl.pallas_call(
         stats_kernel,
-        out_shape=far((64, 8, 128), F32),
+        out_shape=whole((8, 128), F32),
         in_specs=[VECTORS] * 2,
         out_specs=VECTORS,
         compiler_params=LIMIT,
         name="stats",
     )(near(summed), item_targets)
-    sums = jnp.sum(exchange(stats, ("zp", "c", *VOCAB)), axis=0)
+    stats = stats + swap_cores(stats)
+    sums = jnp.sum(exchange(jnp.broadcast_to(stats[None], (32, 8, 128)), ("zp", *VOCAB)), axis=0)
     every = [sums]
     for k in (1, 2, 3):
         every.append(lax.ppermute(sums, "zq", [(j, (j + k) % 4) for j in range(4)]))

time: 167 us -> 166 us (level)
  other arithmetic: 3 us -> 5.39 us
  local copies, waits for them, and re-layouts: 7.53 us -> 5.45 us
  Pallas kernels: 15.3 us -> 13.4 us
    unnamed x15 -> x11, local copies, waits for them, and re-layouts: 3.89 us -> 1.23 us
    pallas_call x4, Pallas kernels: 6.36 us -> 4.03 us  [body(): pl.pallas_call(functools.partial(chunk_kernel, k), out_shape=whole((264,...]
    ppermute x9 -> x10, starting transfers between devices: 11.6 us -> 12.7 us  [swap_cores(): return lax.ppermute(value, 'c', [(0, 1), (1, 0)])]
  transfers between devices with their start and end apart: 27 -> 28, of which waited for: 13 -> 14; matrix products, arithmetic and copies ran while one was open for 3% -> 3% of each run, Pallas kernels for 3% -> 3%
where the time goes in v8:
time: 166 us; the launch traced here: 165 us
  waiting for transfers between devices  57.3 us (35%)
  starting transfers between devices  55.7 us (34%)
  blocking collectives  26.3 us (16%)
  Pallas kernels  13.4 us (8%)
  local copies, waits for them, and re-layouts  5.45 us (3%)
  other arithmetic  5.39 us (3%)
    all_to_all x1, blocking collectives, exchange(): return lax.all_to_all(value, axes, split_axis=0, concat_axis=0, tiled=True)  26.3 us
    all_to_all x2, waiting for transfers between devices, exchange(): return lax.all_to_all(value, axes, split_axis=0, concat_axis=0, tiled=True)  19.8 us
    ppermute x3, waiting for transfers between devices, body(): chunk = lax.ppermute(chunk, 'zq', [(j, (j + k) % 4) for j in range(4)])  16.3 us
    ppermute x3, waiting for transfers between devices, body(): block = lax.ppermute(block, ('zp', 'c'), [(j, j ^ k) for j in range(4)])  14.8 us
    ppermute x7, starting transfers between devices, shifted(): return lax.ppermute(value, Z, [(j, (j + by) % 8) for j in range(8)])  13.5 us
    all_to_all x2, starting transfers between devices, exchange(): return lax.all_to_all(value, axes, split_axis=0, concat_axis=0, tiled=True)  12.9 us
    ppermute x10, starting transfers between devices, swap_cores(): return lax.ppermute(value, 'c', [(0, 1), (1, 0)])  12.7 us
    ppermute x3, starting transfers between devices, body(): chunk = lax.ppermute(chunk, 'zq', [(j, (j + k) % 4) for j in range(4)])  9.16 us
  transfers between devices with their start and end apart: 28, of which 14 were waited for; matrix products, arithmetic and copies ran while one was open for 3% of the time, Pallas kernels for 3%

profile of v8, /device:TPU:1, one launch (start us, length us, event | category | flops | bytes accessed | tf_op | source)
XLA Modules:
  0.0 165.2 jit_solution(14537832763283423923)
XLA Ops:
  2.0 2.7 %pick.1.refs_0_ = bf16[136,384]{1,0:T(8,128)(2,1)S(1)} custom-call(s32[1,32]{1,0:T(1,128)S(1)} %copy-done.1, s32[1]{0:T(128)} %copy.31.count, s32[1,32]{1,0:T(1,128)} %targets.1, bf16[3,1024,384]{2,1,0:T(8,128)(2,1)} %probe_far.1, bf16[1024,384]{1,0:T(8,128)(2,1)} %final_far.1), custom_call_target="tpu_custom_call" | custom-call | tf_op jit(solution)/shard_map/pick/pallas_call | solution.py:235
  4.8 3.9 %collective-permute-start = (bf16[136,384]{1,0:T(8,128)(2,1)S(1)}, bf16[136,384]{1,0:T(8,128)(2,1)S(1)}, u32[]{:S(2)}, u32[]{:S(2)}) collective-permute-start(bf16[136,384]{1,0:T(8,128)(2,1)S(1)} %pick.1.refs_0_), channel_id=1, source_target_pairs={{0,64},{32,96},{64,128},{96,160},{128,192},{160,224},{192,0},{224,... | collective-permute-start | bytes 313352 | tf_op jit(solution)/shard_map/ppermute | solution.py:39
  8.7 3.1 %collective-permute-start.1 = (bf16[136,384]{1,0:T(8,128)(2,1)S(1)}, bf16[136,384]{1,0:T(8,128)(2,1)S(1)}, u32[]{:S(2)}, u32[]{:S(2)}) collective-permute-start(bf16[136,384]{1,0:T(8,128)(2,1)S(1)} %pick.1.refs_0_), channel_id=1, source_target_pairs={{0,192},{32,224},{64,0},{96,32},{128,64},{160,96},{192,128},{224,1... | collective-permute-start | bytes 313352 | tf_op jit(solution)/shard_map/ppermute | solution.py:39
  18.1 2.2 %collective-permute-start.6 = (bf16[136,384]{1,0:T(8,128)(2,1)S(1)}, bf16[136,384]{1,0:T(8,128)(2,1)S(1)}, u32[]{:S(2)}, u32[]{:S(2)}) collective-permute-start(bf16[136,384]{1,0:T(8,128)(2,1)S(1)} %collective-permute-done.refs_1_), channel_id=1, source_target_pairs={{0,64},{32,96},{64,128},{96,160},{128,192},{160,224},{192,0},{224,... | collective-permute-start | bytes 313352 | tf_op jit(solution)/shard_map/ppermute | solution.py:39
  20.3 3.4 %collective-permute-start.8 = (bf16[136,384]{1,0:T(8,128)(2,1)S(1)}, bf16[136,384]{1,0:T(8,128)(2,1)S(1)}, u32[]{:S(2)}, u32[]{:S(2)}) collective-permute-start(bf16[136,384]{1,0:T(8,128)(2,1)S(1)} %collective-permute-done.refs_1_), channel_id=1, source_target_pairs={{0,16},{16,0},{1,17},{17,1},{2,18},{18,2},{3,19},{19,3},{4,20},{20... | collective-permute-start | bytes 313352 | tf_op jit(solution)/shard_map/ppermute | solution.py:43
  29.8 2.9 %translate.1 = (bf16[16,4,16,384]{3,2,1,0:T(8,128)(2,1)}, f32[16,8,128]{2,1,0:T(8,128)}) custom-call(s32[5]{0:T(128)S(1)} %stack.42.flags, bf16[136,384]{1,0:T(8,128)(2,1)S(1)} %pick.1.refs_0_, bf16[136,384]{1,0:T(8,128)(2,1)S(1)} %collective-permute-done.refs_1_, bf16[136,384]{1,0:T(8,128)(2,1)S(1)} %collective-permute-done.1.refs_2_, ...), custom_call_target="tpu_custom_call" | custom-call | tf_op jit(solution)/shard_map/translate/pallas_call | solution.py:257
  32.7 6.8 %all-to-all-start = ((bf16[16,64,384]{2,1,0:T(8,128)(2,1)}), bf16[16,64,384]{2,1,0:T(8,128)(2,1)S(1)}, u32[]{:S(2)}, u32[]{:S(2)}) async-start(bf16[16,64,384]{2,1,0:T(8,128)(2,1)} %bitcast.53), calls=%async_computation | async-start | bytes 1572864 | tf_op jit(solution)/shard_map/all_to_all | solution.py:35
  39.5 13.5 %all-to-all-done.parts = bf16[16,64,384]{2,1,0:T(8,128)(2,1)S(1)} async-done(((bf16[16,64,384]{2,1,0:T(8,128)(2,1)}), bf16[16,64,384]{2,1,0:T(8,128)(2,1)S(1)}, u32[]{:S(2)}, u32[]{:S(2)}) %all-to-all-start) | async-done | bytes 786464 | tf_op jit(solution)/shard_map/all_to_all | solution.py:35
  53.6 26.3 %all_to_all.15.y = bf16[32,72,384]{2,1,0:T(8,128)(2,1)} all-to-all(bf16[32,72,384]{2,1,0:T(8,128)(2,1)S(1)} %scale.1), channel_id=1, replica_groups=mesh['zq'=4,'zp'=2,'c'=2,'y'=4,'x'=4] {'zp','y','x'}, dimensions={0} | all-to-all | bytes 3538944 | tf_op jit(solution)/shard_map/all_to_all | solution.py:35
  79.9 3.4 %collective-permute-start.16 = (bf16[32,72,384]{2,1,0:T(8,128)(2,1)}, bf16[32,72,384]{2,1,0:T(8,128)(2,1)S(1)}, u32[]{:S(2)}, u32[]{:S(2)}) collective-permute-start(bf16[32,72,384]{2,1,0:T(8,128)(2,1)} %all_to_all.15.y), channel_id=1, source_target_pairs={{0,16},{16,0},{1,17},{17,1},{2,18},{18,2},{3,19},{19,3},{4,20},{20... | collective-permute-start | bytes 5308424 | tf_op jit(solution)/shard_map/ppermute | solution.py:43
  83.3 2.4 %dynamic-slice_bitcast_fusion = (bf16[512,384]{1,0:T(8,128)(2,1)}, bf16[512,384]{1,0:T(8,128)(2,1)}, bf16[512,384]{1,0:T(8,128)(2,1)}, bf16[512,384]{1,0:T(8,128)(2,1)S(1)}) fusion(bf16[4,512,384]{2,1,0:T(8,128)(2,1)} %bitcast.52, s32[]{:T(128)S(6)} %select_n.75, s32[]{:T(128)S(6)} %select_n.74, s32[]{:T(128)S(6)} %select_n.73, s32[]{:T(128)S(6)} %select_n.72), kind=kLoop, calls=%fused_computation.2 | loop fusion | bytes 3145744 | tf_op jit(solution)/shard_map/jit(dynamic_index_in_dim)/squeeze | solution.py:269
  87.6 9.0 %collective-permute-done.15.u_far = bf16[512,384]{1,0:T(8,128)(2,1)S(1)} collective-permute-done((bf16[512,384]{1,0:T(8,128)(2,1)}, bf16[512,384]{1,0:T(8,128)(2,1)S(1)}, u32[]{:S(2)}, u32[]{:S(2)}) %collective-permute-start.15) | collective-permute-done | bytes 393248 | tf_op jit(solution)/shard_map/ppermute | solution.py:271
  96.6 2.8 %own_logits.1.own_part = f32[4,264,512]{2,1,0:T(8,128)S(1)} custom-call(s32[5]{0:T(128)S(1)} %stack.42.flags, bf16[32,72,384]{2,1,0:T(8,128)(2,1)} %all_to_all.15.y, bf16[512,384]{1,0:T(8,128)(2,1)S(1)} %get-tuple-element.21.u_near, bf16[512,384]{1,0:T(8,128)(2,1)S(1)} %collective-permute-done.15.u_far), custom_call_target="tpu_custom_call" | custom-call | tf_op jit(solution)/shard_map/own_logits/pallas_call | solution.py:289
  99.4 5.8 %collective-permute-done.18.u_far = bf16[512,384]{1,0:T(8,128)(2,1)S(1)} collective-permute-done((bf16[512,384]{1,0:T(8,128)(2,1)}, bf16[512,384]{1,0:T(8,128)(2,1)S(1)}, u32[]{:S(2)}, u32[]{:S(2)}) %collective-permute-start.18) | collective-permute-done | bytes 393248 | tf_op jit(solution)/shard_map/ppermute | solution.py:271
  108.6 5.5 %collective-permute-start.19 = (f16[264,512]{1,0:T(8,128)(2,1)}, f16[264,512]{1,0:T(8,128)(2,1)}, u32[]{:S(2)}, u32[]{:S(2)}) collective-permute-start(f16[264,512]{1,0:T(8,128)(2,1)} %convert_element_type.23), channel_id=1, source_target_pairs={{0,128},{64,192},{128,0},{192,64},{1,129},{65,193},{129,1},{193,65... | collective-permute-start | bytes 811016 | tf_op jit(solution)/shard_map/ppermute | solution.py:308
  116.9 3.6 %collective-permute-start.21 = (f16[264,512]{1,0:T(8,128)(2,1)S(1)}, f16[264,512]{1,0:T(8,128)(2,1)S(1)}, u32[]{:S(2)}, u32[]{:S(2)}) collective-permute-start(f16[264,512]{1,0:T(8,128)(2,1)S(1)} %convert_element_type.27), channel_id=1, source_target_pairs={{0,192},{64,0},{128,64},{192,128},{1,193},{65,1},{129,65},{193,129... | collective-permute-start | bytes 811016 | tf_op jit(solution)/shard_map/ppermute | solution.py:308
  121.0 5.9 %collective-permute-done.19 = f16[264,512]{1,0:T(8,128)(2,1)} collective-permute-done((f16[264,512]{1,0:T(8,128)(2,1)}, f16[264,512]{1,0:T(8,128)(2,1)}, u32[]{:S(2)}, u32[]{:S(2)}) %collective-permute-start.19) | collective-permute-done | bytes 270368 | tf_op jit(solution)/shard_map/ppermute | solution.py:308
  126.9 6.2 %collective-permute-done.20 = f16[264,512]{1,0:T(8,128)(2,1)} collective-permute-done((f16[264,512]{1,0:T(8,128)(2,1)}, f16[264,512]{1,0:T(8,128)(2,1)}, u32[]{:S(2)}, u32[]{:S(2)}) %collective-permute-start.20) | collective-permute-done | bytes 270368 | tf_op jit(solution)/shard_map/ppermute | solution.py:308
  133.1 4.2 %collective-permute-done.21 = f16[264,512]{1,0:T(8,128)(2,1)S(1)} collective-permute-done((f16[264,512]{1,0:T(8,128)(2,1)S(1)}, f16[264,512]{1,0:T(8,128)(2,1)S(1)}, u32[]{:S(2)}, u32[]{:S(2)}) %collective-permute-start.21) | collective-permute-done | bytes 270368 | tf_op jit(solution)/shard_map/ppermute | solution.py:308
  141.1 6.2 %all-to-all-start.2 = ((f32[32,8,128]{2,1,0:T(8,128)}), f32[32,8,128]{2,1,0:T(8,128)S(1)}, u32[]{:S(2)}, u32[]{:S(2)}) async-start(f32[32,8,128]{2,1,0:T(8,128)} %broadcast_in_dim.128), calls=%async_computation.2 | async-start | bytes 262144 | tf_op jit(solution)/shard_map/all_to_all | solution.py:35
  148.6 6.3 %all-to-all-done.2 = f32[32,8,128]{2,1,0:T(8,128)S(1)} async-done(((f32[32,8,128]{2,1,0:T(8,128)}), f32[32,8,128]{2,1,0:T(8,128)S(1)}, u32[]{:S(2)}, u32[]{:S(2)}) %all-to-all-start.2) | async-done | bytes 131104 | tf_op jit(solution)/shard_map/all_to_all | solution.py:35
  155.0 2.2 %collective-permute-start.23 = (f32[8,128]{1,0:T(8,128)S(1)}, f32[8,128]{1,0:T(8,128)S(1)}, u32[]{:S(2)}, u32[]{:S(2)}) collective-permute-start(f32[8,128]{1,0:T(8,128)S(1)} %reduce_sum.48), channel_id=1, source_target_pairs={{0,64},{64,128},{128,192},{192,0},{1,65},{65,129},{129,193},{193,1... | collective-permute-start | bytes 12296 | tf_op jit(solution)/shard_map/ppermute | solution.py:340
  157.9 2.6 %collective-permute-start.25 = (f32[8,128]{1,0:T(8,128)S(1)}, f32[8,128]{1,0:T(8,128)S(1)}, u32[]{:S(2)}, u32[]{:S(2)}) collective-permute-start(f32[8,128]{1,0:T(8,128)S(1)} %reduce_sum.48), channel_id=1, source_target_pairs={{0,192},{64,0},{128,64},{192,128},{1,193},{65,1},{129,65},{193,129... | collective-permute-start | bytes 12296 | tf_op jit(solution)/shard_map/ppermute | solution.py:340
  160.6 2.9 %collective-permute-done.24 = f32[8,128]{1,0:T(8,128)S(1)} collective-permute-done((f32[8,128]{1,0:T(8,128)S(1)}, f32[8,128]{1,0:T(8,128)S(1)}, u32[]{:S(2)}, u32[]{:S(2)}) %collective-permute-start.24) | collective-permute-done | bytes 4128 | tf_op jit(solution)/shard_map/ppermute | solution.py:340
  (93 shorter events, 29.7 us)
Async XLA Ops:
  4.8 11.2 %collective-permute-start = (bf16[136,384]{1,0:T(8,128)(2,1)S(1)}, bf16[136,384]{1,0:T(8,128)(2,1)S(1)}, u32[]{:S(2)}, u32[]{:S(2)}) collective-permute-start(bf16[136,384]{1,0:T(8,128)(2,1)S(1)} %pick.1.refs_0_), channel_id=1, source_target_pairs={{0,64},{32,96},{64,128},{96,160},{128,192},{160,224},{192,0},{224,... | collective-permute-start | bytes 313352 | tf_op jit(solution)/shard_map/ppermute | solution.py:39
  8.7 9.4 %collective-permute-start.1 = (bf16[136,384]{1,0:T(8,128)(2,1)S(1)}, bf16[136,384]{1,0:T(8,128)(2,1)S(1)}, u32[]{:S(2)}, u32[]{:S(2)}) collective-permute-start(bf16[136,384]{1,0:T(8,128)(2,1)S(1)} %pick.1.refs_0_), channel_id=1, source_target_pairs={{0,192},{32,224},{64,0},{96,32},{128,64},{160,96},{192,128},{224,1... | collective-permute-start | bytes 313352 | tf_op jit(solution)/shard_map/ppermute | solution.py:39
  11.8 8.5 %collective-permute-start.2 = (bf16[136,384]{1,0:T(8,128)(2,1)S(1)}, bf16[136,384]{1,0:T(8,128)(2,1)S(1)}, u32[]{:S(2)}, u32[]{:S(2)}) collective-permute-start(bf16[136,384]{1,0:T(8,128)(2,1)S(1)} %pick.1.refs_0_), channel_id=1, source_target_pairs={{0,32},{32,64},{64,96},{96,128},{128,160},{160,192},{192,224},{224... | collective-permute-start | bytes 313352 | tf_op jit(solution)/shard_map/ppermute | solution.py:39
  12.5 7.8 %collective-permute-start.3 = (bf16[136,384]{1,0:T(8,128)(2,1)S(1)}, bf16[136,384]{1,0:T(8,128)(2,1)S(1)}, u32[]{:S(2)}, u32[]{:S(2)}) collective-permute-start(bf16[136,384]{1,0:T(8,128)(2,1)S(1)} %pick.1.refs_0_), channel_id=1, source_target_pairs={{0,224},{32,0},{64,32},{96,64},{128,96},{160,128},{192,160},{224,1... | collective-permute-start | bytes 313352 | tf_op jit(solution)/shard_map/ppermute | solution.py:39
  14.4 9.3 %collective-permute-start.7 = (bf16[136,384]{1,0:T(8,128)(2,1)S(1)}, bf16[136,384]{1,0:T(8,128)(2,1)S(1)}, u32[]{:S(2)}, u32[]{:S(2)}) collective-permute-start(bf16[136,384]{1,0:T(8,128)(2,1)S(1)} %pick.1.refs_0_), channel_id=1, source_target_pairs={{0,16},{16,0},{1,17},{17,1},{2,18},{18,2},{3,19},{19,3},{4,20},{20... | collective-permute-start | bytes 313352 | tf_op jit(solution)/shard_map/ppermute | solution.py:43
  16.0 7.9 %collective-permute-start.4 = (bf16[136,384]{1,0:T(8,128)(2,1)S(1)}, bf16[136,384]{1,0:T(8,128)(2,1)S(1)}, u32[]{:S(2)}, u32[]{:S(2)}) collective-permute-start(bf16[136,384]{1,0:T(8,128)(2,1)S(1)} %collective-permute-done.refs_1_), channel_id=1, source_target_pairs={{0,32},{32,64},{64,96},{96,128},{128,160},{160,192},{192,224},{224... | collective-permute-start | bytes 313352 | tf_op jit(solution)/shard_map/ppermute | solution.py:39
  18.1 7.6 %collective-permute-start.6 = (bf16[136,384]{1,0:T(8,128)(2,1)S(1)}, bf16[136,384]{1,0:T(8,128)(2,1)S(1)}, u32[]{:S(2)}, u32[]{:S(2)}) collective-permute-start(bf16[136,384]{1,0:T(8,128)(2,1)S(1)} %collective-permute-done.refs_1_), channel_id=1, source_target_pairs={{0,64},{32,96},{64,128},{96,160},{128,192},{160,224},{192,0},{224,... | collective-permute-start | bytes 313352 | tf_op jit(solution)/shard_map/ppermute | solution.py:39
  20.3 7.3 %collective-permute-start.5 = (bf16[136,384]{1,0:T(8,128)(2,1)S(1)}, bf16[136,384]{1,0:T(8,128)(2,1)S(1)}, u32[]{:S(2)}, u32[]{:S(2)}) collective-permute-start(bf16[136,384]{1,0:T(8,128)(2,1)S(1)} %collective-permute-done.1.refs_2_), channel_id=1, source_target_pairs={{0,224},{32,0},{64,32},{96,64},{128,96},{160,128},{192,160},{224,1... | collective-permute-start | bytes 313352 | tf_op jit(solution)/shard_map/ppermute | solution.py:39
  20.3 8.0 %collective-permute-start.8 = (bf16[136,384]{1,0:T(8,128)(2,1)S(1)}, bf16[136,384]{1,0:T(8,128)(2,1)S(1)}, u32[]{:S(2)}, u32[]{:S(2)}) collective-permute-start(bf16[136,384]{1,0:T(8,128)(2,1)S(1)} %collective-permute-done.refs_1_), channel_id=1, source_target_pairs={{0,16},{16,0},{1,17},{17,1},{2,18},{18,2},{3,19},{19,3},{4,20},{20... | collective-permute-start | bytes 313352 | tf_op jit(solution)/shard_map/ppermute | solution.py:43
  23.8 4.6 %collective-permute-start.9 = (bf16[136,384]{1,0:T(8,128)(2,1)S(1)}, bf16[136,384]{1,0:T(8,128)(2,1)S(1)}, u32[]{:S(2)}, u32[]{:S(2)}) collective-permute-start(bf16[136,384]{1,0:T(8,128)(2,1)S(1)} %collective-permute-done.1.refs_2_), channel_id=1, source_target_pairs={{0,16},{16,0},{1,17},{17,1},{2,18},{18,2},{3,19},{19,3},{4,20},{20... | collective-permute-start | bytes 313352 | tf_op jit(solution)/shard_map/ppermute | solution.py:43
  23.9 5.1 %collective-permute-start.10 = (bf16[136,384]{1,0:T(8,128)(2,1)S(1)}, bf16[136,384]{1,0:T(8,128)(2,1)S(1)}, u32[]{:S(2)}, u32[]{:S(2)}) collective-permute-start(bf16[136,384]{1,0:T(8,128)(2,1)S(1)} %collective-permute-done.2.refs_3_), channel_id=1, source_target_pairs={{0,16},{16,0},{1,17},{17,1},{2,18},{18,2},{3,19},{19,3},{4,20},{20... | collective-permute-start | bytes 313352 | tf_op jit(solution)/shard_map/ppermute | solution.py:43
  25.7 3.3 %collective-permute-start.11 = (bf16[136,384]{1,0:T(8,128)(2,1)S(1)}, bf16[136,384]{1,0:T(8,128)(2,1)S(1)}, u32[]{:S(2)}, u32[]{:S(2)}) collective-permute-start(bf16[136,384]{1,0:T(8,128)(2,1)S(1)} %collective-permute-done.3.refs_4_), channel_id=1, source_target_pairs={{0,16},{16,0},{1,17},{17,1},{2,18},{18,2},{3,19},{19,3},{4,20},{20... | collective-permute-start | bytes 313352 | tf_op jit(solution)/shard_map/ppermute | solution.py:43
  32.7 20.3 %all-to-all-start = ((bf16[16,64,384]{2,1,0:T(8,128)(2,1)}), bf16[16,64,384]{2,1,0:T(8,128)(2,1)S(1)}, u32[]{:S(2)}, u32[]{:S(2)}) async-start(bf16[16,64,384]{2,1,0:T(8,128)(2,1)} %bitcast.53), calls=%async_computation | async-start | bytes 1572864 | tf_op jit(solution)/shard_map/all_to_all | solution.py:35
  79.9 25.3 %collective-permute-start.16 = (bf16[32,72,384]{2,1,0:T(8,128)(2,1)}, bf16[32,72,384]{2,1,0:T(8,128)(2,1)S(1)}, u32[]{:S(2)}, u32[]{:S(2)}) collective-permute-start(bf16[32,72,384]{2,1,0:T(8,128)(2,1)} %all_to_all.15.y), channel_id=1, source_target_pairs={{0,16},{16,0},{1,17},{17,1},{2,18},{18,2},{3,19},{19,3},{4,20},{20... | collective-permute-start | bytes 5308424 | tf_op jit(solution)/shard_map/ppermute | solution.py:43
  85.7 10.9 %collective-permute-start.15 = (bf16[512,384]{1,0:T(8,128)(2,1)}, bf16[512,384]{1,0:T(8,128)(2,1)S(1)}, u32[]{:S(2)}, u32[]{:S(2)}) collective-permute-start(bf16[512,384]{1,0:T(8,128)(2,1)} %get-tuple-element.20), channel_id=1, source_target_pairs={{0,32},{16,48},{32,0},{48,16},{1,33},{17,49},{33,1},{49,17},{2,34}... | collective-permute-start | bytes 1179656 | tf_op jit(solution)/shard_map/ppermute | solution.py:271
  86.2 13.2 %collective-permute-start.17 = (bf16[512,384]{1,0:T(8,128)(2,1)}, bf16[512,384]{1,0:T(8,128)(2,1)S(1)}, u32[]{:S(2)}, u32[]{:S(2)}) collective-permute-start(bf16[512,384]{1,0:T(8,128)(2,1)} %get-tuple-element.19), channel_id=1, source_target_pairs={{0,16},{16,0},{32,48},{48,32},{1,17},{17,1},{33,49},{49,33},{2,18}... | collective-permute-start | bytes 1179656 | tf_op jit(solution)/shard_map/ppermute | solution.py:271
  86.5 18.7 %collective-permute-start.18 = (bf16[512,384]{1,0:T(8,128)(2,1)}, bf16[512,384]{1,0:T(8,128)(2,1)S(1)}, u32[]{:S(2)}, u32[]{:S(2)}) collective-permute-start(bf16[512,384]{1,0:T(8,128)(2,1)} %get-tuple-element.18), channel_id=1, source_target_pairs={{0,48},{16,32},{32,16},{48,0},{1,49},{17,33},{33,17},{49,1},{2,50}... | collective-permute-start | bytes 1179656 | tf_op jit(solution)/shard_map/ppermute | solution.py:271
  108.6 18.3 %collective-permute-start.19 = (f16[264,512]{1,0:T(8,128)(2,1)}, f16[264,512]{1,0:T(8,128)(2,1)}, u32[]{:S(2)}, u32[]{:S(2)}) collective-permute-start(f16[264,512]{1,0:T(8,128)(2,1)} %convert_element_type.23), channel_id=1, source_target_pairs={{0,128},{64,192},{128,0},{192,64},{1,129},{65,193},{129,1},{193,65... | collective-permute-start | bytes 811016 | tf_op jit(solution)/shard_map/ppermute | solution.py:308
  115.9 17.3 %collective-permute-start.20 = (f16[264,512]{1,0:T(8,128)(2,1)}, f16[264,512]{1,0:T(8,128)(2,1)}, u32[]{:S(2)}, u32[]{:S(2)}) collective-permute-start(f16[264,512]{1,0:T(8,128)(2,1)} %convert_element_type.25), channel_id=1, source_target_pairs={{0,64},{64,128},{128,192},{192,0},{1,65},{65,129},{129,193},{193,1... | collective-permute-start | bytes 811016 | tf_op jit(solution)/shard_map/ppermute | solution.py:308
  116.9 20.4 %collective-permute-start.21 = (f16[264,512]{1,0:T(8,128)(2,1)S(1)}, f16[264,512]{1,0:T(8,128)(2,1)S(1)}, u32[]{:S(2)}, u32[]{:S(2)}) collective-permute-start(f16[264,512]{1,0:T(8,128)(2,1)S(1)} %convert_element_type.27), channel_id=1, source_target_pairs={{0,192},{64,0},{128,64},{192,128},{1,193},{65,1},{129,65},{193,129... | collective-permute-start | bytes 811016 | tf_op jit(solution)/shard_map/ppermute | solution.py:308
  141.1 13.9 %all-to-all-start.2 = ((f32[32,8,128]{2,1,0:T(8,128)}), f32[32,8,128]{2,1,0:T(8,128)S(1)}, u32[]{:S(2)}, u32[]{:S(2)}) async-start(f32[32,8,128]{2,1,0:T(8,128)} %broadcast_in_dim.128), calls=%async_computation.2 | async-start | bytes 262144 | tf_op jit(solution)/shard_map/all_to_all | solution.py:35
  155.0 5.6 %collective-permute-start.23 = (f32[8,128]{1,0:T(8,128)S(1)}, f32[8,128]{1,0:T(8,128)S(1)}, u32[]{:S(2)}, u32[]{:S(2)}) collective-permute-start(f32[8,128]{1,0:T(8,128)S(1)} %reduce_sum.48), channel_id=1, source_target_pairs={{0,64},{64,128},{128,192},{192,0},{1,65},{65,129},{129,193},{193,1... | collective-permute-start | bytes 12296 | tf_op jit(solution)/shard_map/ppermute | solution.py:340
  157.1 6.4 %collective-permute-start.24 = (f32[8,128]{1,0:T(8,128)S(1)}, f32[8,128]{1,0:T(8,128)S(1)}, u32[]{:S(2)}, u32[]{:S(2)}) collective-permute-start(f32[8,128]{1,0:T(8,128)S(1)} %reduce_sum.48), channel_id=1, source_target_pairs={{0,128},{64,192},{128,0},{192,64},{1,129},{65,193},{129,1},{193,65... | collective-permute-start | bytes 12296 | tf_op jit(solution)/shard_map/ppermute | solution.py:340
  157.9 5.6 %collective-permute-start.25 = (f32[8,128]{1,0:T(8,128)S(1)}, f32[8,128]{1,0:T(8,128)S(1)}, u32[]{:S(2)}, u32[]{:S(2)}) collective-permute-start(f32[8,128]{1,0:T(8,128)S(1)} %reduce_sum.48), channel_id=1, source_target_pairs={{0,192},{64,0},{128,64},{192,128},{1,193},{65,1},{129,65},{193,129... | collective-permute-start | bytes 12296 | tf_op jit(solution)/shard_map/ppermute | solution.py:340
  (9 other events, 63.6 us)
